TPU v7x, 256 devices: a whole 4x4x8 slice. The times are simulated.
256 devices in a mesh: dom: 256 (over y, z, x, core).
Axes of the slice: x: 4, y: 4, z: 8, core: 2. Of those that a mesh axis runs over, the one named last changes fastest.
Arguments:
- rhs: float32 [1024, 12, 512], P('dom'), may hold values from -18 to 18
- stiffness: float32 [512, 512], replicated, may hold values from -0.25 to 0.25
- vol_jac: float32 [1024, 12, 12], P('dom'), may hold values from -0.9 to 0.9
- face_jac: float32 [1024, 6, 12, 12], P('dom'), may hold values from -1.5 to 1.5
- block_inv: float32 [1024, 12, 12, 512], P('dom'), as said below
- face_owner: int32 [1024, 6], P('dom'), may hold values from -1 to 255, as said below
- face_elem: int32 [1024, 6], P('dom'), may hold values from 0 to 3
- face_side: int32 [1024, 6], P('dom'), may hold values from 0 to 5
- face_turn: int32 [1024, 6], P('dom'), may hold values from 0 to 7
Outputs:
- correction: float32 [1024, 12, 512], P('dom')
Inputs may be any that keep to these rules, and one draw needn't show every extreme that they name: `face_owner`: -1 marks a face with no neighbour; any other value is the element's own partition or one next to it along the axis; of the faces of one partition exactly 8 name the partition below and exactly 8 the partition above, where that partition exists. Each block_inv[e, :, :, m] is a full 12 x 12 matrix.
All inputs are finite; a program needn't handle non-finite values.
Results may differ from a plain program's by a relative error of at most 0.0001.
Values sent between devices are 32-bit elements; how exact they have to be, the bound alone decides.
No kernel may reach another device: no remote copies, remote signals or barrier semaphores. Data moves between devices by JAX's collectives and lax.ppermute only.
A program may use at most 64 MiB of HBM per device.

v0:
```python
import jax
import jax.numpy as jnp
import numpy as np
from jax import lax
from jax.sharding import PartitionSpec as P

QF = 8
QC = 4


PRECISE = lax.Precision.HIGHEST
SIGMA = 2.0
OMEGA = 0.7


def from_behind(block, axis, distance):
    devices = range(lax.axis_size(axis))
    route = [(i - distance, i) for i in devices if i - distance in devices]
    return lax.ppermute(block, axis, route)


def trace_table(degree_count, keep_count):
    matrix = np.zeros((degree_count**3, 6 * keep_count * keep_count), np.float32)
    for index_i in range(degree_count):
        for index_j in range(degree_count):
            for index_k in range(degree_count):
                mode_id = (index_i * degree_count + index_j) * degree_count + index_k
                triple = (index_i, index_j, index_k)
                for face_id in range(6):
                    normal_axis = face_id // 2
                    normal = triple[normal_axis]
                    tangent = [triple[place] for place in range(3) if place != normal_axis]
                    if tangent[0] < keep_count and tangent[1] < keep_count:
                        sign_val = (-1.0) ** normal if face_id % 2 == 0 else 1.0
                        column = (
                            face_id * keep_count * keep_count + tangent[0] * keep_count + tangent[1]
                        )
                        matrix[mode_id, column] = sign_val
    return matrix


def lift_table(degree_count):
    matrix = np.zeros((6 * degree_count * degree_count, degree_count**3), np.float32)
    for index_i in range(degree_count):
        for index_j in range(degree_count):
            for index_k in range(degree_count):
                mode_id = (index_i * degree_count + index_j) * degree_count + index_k
                triple = (index_i, index_j, index_k)
                for face_id in range(6):
                    normal_axis = face_id // 2
                    normal = triple[normal_axis]
                    tangent = [triple[place] for place in range(3) if place != normal_axis]
                    sign_val = (-1.0) ** normal if face_id % 2 == 0 else 1.0
                    column = (
                        face_id * degree_count * degree_count
                        + tangent[0] * degree_count
                        + tangent[1]
                    )
                    matrix[column, mode_id] = (2.0 * normal + 1.0) / 16.0 * sign_val
    return matrix


def turn_table(degree_count):
    span = degree_count * degree_count
    matrix = np.zeros((span, 8 * span), np.float32)
    for turn_id in range(8):
        for index_a in range(degree_count):
            for index_b in range(degree_count):
                if turn_id % 2 == 1:
                    source = index_b * degree_count + index_a
                else:
                    source = index_a * degree_count + index_b
                sign_val = 1.0
                if turn_id // 2 % 2 == 1:
                    sign_val = sign_val * (-1.0) ** index_a
                if turn_id // 4 % 2 == 1:
                    sign_val = sign_val * (-1.0) ** index_b
                matrix[source, turn_id * span + index_a * degree_count + index_b] = sign_val
    return matrix


def select_table():
    matrix = np.zeros((QF**3, QC**3), np.float32)
    for index_i in range(QC):
        for index_j in range(QC):
            for index_k in range(QC):
                matrix[
                    (index_i * QF + index_j) * QF + index_k, (index_i * QC + index_j) * QC + index_k
                ] = 1.0
    return matrix


def faces_of(iterate, matrix):
    elements, variables = (iterate.shape[0], iterate.shape[1])
    face_span = matrix.shape[1] // 6
    traced = jnp.dot(iterate.reshape(elements * variables, -1), matrix, precision=PRECISE)
    traced = traced.reshape(elements, variables, 6, face_span).transpose(0, 2, 1, 3)
    return traced.reshape(elements * 6, variables * face_span)


def pick_faces(pooled, slot_ids, turning, present, turns, variables):
    gathered = jnp.take(pooled, slot_ids, axis=0)
    count = gathered.shape[0]
    span = turns.shape[0]
    rotated = jnp.dot(gathered.reshape(count * variables, span), turns, precision=PRECISE)
    rotated = rotated.reshape(count, variables, 8, span)
    weights = (turning[:, None] == jnp.arange(8, dtype=jnp.int32)[None, :]).astype(jnp.float32)
    weights = weights * present.astype(jnp.float32)[:, None]
    oriented = jnp.einsum("cvtq,ct->cvq", rotated, weights, precision=PRECISE)
    return oriented.reshape(count, variables * span)


def finish(iterate, inside, outside, vol_jac, face_jac, kernel, lift):
    elements, variables = (iterate.shape[0], iterate.shape[1])
    face_span = inside.shape[1] // variables
    jump_in = (inside - outside).reshape(elements, 6, variables, face_span)
    jumps = jnp.einsum("efvw,efwq->efvq", face_jac, jump_in, precision=PRECISE)
    lifted = jnp.dot(
        jumps.transpose(0, 2, 1, 3).reshape(elements * variables, 6 * face_span),
        lift,
        precision=PRECISE,
    )
    blended = jnp.dot(iterate.reshape(elements * variables, -1), kernel, precision=PRECISE).reshape(
        elements, variables, -1
    )
    volume = jnp.einsum("evw,ewm->evm", vol_jac, blended, precision=PRECISE)
    return volume + lifted.reshape(elements, variables, -1)


def smooth(inverse, residual):
    summed = inverse[:, :, 0, :] * residual[:, None, 0, :]
    for column in range(1, residual.shape[1]):
        summed = summed + inverse[:, :, column, :] * residual[:, None, column, :]
    return summed


def local(
    rhs, stiffness, vol_jac, face_jac, block_inv, face_owner, face_elem, face_side, face_turn
):
    elements, variables, mode_count = rhs.shape
    me_index = lax.axis_index("dom")
    trace_fine = jnp.asarray(trace_table(QF, QF))
    trace_low = jnp.asarray(trace_table(QF, QC))
    trace_coarse = jnp.asarray(trace_table(QC, QC))
    lift_fine = jnp.asarray(lift_table(QF))
    lift_coarse = jnp.asarray(lift_table(QC))
    turns_fine = jnp.asarray(turn_table(QF))
    turns_coarse = jnp.asarray(turn_table(QC))
    select = jnp.asarray(select_table())

    def restrict(values):
        leading = values.shape[:-1]
        return jnp.dot(values.reshape(-1, values.shape[-1]), select, precision=PRECISE).reshape(
            leading + (select.shape[1],)
        )

    flat_owner = face_owner.reshape(-1)
    flat_slot = (face_elem * 6 + face_side).reshape(-1).astype(jnp.int32)
    present = flat_owner >= 0
    offset = flat_owner - me_index
    slot_full = jnp.where(present, (offset + 1) * (elements * 6) + flat_slot, 0).astype(jnp.int32)
    turning = face_turn.reshape(-1)

    def neighbour_pool(inside):
        shifted = [from_behind(inside, "dom", stride) for stride in (1, -1)]
        return jnp.concatenate([shifted[0], inside, shifted[1]], axis=0)

    def fine_apply(iterate):
        inside = faces_of(iterate, trace_fine)
        outside = pick_faces(
            neighbour_pool(inside), slot_full, turning, present, turns_fine, variables
        )
        return SIGMA * iterate + finish(
            iterate, inside, outside, vol_jac, face_jac, stiffness, lift_fine
        )

    iterate = OMEGA * smooth(block_inv, rhs)
    iterate = iterate + OMEGA * smooth(block_inv, rhs - fine_apply(iterate))
    inside = faces_of(iterate, trace_low)
    shifted = [from_behind(inside, "dom", stride) for stride in (1, -1)]
    pooled = jnp.concatenate([shifted[0], inside, shifted[1]], axis=0)
    outside = pick_faces(pooled, slot_full, turning, present, turns_coarse, variables)
    kernel_low = restrict(stiffness)
    coarse_rhs = restrict(rhs - SIGMA * iterate) - finish(
        iterate, inside, outside, vol_jac, face_jac, kernel_low, lift_coarse
    )
    coarse_inv = restrict(block_inv)
    coarse_mat = restrict(restrict(stiffness).T).T
    sweep_one = OMEGA * smooth(coarse_inv, coarse_rhs)
    inside = faces_of(sweep_one, trace_coarse)
    shifted = [from_behind(inside, "dom", stride) for stride in (1, -1)]
    pooled = jnp.concatenate([shifted[0], inside, shifted[1]], axis=0)
    outside = pick_faces(pooled, slot_full, turning, present, turns_coarse, variables)
    result = SIGMA * sweep_one + finish(
        sweep_one, inside, outside, vol_jac, face_jac, coarse_mat, lift_coarse
    )
    correction_low = sweep_one + OMEGA * smooth(coarse_inv, coarse_rhs - result)
    leading = correction_low.shape[:-1]
    iterate = iterate + jnp.dot(
        correction_low.reshape(-1, correction_low.shape[-1]), select.T, precision=PRECISE
    ).reshape(leading + (select.shape[0],))
    for sweep in range(2):
        iterate = iterate + OMEGA * smooth(block_inv, rhs - fine_apply(iterate))
    return iterate


def solution(mesh):
    return jax.shard_map(
        local,
        mesh=mesh,
        in_specs=(
            P("dom", None, None),
            P(),
            P("dom", None, None),
            P("dom", None, None, None),
            P("dom", None, None, None),
            P("dom", None),
            P("dom", None),
            P("dom", None),
            P("dom", None),
        ),
        out_specs=P("dom", None, None),
        check_vma=False,
    )
```

profile of v0, /device:TPU:24, one launch (start us, length us, event | category | flops | bytes accessed | tf_op | source)
XLA Modules:
  0.0 159.7 jit_solution(1169475324405312941)
XLA Ops:
  0.0 1.8 %fusion.249 = (f32[4,12,1,512]{3,0,2,1:T(4,128)S(1)}, f32[4,12,1,512]{3,0,2,1:T(4,128)S(1)}, f32[4,12,1,512]{3,0,2,1:T(4,128)S(1)}, f32[4,12,1,512]{3,0,2,1:T(4,...) fusion(f32[4,12,12,512]{3,0,2,1:T(4,128)} %param.25), kind=kLoop, calls=%fused_computation.407 | loop fusion | bytes 2359296 | tf_op jit(solution)/shard_map/slice | solution.py:133
  2.0 1.7 %convolution_bitcast_fusion.5 = f32[4,6,12,64]{3,2,1,0:T(8,128)S(1)} fusion(f32[6,64,512,1]{2,1,0,3:T(8,128)S(1)} %copy-done.2, f32[4,12,1,512]{3,0,2,1:T(4,128)S(1)} %get-tuple-element.18, f32[4,12,1,512]{3,0,2,1:T(4,128)S(1)} %get-tuple-element.17, f32[4,12,1,512]{3,0,2,1:T(4,128)S(1)} %get-tuple-element.16, f32[4,12,1,512]{3,0,2,1:T(4,128)S(1)} %get-tuple-element.15, ...), kind=kOutput, calls=%fused_computation.19 | convolution fusion | flops 113836032 | bytes 2138112 | tf_op jit(solution)/shard_map/dot_general | solution.py:96
  3.9 1.9 %collective-permute-start = (f32[24,768]{1,0:T(8,128)S(1)}, f32[24,768]{1,0:T(8,128)S(1)}, u32[]{:S(2)}, u32[]{:S(2)}) collective-permute-start(f32[24,768]{1,0:T(8,128)S(1)} %reshape.370), channel_id=1, source_target_pairs={{0,1},{1,2},{2,3},{3,4},{4,5},{5,6},{6,7},{7,8},{8,9},{9,10},{10,1... | collective-permute-start | bytes 221192 | tf_op jit(solution)/shard_map/ppermute | solution.py:19
  5.8 9.6 %collective-permute-start.1 = (f32[24,768]{1,0:T(8,128)S(1)}, f32[24,768]{1,0:T(8,128)}, u32[]{:S(2)}, u32[]{:S(2)}) collective-permute-start(f32[24,768]{1,0:T(8,128)S(1)} %reshape.370), channel_id=1, source_target_pairs={{1,0},{2,1},{3,2},{4,3},{5,4},{6,5},{7,6},{8,7},{9,8},{10,9},{11,1... | collective-permute-start | bytes 221192 | tf_op jit(solution)/shard_map/ppermute | solution.py:19
  31.4 1.7 %reshape.467 = f32[4,12,384]{2,1,0:T(8,128)} reshape(f32[4,12,6,64]{3,2,1,0:T(8,128)} %copy.834) | data formatting | bytes 147456 | tf_op jit(solution)/shard_map/dot_general | solution.py:118
  33.3 1.9 %fusion.14 = f32[4,12,512]{2,1,0:T(8,128)S(1)} fusion(f32[4,12,512]{2,1,0:T(8,128)} %convolution_bitcast_fusion.10, f32[4,12,384]{2,1,0:T(8,128)} %reshape.467, f32[384,512,1]{1,0,2:T(8,128)S(1)} %copy-done.1, f32[4,12,512]{2,0,1:T(4,128)} %param.21, f32[4,12,512]{2,1,0:T(8,128)} %copy-done.34), kind=kOutput, calls=%fused_computation.28 | convolution fusion | flops 113344512 | bytes 1253376 | tf_op jit(solution)/shard_map/dot_general | solution.py:118
  36.2 2.3 %convolution_bitcast_fusion.6 = f32[4,6,12,16]{3,2,1,0:T(8,128)} fusion(f32[6,16,512,1]{2,1,0,3:T(8,128)S(1)} %copy-done.71, f32[4,12,1,512]{3,0,2,1:T(4,128)S(1)} %copy-done.18, f32[4,12,1,512]{3,0,2,1:T(4,128)S(1)} %copy-done.14, f32[4,12,1,512]{3,0,2,1:T(4,128)S(1)} %copy-done.10, f32[4,12,1,512]{3,0,2,1:T(4,128)S(1)} %copy-done.6, ...), kind=kOutput, calls=%fused_computation.20 | convolution fusion | flops 29515776 | bytes 1591296 | tf_op jit(solution)/shard_map/dot_general | solution.py:96
  40.1 2.1 %collective-permute-start.2 = (f32[24,192]{1,0:T(8,128)}, f32[24,192]{1,0:T(8,128)S(1)}, u32[]{:S(2)}, u32[]{:S(2)}) collective-permute-start(f32[24,192]{1,0:T(8,128)} %reshape.372), channel_id=1, source_target_pairs={{0,1},{1,2},{2,3},{3,4},{4,5},{5,6},{6,7},{7,8},{8,9},{9,10},{10,1... | collective-permute-start | bytes 55304 | tf_op jit(solution)/shard_map/ppermute | solution.py:19
  42.2 8.0 %collective-permute-start.3 = (f32[24,192]{1,0:T(8,128)}, f32[24,192]{1,0:T(8,128)S(1)}, u32[]{:S(2)}, u32[]{:S(2)}) collective-permute-start(f32[24,192]{1,0:T(8,128)} %reshape.372), channel_id=1, source_target_pairs={{1,0},{2,1},{3,2},{4,3},{5,4},{6,5},{7,6},{8,7},{9,8},{10,9},{11,1... | collective-permute-start | bytes 55304 | tf_op jit(solution)/shard_map/ppermute | solution.py:19
  50.2 1.7 %fusion.115 = f32[4,12,512]{2,1,0:T(8,128)S(1)} fusion(f32[4,12,1,512]{3,0,2,1:T(4,128)} %copy-done.17, f32[4,12,1,512]{3,0,2,1:T(4,128)} %copy-done.13, f32[4,12,1,512]{3,0,2,1:T(4,128)} %copy-done.9, f32[4,12,1,512]{3,0,2,1:T(4,128)} %copy-done.5, f32[4,12,1,512]{3,0,2,1:T(4,128)S(1)} %get-tuple-element.14, f32[4,12,1,512]{3,0,2,1:T(4,128)S(1)} %get-tuple-element.13, ...), kind=kLoop, calls=%fused_computation.178 | loop fusion | flops 638976 | bytes 1474560 | tf_op jit(solution)/shard_map/add | solution.py:178
  54.5 2.2 %gather_fusion.1 = f32[24,192]{1,0:T(8,128)} fusion(f32[72,192]{1,0:T(8,128)} %pad_maximum_fusion.3, s32[1024]{0:T(1024)} %copy-done.130), kind=kCustom, calls=%fused_computation.1.clone | custom fusion | bytes 36960 | tf_op jit(solution)/shard_map/jit(_take)/gather | solution.py:102
  59.6 2.5 %fusion.257 = f32[24,12,8,16]{0,3,2,1:T(8,128)} fusion(f32[24,12,16,1]{0,2,3,1:T(8,128)} %bitcast.655, f32[8,16,16,1]{2,1,0,3:T(8,128)} %constant.92), kind=kOutput, calls=%fused_computation.415 | convolution fusion | flops 7077888 | bytes 174080 | tf_op jit(solution)/shard_map/dot_general | solution.py:105
  62.1 3.0 %copy.816 = f32[24,12,8,16]{3,2,1,0:T(8,128)} copy(f32[24,12,8,16]{0,3,2,1:T(8,128)} %fusion.257) | data formatting | bytes 294912 | tf_op jit(solution)/shard_map/dot_general | solution.py:105
  65.2 2.4 %fusion.258 = f32[24,1,12,16]{3,1,2,0:T(1,128)S(1)} fusion(f32[24,12,8,16]{3,2,1,0:T(8,128)} %copy.816, f32[24,8,1,1]{1,2,3,0:T(1,128)} %bitcast.650), kind=kOutput, calls=%fused_computation.416 | convolution fusion | flops 442368 | bytes 166656 | tf_op jit(solution)/shard_map/cvtq,ct->cvq/dot_general | solution.py:109
  72.9 1.9 %collective-permute-start.4 = (f32[24,192]{1,0:T(8,128)}, f32[24,192]{1,0:T(8,128)S(1)}, u32[]{:S(2)}, u32[]{:S(2)}) collective-permute-start(f32[24,192]{1,0:T(8,128)} %reshape.374), channel_id=1, source_target_pairs={{0,1},{1,2},{2,3},{3,4},{4,5},{5,6},{6,7},{7,8},{8,9},{9,10},{10,1... | collective-permute-start | bytes 55304 | tf_op jit(solution)/shard_map/ppermute | solution.py:19
  74.9 7.9 %collective-permute-start.5 = (f32[24,192]{1,0:T(8,128)}, f32[24,192]{1,0:T(8,128)S(1)}, u32[]{:S(2)}, u32[]{:S(2)}) collective-permute-start(f32[24,192]{1,0:T(8,128)} %reshape.374), channel_id=1, source_target_pairs={{1,0},{2,1},{3,2},{4,3},{5,4},{6,5},{7,6},{8,7},{9,8},{10,9},{11,1... | collective-permute-start | bytes 55304 | tf_op jit(solution)/shard_map/ppermute | solution.py:19
  88.2 2.2 %gather_fusion.2 = f32[24,192]{1,0:T(8,128)} fusion(f32[72,192]{1,0:T(8,128)} %pad_maximum_fusion.4, s32[1024]{0:T(1024)} %copy-done.130), kind=kCustom, calls=%fused_computation.4.clone | custom fusion | bytes 36960 | tf_op jit(solution)/shard_map/jit(_take)/gather | solution.py:102
  93.3 2.5 %fusion.259 = f32[24,12,8,16]{0,3,2,1:T(8,128)} fusion(f32[24,12,16,1]{0,2,3,1:T(8,128)} %bitcast.654, f32[8,16,16,1]{2,1,0,3:T(8,128)} %constant.92), kind=kOutput, calls=%fused_computation.417 | convolution fusion | flops 7077888 | bytes 174080 | tf_op jit(solution)/shard_map/dot_general | solution.py:105
  95.8 3.0 %copy.822 = f32[24,12,8,16]{3,2,1,0:T(8,128)} copy(f32[24,12,8,16]{0,3,2,1:T(8,128)} %fusion.259) | data formatting | bytes 294912 | tf_op jit(solution)/shard_map/dot_general | solution.py:105
  99.0 2.6 %fusion.260 = f32[24,1,12,16]{3,1,2,0:T(1,128)S(1)} fusion(f32[24,12,8,16]{3,2,1,0:T(8,128)} %copy.822, f32[24,8,1,1]{1,2,3,0:T(1,128)} %bitcast.651), kind=kOutput, calls=%fused_computation.418 | convolution fusion | flops 442368 | bytes 166656 | tf_op jit(solution)/shard_map/cvtq,ct->cvq/dot_general | solution.py:109
  103.8 2.0 %convolution_bitcast_fusion.3 = f32[4,6,12,64]{3,2,1,0:T(8,128)} fusion(f32[6,64,512,1]{2,1,0,3:T(8,128)S(1)} %copy-done.2, f32[4,12,512]{2,1,0:T(8,128)S(1)} %convolution_add_fusion.3), kind=kOutput, calls=%fused_computation.17 | convolution fusion | flops 113246208 | bytes 958464 | tf_op jit(solution)/shard_map/dot_general | solution.py:96
  107.4 2.0 %collective-permute-start.6 = (f32[24,768]{1,0:T(8,128)}, f32[24,768]{1,0:T(8,128)S(1)}, u32[]{:S(2)}, u32[]{:S(2)}) collective-permute-start(f32[24,768]{1,0:T(8,128)} %reshape.376), channel_id=1, source_target_pairs={{0,1},{1,2},{2,3},{3,4},{4,5},{5,6},{6,7},{7,8},{8,9},{9,10},{10,1... | collective-permute-start | bytes 221192 | tf_op jit(solution)/shard_map/ppermute | solution.py:19
  109.4 8.1 %collective-permute-start.7 = (f32[24,768]{1,0:T(8,128)}, f32[24,768]{1,0:T(8,128)S(1)}, u32[]{:S(2)}, u32[]{:S(2)}) collective-permute-start(f32[24,768]{1,0:T(8,128)} %reshape.376), channel_id=1, source_target_pairs={{1,0},{2,1},{3,2},{4,3},{5,4},{6,5},{7,6},{8,7},{9,8},{10,9},{11,1... | collective-permute-start | bytes 221192 | tf_op jit(solution)/shard_map/ppermute | solution.py:19
  117.5 1.7 %fusion.22 = f32[4,12,512]{2,1,0:T(8,128)S(1)} fusion(f32[4,12,512]{2,1,0:T(8,128)} %copy-done.26, f32[512,512]{1,0:T(8,128)S(1)} %copy-done), kind=kOutput, calls=%fused_computation.45 | convolution fusion | flops 150994944 | bytes 1245184 | tf_op jit(solution)/shard_map/dot_general | solution.py:123
  120.8 2.3 %gather_fusion.3 = f32[24,768]{1,0:T(8,128)} fusion(f32[72,768]{1,0:T(8,128)} %pad_maximum_fusion.1, s32[1024]{0:T(1024)} %copy-done.130), kind=kCustom, calls=%fused_computation.2.clone | custom fusion | bytes 147552 | tf_op jit(solution)/shard_map/jit(_take)/gather | solution.py:102
  124.7 1.7 %reshape.461 = f32[24,12,64,1]{2,1,0,3:T(8,128)} reshape(f32[24,768]{1,0:T(8,128)} %broadcast_select_fusion.1) | data formatting | bytes 147456 | tf_op jit(solution)/shard_map/dot_general | solution.py:105
  126.4 2.5 %fusion.35 = f32[24,12,8,64]{3,1,2,0:T(8,128)S(1)} fusion(f32[8,64,64,1]{2,1,0,3:T(8,128)} %constant.87, f32[24,12,64,1]{2,1,0,3:T(8,128)} %reshape.461), kind=kOutput, calls=%fused_computation.61 | convolution fusion | flops 113246208 | bytes 794624 | tf_op jit(solution)/shard_map/dot_general | solution.py:105
  133.1 1.7 %fusion.15 = f32[4,12,512]{2,1,0:T(8,128)S(1)} fusion(f32[4,12,512]{2,1,0:T(8,128)} %convolution_bitcast_fusion.9, f32[4,12,384]{2,1,0:T(8,128)} %reshape.469, f32[384,512,1]{1,0,2:T(8,128)S(1)} %copy-done.1, f32[4,12,512]{2,0,1:T(4,128)} %param.21, f32[4,12,512]{2,1,0:T(8,128)} %copy-done.26), kind=kOutput, calls=%fused_computation.29 | convolution fusion | flops 113344512 | bytes 1253376 | tf_op jit(solution)/shard_map/dot_general | solution.py:118
  136.2 2.0 %convolution_bitcast_fusion.1 = f32[4,6,12,64]{3,2,1,0:T(8,128)} fusion(f32[6,64,512,1]{2,1,0,3:T(8,128)S(1)} %copy-done.2, f32[4,12,512]{2,1,0:T(8,128)S(1)} %fusion.128), kind=kOutput, calls=%fused_computation.15 | convolution fusion | flops 113246208 | bytes 958464 | tf_op jit(solution)/shard_map/dot_general | solution.py:96
  139.2 1.9 %collective-permute-start.8 = (f32[24,768]{1,0:T(8,128)S(1)}, f32[24,768]{1,0:T(8,128)S(1)}, u32[]{:S(2)}, u32[]{:S(2)}) collective-permute-start(f32[24,768]{1,0:T(8,128)S(1)} %reshape.378), channel_id=1, source_target_pairs={{0,1},{1,2},{2,3},{3,4},{4,5},{5,6},{6,7},{7,8},{8,9},{9,10},{10,1... | collective-permute-start | bytes 221192 | tf_op jit(solution)/shard_map/ppermute | solution.py:19
  141.1 7.9 %collective-permute-start.9 = (f32[24,768]{1,0:T(8,128)S(1)}, f32[24,768]{1,0:T(8,128)S(1)}, u32[]{:S(2)}, u32[]{:S(2)}) collective-permute-start(f32[24,768]{1,0:T(8,128)S(1)} %reshape.378), channel_id=1, source_target_pairs={{1,0},{2,1},{3,2},{4,3},{5,4},{6,5},{7,6},{8,7},{9,8},{10,9},{11,1... | collective-permute-start | bytes 221192 | tf_op jit(solution)/shard_map/ppermute | solution.py:19
  149.0 1.7 %fusion.20 = f32[4,12,512]{2,1,0:T(8,128)S(1)} fusion(f32[4,12,512]{2,1,0:T(8,128)} %copy-done.24, f32[512,512]{1,0:T(8,128)S(1)} %copy-done), kind=kOutput, calls=%fused_computation.43 | convolution fusion | flops 150994944 | bytes 1245184 | tf_op jit(solution)/shard_map/dot_general | solution.py:123
  (397 shorter events, 59.2 us)
Async XLA Ops:
  0.0 16.4 %copy-start = (f32[512,512]{1,0:T(8,128)S(1)}, f32[512,512]{1,0:T(8,128)}, u32[]{:S(2)}) copy-start(f32[512,512]{1,0:T(8,128)} %param.22) | copy-start | bytes 3145732
  1.8 13.8 %copy-start.5 = (f32[4,12,1,512]{3,0,2,1:T(4,128)}, f32[4,12,1,512]{3,0,2,1:T(4,128)S(1)}, u32[]{:S(2)}) copy-start(f32[4,12,1,512]{3,0,2,1:T(4,128)S(1)} %get-tuple-element.15) | copy-start | bytes 294916
  1.8 13.8 %copy-start.9 = (f32[4,12,1,512]{3,0,2,1:T(4,128)}, f32[4,12,1,512]{3,0,2,1:T(4,128)S(1)}, u32[]{:S(2)}) copy-start(f32[4,12,1,512]{3,0,2,1:T(4,128)S(1)} %get-tuple-element.16) | copy-start | bytes 294916
  1.8 13.8 %copy-start.13 = (f32[4,12,1,512]{3,0,2,1:T(4,128)}, f32[4,12,1,512]{3,0,2,1:T(4,128)S(1)}, u32[]{:S(2)}) copy-start(f32[4,12,1,512]{3,0,2,1:T(4,128)S(1)} %get-tuple-element.17) | copy-start | bytes 294916
  1.8 13.8 %copy-start.17 = (f32[4,12,1,512]{3,0,2,1:T(4,128)}, f32[4,12,1,512]{3,0,2,1:T(4,128)S(1)}, u32[]{:S(2)}) copy-start(f32[4,12,1,512]{3,0,2,1:T(4,128)S(1)} %get-tuple-element.18) | copy-start | bytes 294916
  1.9 13.7 %copy-start.78 = (f32[4,512]{1,0:T(4,128)}, f32[4,512]{1,0:T(4,128)S(1)}, u32[]{:S(2)}) copy-start(f32[4,512]{1,0:T(4,128)S(1)} %get-tuple-element.67) | copy-start | bytes 24580
  1.9 13.7 %copy-start.80 = (f32[4,512]{1,0:T(4,128)}, f32[4,512]{1,0:T(4,128)S(1)}, u32[]{:S(2)}) copy-start(f32[4,512]{1,0:T(4,128)S(1)} %get-tuple-element.68) | copy-start | bytes 24580
  1.9 13.7 %copy-start.82 = (f32[4,512]{1,0:T(4,128)}, f32[4,512]{1,0:T(4,128)S(1)}, u32[]{:S(2)}) copy-start(f32[4,512]{1,0:T(4,128)S(1)} %get-tuple-element.69) | copy-start | bytes 24580
  1.9 13.7 %copy-start.84 = (f32[4,512]{1,0:T(4,128)}, f32[4,512]{1,0:T(4,128)S(1)}, u32[]{:S(2)}) copy-start(f32[4,512]{1,0:T(4,128)S(1)} %get-tuple-element.70) | copy-start | bytes 24580
  1.9 13.7 %copy-start.86 = (f32[4,512]{1,0:T(4,128)}, f32[4,512]{1,0:T(4,128)S(1)}, u32[]{:S(2)}) copy-start(f32[4,512]{1,0:T(4,128)S(1)} %get-tuple-element.71) | copy-start | bytes 24580
  1.9 13.7 %copy-start.88 = (f32[4,512]{1,0:T(4,128)}, f32[4,512]{1,0:T(4,128)S(1)}, u32[]{:S(2)}) copy-start(f32[4,512]{1,0:T(4,128)S(1)} %get-tuple-element.72) | copy-start | bytes 24580
  1.9 13.7 %copy-start.90 = (f32[4,512]{1,0:T(4,128)}, f32[4,512]{1,0:T(4,128)S(1)}, u32[]{:S(2)}) copy-start(f32[4,512]{1,0:T(4,128)S(1)} %get-tuple-element.73) | copy-start | bytes 24580
  1.9 13.7 %copy-start.92 = (f32[4,512]{1,0:T(4,128)}, f32[4,512]{1,0:T(4,128)S(1)}, u32[]{:S(2)}) copy-start(f32[4,512]{1,0:T(4,128)S(1)} %get-tuple-element.74) | copy-start | bytes 24580
  1.9 13.7 %copy-start.94 = (f32[4,512]{1,0:T(4,128)}, f32[4,512]{1,0:T(4,128)S(1)}, u32[]{:S(2)}) copy-start(f32[4,512]{1,0:T(4,128)S(1)} %get-tuple-element.75) | copy-start | bytes 24580
  2.0 13.7 %copy-start.96 = (f32[4,512]{1,0:T(4,128)}, f32[4,512]{1,0:T(4,128)S(1)}, u32[]{:S(2)}) copy-start(f32[4,512]{1,0:T(4,128)S(1)} %get-tuple-element.76) | copy-start | bytes 24580
  2.0 13.7 %copy-start.98 = (f32[4,512]{1,0:T(4,128)}, f32[4,512]{1,0:T(4,128)S(1)}, u32[]{:S(2)}) copy-start(f32[4,512]{1,0:T(4,128)S(1)} %get-tuple-element.77) | copy-start | bytes 24580
  2.0 13.7 %copy-start.100 = (f32[4,512]{1,0:T(4,128)}, f32[4,512]{1,0:T(4,128)S(1)}, u32[]{:S(2)}) copy-start(f32[4,512]{1,0:T(4,128)S(1)} %get-tuple-element.78) | copy-start | bytes 24580
  2.0 13.4 %copy-start.131 = (s32[4,6]{1,0:T(4,128)S(1)}, s32[4,6]{1,0:T(4,128)}, u32[]{:S(2)}) copy-start(s32[4,6]{1,0:T(4,128)} %param.26) | copy-start | bytes 292
  2.0 13.4 %copy-start.132 = (s32[4,6]{1,0:T(4,128)S(1)}, s32[4,6]{1,0:T(4,128)}, u32[]{:S(2)}) copy-start(s32[4,6]{1,0:T(4,128)} %param.28) | copy-start | bytes 292
  2.0 13.4 %copy-start.133 = (s32[4,6]{1,0:T(4,128)S(1)}, s32[4,6]{1,0:T(4,128)}, u32[]{:S(2)}) copy-start(s32[4,6]{1,0:T(4,128)} %param.27) | copy-start | bytes 292
  3.9 21.8 %collective-permute-start = (f32[24,768]{1,0:T(8,128)S(1)}, f32[24,768]{1,0:T(8,128)S(1)}, u32[]{:S(2)}, u32[]{:S(2)}) collective-permute-start(f32[24,768]{1,0:T(8,128)S(1)} %reshape.370), channel_id=1, source_target_pairs={{0,1},{1,2},{2,3},{3,4},{4,5},{5,6},{6,7},{7,8},{8,9},{9,10},{10,1... | collective-permute-start | bytes 221192 | tf_op jit(solution)/shard_map/ppermute | solution.py:19
  5.8 19.9 %collective-permute-start.1 = (f32[24,768]{1,0:T(8,128)S(1)}, f32[24,768]{1,0:T(8,128)}, u32[]{:S(2)}, u32[]{:S(2)}) collective-permute-start(f32[24,768]{1,0:T(8,128)S(1)} %reshape.370), channel_id=1, source_target_pairs={{1,0},{2,1},{3,2},{4,3},{5,4},{6,5},{7,6},{8,7},{9,8},{10,9},{11,1... | collective-permute-start | bytes 221192 | tf_op jit(solution)/shard_map/ppermute | solution.py:19
  40.1 13.8 %copy-start.102 = (f32[24,192]{1,0:T(8,128)S(1)}, f32[24,192]{1,0:T(8,128)}, u32[]{:S(2)}) copy-start(f32[24,192]{1,0:T(8,128)} %reshape.372) | copy-start | bytes 55300
  40.1 13.8 %collective-permute-start.2 = (f32[24,192]{1,0:T(8,128)}, f32[24,192]{1,0:T(8,128)S(1)}, u32[]{:S(2)}, u32[]{:S(2)}) collective-permute-start(f32[24,192]{1,0:T(8,128)} %reshape.372), channel_id=1, source_target_pairs={{0,1},{1,2},{2,3},{3,4},{4,5},{5,6},{6,7},{7,8},{8,9},{9,10},{10,1... | collective-permute-start | bytes 55304 | tf_op jit(solution)/shard_map/ppermute | solution.py:19
  42.2 11.7 %collective-permute-start.3 = (f32[24,192]{1,0:T(8,128)}, f32[24,192]{1,0:T(8,128)S(1)}, u32[]{:S(2)}, u32[]{:S(2)}) collective-permute-start(f32[24,192]{1,0:T(8,128)} %reshape.372), channel_id=1, source_target_pairs={{1,0},{2,1},{3,2},{4,3},{5,4},{6,5},{7,6},{8,7},{9,8},{10,9},{11,1... | collective-permute-start | bytes 55304 | tf_op jit(solution)/shard_map/ppermute | solution.py:19
  72.9 13.9 %collective-permute-start.4 = (f32[24,192]{1,0:T(8,128)}, f32[24,192]{1,0:T(8,128)S(1)}, u32[]{:S(2)}, u32[]{:S(2)}) collective-permute-start(f32[24,192]{1,0:T(8,128)} %reshape.374), channel_id=1, source_target_pairs={{0,1},{1,2},{2,3},{3,4},{4,5},{5,6},{6,7},{7,8},{8,9},{9,10},{10,1... | collective-permute-start | bytes 55304 | tf_op jit(solution)/shard_map/ppermute | solution.py:19
  74.9 11.9 %collective-permute-start.5 = (f32[24,192]{1,0:T(8,128)}, f32[24,192]{1,0:T(8,128)S(1)}, u32[]{:S(2)}, u32[]{:S(2)}) collective-permute-start(f32[24,192]{1,0:T(8,128)} %reshape.374), channel_id=1, source_target_pairs={{1,0},{2,1},{3,2},{4,3},{5,4},{6,5},{7,6},{8,7},{9,8},{10,9},{11,1... | collective-permute-start | bytes 55304 | tf_op jit(solution)/shard_map/ppermute | solution.py:19
  107.4 12.7 %collective-permute-start.6 = (f32[24,768]{1,0:T(8,128)}, f32[24,768]{1,0:T(8,128)S(1)}, u32[]{:S(2)}, u32[]{:S(2)}) collective-permute-start(f32[24,768]{1,0:T(8,128)} %reshape.376), channel_id=1, source_target_pairs={{0,1},{1,2},{2,3},{3,4},{4,5},{5,6},{6,7},{7,8},{8,9},{9,10},{10,1... | collective-permute-start | bytes 221192 | tf_op jit(solution)/shard_map/ppermute | solution.py:19
  109.4 10.7 %collective-permute-start.7 = (f32[24,768]{1,0:T(8,128)}, f32[24,768]{1,0:T(8,128)S(1)}, u32[]{:S(2)}, u32[]{:S(2)}) collective-permute-start(f32[24,768]{1,0:T(8,128)} %reshape.376), channel_id=1, source_target_pairs={{1,0},{2,1},{3,2},{4,3},{5,4},{6,5},{7,6},{8,7},{9,8},{10,9},{11,1... | collective-permute-start | bytes 221192 | tf_op jit(solution)/shard_map/ppermute | solution.py:19
  139.2 13.2 %copy-start.129 = (pred[24]{0:T(512)(128)(4,1)S(1)}, pred[24]{0:T(512)(128)(4,1)}, u32[]{:S(2)}) copy-start(pred[24]{0:T(512)(128)(4,1)} %copy-done.128) | copy-start | bytes 76
  139.2 12.4 %collective-permute-start.8 = (f32[24,768]{1,0:T(8,128)S(1)}, f32[24,768]{1,0:T(8,128)S(1)}, u32[]{:S(2)}, u32[]{:S(2)}) collective-permute-start(f32[24,768]{1,0:T(8,128)S(1)} %reshape.378), channel_id=1, source_target_pairs={{0,1},{1,2},{2,3},{3,4},{4,5},{5,6},{6,7},{7,8},{8,9},{9,10},{10,1... | collective-permute-start | bytes 221192 | tf_op jit(solution)/shard_map/ppermute | solution.py:19
  141.1 10.5 %collective-permute-start.9 = (f32[24,768]{1,0:T(8,128)S(1)}, f32[24,768]{1,0:T(8,128)S(1)}, u32[]{:S(2)}, u32[]{:S(2)}) collective-permute-start(f32[24,768]{1,0:T(8,128)S(1)} %reshape.378), channel_id=1, source_target_pairs={{1,0},{2,1},{3,2},{4,3},{5,4},{6,5},{7,6},{8,7},{9,8},{10,9},{11,1... | collective-permute-start | bytes 221192 | tf_op jit(solution)/shard_map/ppermute | solution.py:19
  (113 other events, 355.0 us)
where the time goes:
time: 161 us; the launch traced here: 160 us
  starting transfers between devices  51.3 us (32%)
  matrix products  50.8 us (32%)
  local copies, waits for them, and re-layouts  42.5 us (26%)
  other arithmetic  12.7 us (8%)
  between operations  2.32 us (1%)
    ppermute x10, starting transfers between devices, from_behind(): return lax.ppermute(block, axis, route)  51.3 us
    dot_general x5, matrix products, pick_faces(): jnp.dot(gathered.reshape(count * variables, span), turns, precision=PRECISE)  10.3 us
    dot_general x5, matrix products, pick_faces(): oriented = jnp.einsum('cvtq,ct->cvq', rotated, weights, precision=PRECISE)  9.23 us
    dot_general x5, matrix products, faces_of(): jnp.dot(iterate.reshape(elements * variables, -1), matrix, precision=PREC...  9.2 us
    gather x5, local copies, waits for them, and re-layouts, pick_faces(): gathered = jnp.take(pooled, slot_ids, axis=0)  8.02 us
    dot_general x5, local copies, waits for them, and re-layouts, pick_faces(): jnp.dot(gathered.reshape(count * variables, span), turns, precision=PRECISE)  7.94 us
    dot_general x6, local copies, waits for them, and re-layouts, finish(): jnp.dot(jumps.transpose(0, 2, 1, 3).reshape(elements * variables, 6 * fac...  6.55 us
    reshape x5, local copies, waits for them, and re-layouts, faces_of(): return traced.reshape(elements * 6, variables * face_span)  6.05 us
  transfers between devices with their start and end apart: 10, of which 0 were waited for; matrix products, arithmetic and copies ran while one was open for 14% of the time, Pallas kernels for 0%

commit v1 on v0

v1 whole, which is shorter than its diff:
```python
import jax
import jax.numpy as jnp
import numpy as np
from jax import lax
from jax.experimental import pallas as pl
from jax.experimental.pallas import tpu as pltpu
from jax.sharding import PartitionSpec as P


QF = 8
QC = 4
VARS = 12
SIGMA = 2.0
OMEGA = 0.7
F32 = jnp.float32
BF16 = jnp.bfloat16
VMEM = pltpu.VMEM


def trace_matrix():
    matrix = np.zeros((512, 384), np.float32)
    for i in range(QF):
        for j in range(QF):
            for k in range(QF):
                mode = (i * QF + j) * QF + k
                triple = (i, j, k)
                for face in range(6):
                    normal = triple[face // 2]
                    a, b = [triple[place] for place in range(3) if place != face // 2]
                    matrix[mode, face * 64 + a * 8 + b] = (-1.0) ** normal if face % 2 == 0 else 1.0
    return matrix


def lift_matrix():
    degrees = np.stack(np.meshgrid(*[np.arange(QF)] * 3, indexing="ij"), -1).reshape(512, 3)
    scale = np.stack([(2.0 * degrees[:, face // 2] + 1.0) / 16.0 for face in range(6)], -1)
    return (trace_matrix().reshape(512, 6, 64) * scale[:, :, None]).reshape(512, 384).T


def rows8():
    return lax.broadcasted_iota(jnp.int32, (8, 128), 0)


def lanes8():
    return lax.broadcasted_iota(jnp.int32, (8, 128), 1)


def half_swap(tile):
    return pltpu.roll(tile, 4, axis=0)


def pair_turn(first, second, low):
    return jnp.where(low, first, half_swap(second)), jnp.where(low, half_swap(first), second)


def prepare_body(me_ref, owner_ref, elem_ref, side_ref, turn_ref, vj_ref, fj_ref, stiff_ref,
                 start_ref, idx_ref, sign_ref, vjc_ref, fjc_ref, khi_ref, klo_ref):
    me = me_ref[0]
    rows = rows8()
    lane = lanes8()
    low = rows < 4
    element = rows & 3
    a = (lane >> 3) & 7
    b = lane & 7
    signs = []
    for face in range(6):
        swap = jnp.zeros((8, 128), jnp.int32)
        parity = jnp.zeros((8, 128), jnp.int32)
        turns = jnp.zeros((8, 128), jnp.int32)
        present = jnp.zeros((8, 128), jnp.int32)
        for e in range(4):
            owner = owner_ref[e, face]
            side = side_ref[e, face]
            block = jnp.where(owner == me, 0, jnp.where(owner == (me ^ 1), 1, 2))
            block = jnp.where(owner < 0, 0, block)
            start_ref[face * 4 + e] = block * 144 + (side >> 1) * 48 + elem_ref[e, face]
            here = element == e
            turns = jnp.where(here, turn_ref[e, face], turns)
            parity = jnp.where(here, side & 1, parity)
            present = jnp.where(here, jnp.where(owner >= 0, 1, 0), present)
        swap = turns & 1
        idx_ref[face] = parity * 64 + jnp.where(swap == 1, b * 8 + a, a * 8 + b)
        flips = (((turns >> 1) & a) + ((turns >> 2) & b)) & 1
        signs.append((present * (1 - 2 * flips)).astype(F32))
    for f2 in range(3):
        sign_ref[f2] = jnp.where(lane < 64, signs[2 * f2], signs[2 * f2 + 1])
    for vp in range(6):
        block = vj_ref[vp]
        for w in range(VARS):
            spread = jnp.broadcast_to(block[:, w : w + 1], (8, 128))
            other = half_swap(spread)
            vjc_ref[(2 * vp) * VARS + w] = jnp.where(low, spread, other)
            vjc_ref[(2 * vp + 1) * VARS + w] = jnp.where(low, other, spread)
    for f2 in range(3):
        for vp in range(6):
            even = fj_ref[2 * f2 * 6 + vp]
            odd = fj_ref[(2 * f2 + 1) * 6 + vp]
            for w in range(VARS):
                fjc_ref[(f2 * 6 + vp) * VARS + w] = jnp.where(
                    lane < 64,
                    jnp.broadcast_to(even[:, w : w + 1], (8, 128)),
                    jnp.broadcast_to(odd[:, w : w + 1], (8, 128)),
                )
    stiff = stiff_ref[...]
    high = stiff.astype(BF16)
    khi_ref[...] = high
    klo_ref[...] = (stiff - high.astype(F32)).astype(BF16)


def apply_inverse(inv_ref, residual, halves):
    result = {}
    for h in range(halves):
        for v in range(VARS):
            acc = inv_ref[(v * VARS) * 2 + h] * residual[0, h]
            for w in range(1, VARS):
                acc = acc + inv_ref[(v * VARS + w) * 2 + h] * residual[w, h]
            result[v, h] = OMEGA * acc
    return result


def store_split(ref, row, column, first, second):
    both = jnp.concatenate([first, second], axis=0)
    high = both.astype(BF16)
    ref[row : row + 16, column : column + 128] = high
    ref[48 + row : 64 + row, column : column + 128] = (both - high.astype(F32)).astype(BF16)


def emit(state, halves, trace_ref, split_ref, face_ref):
    low = rows8() < 4
    for h in range(halves):
        matrix = {}
        for vp in range(6):
            matrix[vp] = pair_turn(state[2 * vp, h], state[2 * vp + 1, h], low)
        for part in range(2):
            for vq in range(3):
                store_split(split_ref, vq * 16, (2 * h + part) * 128, matrix[2 * vq][part], matrix[2 * vq + 1][part])
    width = 256 * halves
    both = jnp.dot(split_ref[:, :width], trace_ref[:width, :], preferred_element_type=F32)
    traces = both[:48] + both[48:]
    for f2 in range(3):
        face_ref[f2 * 48 : f2 * 48 + 48, :] = traces[:, f2 * 128 : f2 * 128 + 128]


def to_state(matrix, halves, low):
    state = {}
    for h in range(halves):
        for vp in range(6):
            first = matrix[vp * 8 : vp * 8 + 8, 256 * h : 256 * h + 128]
            second = matrix[vp * 8 : vp * 8 + 8, 256 * h + 128 : 256 * h + 256]
            state[2 * vp, h], state[2 * vp + 1, h] = pair_turn(first, second, low)
    return state


def residual_of(u_ref, base_ref, split_ref, own_ref, even_ref, odd_ref, start_ref, idx_ref, sign_ref,
                vjc_ref, fjc_ref, khi_ref, klo_ref, lift_ref, pool, pick0, pick1, jump_ref, halves_in, halves):
    low = rows8() < 4
    left = lanes8() < 64
    pool[0:144, :] = own_ref[...]
    pool[144:288, :] = even_ref[...]
    pool[288:432, :] = odd_ref[...]
    for face in range(6):
        target = pick1 if face % 2 else pick0
        for e in range(4):
            target[pl.ds((face // 2) * 48 + e, 12, stride=4), :] = pool[pl.ds(start_ref[face * 4 + e], 12, stride=4), :]
    for f2 in range(3):
        spread = {}
        for vp in range(6):
            at = f2 * 48 + vp * 8
            even = jnp.take_along_axis(pick0[at : at + 8, :], idx_ref[2 * f2], axis=1)
            odd = jnp.take_along_axis(pick1[at : at + 8, :], idx_ref[2 * f2 + 1], axis=1)
            jump = own_ref[at : at + 8, :] - jnp.where(left, even, odd) * sign_ref[f2]
            spread[2 * vp], spread[2 * vp + 1] = pair_turn(jump, jump, low)
        flux = []
        for vp in range(6):
            acc = fjc_ref[(f2 * 6 + vp) * VARS] * spread[0]
            for w in range(1, VARS):
                acc = acc + fjc_ref[(f2 * 6 + vp) * VARS + w] * spread[w]
            flux.append(acc)
        for vq in range(3):
            store_split(jump_ref, vq * 16, f2 * 128, flux[2 * vq], flux[2 * vq + 1])
    kin = 256 * halves_in
    kout = 256 * halves
    blended = jnp.dot(split_ref[:, :kin], khi_ref[:kin, :kout], preferred_element_type=F32)
    rest = jnp.dot(split_ref[0:48, :kin], klo_ref[:kin, :kout], preferred_element_type=F32)
    blended = to_state(blended[:48] + blended[48:] + rest, halves, low)
    lifted = jnp.dot(jump_ref[...], lift_ref[:, :kout], preferred_element_type=F32)
    lifted = to_state(lifted[:48] + lifted[48:], halves, low)
    residual = {}
    for h in range(halves):
        for v in range(VARS):
            acc = vjc_ref[v * VARS] * blended[0, h]
            for w in range(1, VARS):
                acc = acc + vjc_ref[v * VARS + w] * blended[w, h]
            residual[v, h] = base_ref[2 * v + h] - SIGMA * u_ref[2 * v + h] - acc - lifted[v, h]
    return residual


def coarse_mask():
    lane = lanes8()
    return jnp.where((((lane >> 3) & 7) < QC) & ((lane & 7) < QC), 1.0, 0.0).astype(F32)


def zero_tile():
    return jnp.zeros((8, 128), F32)


def first_body(inv_ref, rhs_ref, trace_ref, u_ref, split_ref, face_ref):
    state = apply_inverse(inv_ref, {(v, h): rhs_ref[2 * v + h] for v in range(VARS) for h in range(2)}, 2)
    for v in range(VARS):
        for h in range(2):
            u_ref[2 * v + h] = state[v, h]
    emit(state, 2, trace_ref, split_ref, face_ref)


def fine_body(inv_ref, trace_ref, u_ref, *rest):
    shared, (out_ref, split_ref, face_ref), scratch = rest[:13], rest[13:16], rest[16:]
    residual = residual_of(u_ref, *shared, *scratch, 2, 2)
    state = apply_inverse(inv_ref, residual, 2)
    for v in range(VARS):
        for h in range(2):
            state[v, h] = state[v, h] + u_ref[2 * v + h]
            out_ref[2 * v + h] = state[v, h]
    emit(state, 2, trace_ref, split_ref, face_ref)


def last_body(inv_ref, u_ref, *rest):
    shared, out_ref, scratch = rest[:13], rest[13], rest[14:]
    residual = residual_of(u_ref, *shared, *scratch, 2, 2)
    state = apply_inverse(inv_ref, residual, 2)
    for v in range(VARS):
        for h in range(2):
            out_ref[2 * v + h] = state[v, h] + u_ref[2 * v + h]


def restrict_body(inv_ref, trace_ref, u_ref, *rest):
    shared, (low_ref, out_ref, split_ref, face_ref), scratch = rest[:13], rest[13:17], rest[17:]
    residual = residual_of(u_ref, *shared, *scratch, 2, 1)
    mask = coarse_mask()
    residual = {key: tile * mask for key, tile in residual.items()}
    state = apply_inverse(inv_ref, residual, 1)
    for v in range(VARS):
        low_ref[2 * v] = residual[v, 0]
        low_ref[2 * v + 1] = zero_tile()
        out_ref[2 * v] = state[v, 0]
        out_ref[2 * v + 1] = zero_tile()
    emit(state, 1, trace_ref, split_ref, face_ref)


def coarse_body(inv_ref, trace_ref, fine_ref, u_ref, *rest):
    shared, (out_ref, split_ref, face_ref), scratch = rest[:13], rest[13:16], rest[16:]
    residual = residual_of(u_ref, *shared, *scratch, 1, 1)
    mask = coarse_mask()
    residual = {key: tile * mask for key, tile in residual.items()}
    state = apply_inverse(inv_ref, residual, 1)
    for v in range(VARS):
        state[v, 0] = state[v, 0] + u_ref[2 * v] + fine_ref[2 * v]
        state[v, 1] = fine_ref[2 * v + 1]
        out_ref[2 * v] = state[v, 0]
        out_ref[2 * v + 1] = state[v, 1]
    emit(state, 2, trace_ref, split_ref, face_ref)


STATE = VMEM((24, 8, 128), F32)
SPLIT = VMEM((96, 512), BF16)
FACES = VMEM((144, 128), F32)


def in_vmem(value):
    return pltpu.with_memory_space_constraint(value, VMEM)


def call(body, outs, args, scratch=(), smem=(), smem_outs=()):
    spec = pl.BlockSpec(memory_space=VMEM)
    scalar = pl.BlockSpec(memory_space=pltpu.SMEM)
    return pl.pallas_call(
        body,
        out_shape=list(outs),
        in_specs=[scalar if at in smem else spec for at in range(len(args))],
        out_specs=[scalar if at in smem_outs else spec for at in range(len(outs))],
        scratch_shapes=list(scratch),
        compiler_params=pltpu.CompilerParams(vmem_limit_bytes=32 * 1024 * 1024),
    )(*args)


def exchange(faces):
    count = lax.axis_size("dom")
    odd = []
    for at in range(1, count - 1, 2):
        odd += [(at, at + 1), (at + 1, at)]
    even = [(at, at ^ 1) for at in range(count)]
    from_odd = lax.ppermute(faces, "dom", odd)
    from_even = lax.ppermute(faces, "dom", even)
    return in_vmem(from_even), in_vmem(from_odd)


def local(rhs, stiffness, vol_jac, face_jac, block_inv, face_owner, face_elem, face_side, face_turn):
    me = lax.axis_index("dom").astype(jnp.int32).reshape(1)
    rhs_state = in_vmem(rhs.reshape(4, 12, 4, 128).transpose(1, 2, 0, 3).reshape(24, 8, 128))
    inverse = in_vmem(block_inv.reshape(4, 12, 12, 4, 128).transpose(1, 2, 3, 0, 4).reshape(288, 8, 128))
    vj = vol_jac.transpose(1, 0, 2).reshape(6, 8, 12)
    fj = face_jac.transpose(1, 2, 0, 3).reshape(36, 8, 12)
    trace = in_vmem(jnp.asarray(trace_matrix(), BF16))
    lift = in_vmem(jnp.asarray(lift_matrix(), BF16))

    u, split, faces = call(first_body, (STATE, SPLIT, FACES), (inverse, rhs_state, trace))
    start, idx, sign, vjc, fjc, khi, klo = call(
        prepare_body,
        (
            pltpu.SMEM((24,), jnp.int32),
            VMEM((6, 8, 128), jnp.int32),
            VMEM((3, 8, 128), F32),
            VMEM((144, 8, 128), F32),
            VMEM((216, 8, 128), F32),
            VMEM((512, 512), BF16),
            VMEM((512, 512), BF16),
        ),
        (me, face_owner, face_elem, face_side, face_turn, vj, fj, stiffness),
        smem=(0, 1, 2, 3, 4),
        smem_outs=(0,),
    )
    tables = (start, idx, sign, vjc, fjc, khi, klo, lift)
    scratch = (VMEM((432, 128), F32), FACES, FACES, VMEM((96, 384), BF16))

    def stage(body, outs, head, u, base, split, faces):
        even, odd = exchange(faces)
        args = (*head, u, base, split, faces, even, odd, *tables)
        return call(body, outs, args, scratch, smem=(len(head) + 6,))

    fine_two, split, faces = stage(fine_body, (STATE, SPLIT, FACES), (inverse, trace), u, rhs_state, split, faces)
    low_rhs, coarse, split, faces = stage(
        restrict_body, (STATE, STATE, SPLIT, FACES), (inverse, trace), fine_two, rhs_state, split, faces
    )
    u, split, faces = stage(
        coarse_body, (STATE, SPLIT, FACES), (inverse, trace, fine_two), coarse, low_rhs, split, faces
    )
    u, split, faces = stage(fine_body, (STATE, SPLIT, FACES), (inverse, trace), u, rhs_state, split, faces)
    (u,) = stage(last_body, (jax.ShapeDtypeStruct((24, 8, 128), F32),), (inverse,), u, rhs_state, split, faces)
    return u.reshape(12, 4, 4, 128).transpose(2, 0, 1, 3).reshape(4, 12, 512)


def solution(mesh):
    dom = P("dom")
    return jax.shard_map(
        local,
        mesh=mesh,
        in_specs=(dom, P(), dom, dom, dom, dom, dom, dom, dom),
        out_specs=dom,
        check_vma=False,
    )
```

time: 161 us -> 64 us (0.40)
  matrix products: 50.8 us -> 0 us
  local copies, waits for them, and re-layouts: 42.5 us -> 8.1 us
  starting transfers between devices: 51.3 us -> 22.4 us
  waiting for transfers between devices: 0.03 us -> 26.9 us
  other arithmetic: 12.7 us -> 0 us
  Pallas kernels: 0 us -> 5.85 us
  between operations: 2.32 us -> 0.21 us
    dot_general x40 -> x0, matrix products: 50.8 us -> none  [the longest x5 10.3 us: pick_faces(): jnp.dot(gathered.reshape(count * variables, span), turns, precision=PRECISE)]
    ppermute x10, starting transfers between devices: 51.3 us -> 22.4 us  [the longest x5 22 us: exchange(): from_odd = lax.ppermute(faces, 'dom', odd)]
    ppermute x10, waiting for transfers between devices: 0.03 us -> 26.9 us  [the longest x5 26.9 us: exchange(): from_odd = lax.ppermute(faces, 'dom', odd)]
    dot_general x16 -> x0, local copies, waits for them, and re-layouts: 14.6 us -> none  [the longest x5 7.94 us: pick_faces(): jnp.dot(gathered.reshape(count * variables, span), turns, precision=PRECISE)]
    gather x5 -> x0, local copies, waits for them, and re-layouts: 8.02 us -> none  [pick_faces(): gathered = jnp.take(pooled, slot_ids, axis=0)]
    reshape x5 -> x0, local copies, waits for them, and re-layouts: 6.05 us -> none  [faces_of(): return traced.reshape(elements * 6, variables * face_span)]
    pallas_call x0 -> x7, Pallas kernels: none -> 5.85 us  [call(): pl.pallas_call(body, out_shape=list(outs), in_specs=[scalar if at in smem...]
    select_n x7 -> x0, other arithmetic: 4.6 us -> none  [the longest x6 4.59 us: pick_faces(): gathered = jnp.take(pooled, slot_ids, axis=0)]
  transfers between devices with their start and end apart: 10 -> 10, of which waited for: 0 -> 4; matrix products, arithmetic and copies ran while one was open for 14% -> 0% of each run, Pallas kernels for 0% -> 3%
where the time goes in v1:
time: 64 us; the launch traced here: 63.5 us
  waiting for transfers between devices  26.9 us (42%)
  starting transfers between devices  22.4 us (35%)
  local copies, waits for them, and re-layouts  8.1 us (13%)
  Pallas kernels  5.85 us (9%)
    ppermute x5, waiting for transfers between devices, exchange(): from_odd = lax.ppermute(faces, 'dom', odd)  26.9 us
    ppermute x5, starting transfers between devices, exchange(): from_odd = lax.ppermute(faces, 'dom', odd)  22 us
    unnamed x28, local copies, waits for them, and re-layouts  8.1 us
    pallas_call x7, Pallas kernels, call(): pl.pallas_call(body, out_shape=list(outs), in_specs=[scalar if at in smem...  5.85 us
  transfers between devices with their start and end apart: 10, of which 4 were waited for; matrix products, arithmetic and copies ran while one was open for 0% of the time, Pallas kernels for 3%

profile of v1, /device:TPU:24, one launch (start us, length us, event | category | flops | bytes accessed | tf_op | source)
XLA Modules:
  0.0 63.5 jit_solution(14656478126589609553)
XLA Ops:
  0.0 1.3 %copy-done = f32[4,12,12,512]{3,0,2,1:T(4,128)S(1)} copy-done((f32[4,12,12,512]{3,0,2,1:T(4,128)S(1)}, f32[4,12,12,512]{3,0,2,1:T(4,128)}, u32[]{:S(2)}) %copy-start) | copy-done | bytes 1179672
  1.3 1.0 %copy-done.3 = bf16[512,384]{1,0:T(8,128)(2,1)S(1)} copy-done((bf16[512,384]{1,0:T(8,128)(2,1)S(1)}, bf16[512,384]{1,0:T(8,128)(2,1)}, u32[]{:S(2)}) %copy-start.3) | copy-done | bytes 393240
  2.3 0.9 %copy-done.5 = f32[4,12,512]{2,0,1:T(4,128)S(1)} copy-done((f32[4,12,512]{2,0,1:T(4,128)S(1)}, f32[4,12,512]{2,0,1:T(4,128)}, u32[]{:S(2)}) %copy-start.5) | copy-done | bytes 98328
  3.2 0.3 shard_map.109
  3.5 9.7 %collective-permute-start.1 = (f32[144,128]{1,0:T(8,128)S(1)}, f32[144,128]{1,0:T(8,128)S(1)}, u32[]{:S(2)}, u32[]{:S(2)}) collective-permute-start(f32[144,128]{1,0:T(8,128)S(1)} %get-tuple-element.30.rest_2_), channel_id=1, source_target_pairs={{1,2},{2,1},{3,4},{4,3},{5,6},{6,5},{7,8},{8,7},{9,10},{10,9},{11,... | collective-permute-start | bytes 221192 | tf_op jit(solution)/shard_map/ppermute | solution.py:291
  13.2 0.1 collective-permute-start
  13.3 0.0 copy-start.7
  13.3 1.2 %copy-done.7 = f32[512,512]{1,0:T(8,128)S(1)} copy-done((f32[512,512]{1,0:T(8,128)S(1)}, f32[512,512]{1,0:T(8,128)}, u32[]{:S(2)}) %copy-start.7) | copy-done | bytes 1048600
  14.5 0.9 %copy-done.8 = f32[4,6,12,12]{3,0,2,1:T(4,128)S(1)} copy-done((f32[4,6,12,12]{3,0,2,1:T(4,128)S(1)}, f32[4,6,12,12]{3,0,2,1:T(4,128)}, u32[]{:S(2)}) %copy-start.8) | copy-done | bytes 13848
  15.4 0.7 %copy-done.9 = f32[4,12,12]{2,0,1:T(4,128)S(1)} copy-done((f32[4,12,12]{2,0,1:T(4,128)S(1)}, f32[4,12,12]{2,0,1:T(4,128)}, u32[]{:S(2)}) %copy-start.9) | copy-done | bytes 2328
  16.2 0.7 %copy-done.11 = s32[4,6]{1,0:T(4,128)S(1)} copy-done((s32[4,6]{1,0:T(4,128)S(1)}, s32[4,6]{1,0:T(4,128)}, u32[]{:S(2)}) %copy-start.11) | copy-done | bytes 120
  16.9 0.7 %copy-done.12 = s32[4,6]{1,0:T(4,128)S(1)} copy-done((s32[4,6]{1,0:T(4,128)S(1)}, s32[4,6]{1,0:T(4,128)}, u32[]{:S(2)}) %copy-start.12) | copy-done | bytes 120
  17.5 0.7 %copy-done.13 = s32[4,6]{1,0:T(4,128)S(1)} copy-done((s32[4,6]{1,0:T(4,128)S(1)}, s32[4,6]{1,0:T(4,128)}, u32[]{:S(2)}) %copy-start.13) | copy-done | bytes 120
  18.2 1.7 %shard_map.110 = (s32[24]{0:T(128)S(4)}, s32[6,8,128]{2,1,0:T(8,128)S(1)}, f32[3,8,128]{2,1,0:T(8,128)S(1)}, f32[144,8,128]{2,1,0:T(8,128)S(1)}, f32[216,8,128]{...) custom-call(s32[1]{0:T(128)} %bitcast.8.me_ref, s32[4,6]{1,0:T(4,128)S(1)} %copy-done.10, ...), custom_call_target="tpu_custom_call" | custom-call | tf_op jit(solution)/shard_map/pallas_call | solution.py:275
  20.0 0.0 collective-permute-done.1.rest_4_
  20.0 0.7 %shard_map.111 = (f32[24,8,128]{2,1,0:T(8,128)S(1)}, bf16[96,512]{1,0:T(8,128)(2,1)S(1)}, f32[144,128]{1,0:T(8,128)S(1)}) custom-call(f32[288,8,128]{2,1,0:T(8,128)S(1)} %bitcast.23, bf16[512,384]{1,0:T(8,128)(2,1)S(1)} %copy-done.4, f32[24,8,128]{2,1,0:T(8,128)S(1)} %get-tuple-element.28.u_ref, f32[24,8,128]{2,1,0:T(8,128)S(1)} %bitcast.29, ...), custom_call_target="tpu_custom_call" | custom-call | tf_op jit(solution)/shard_map/pallas_call | solution.py:275
  20.8 3.1 %collective-permute-start.3 = (f32[144,128]{1,0:T(8,128)S(1)}, f32[144,128]{1,0:T(8,128)S(1)}, u32[]{:S(2)}, u32[]{:S(2)}) collective-permute-start(f32[144,128]{1,0:T(8,128)S(1)} %get-tuple-element.40.rest_2_), channel_id=1, source_target_pairs={{1,2},{2,1},{3,4},{4,3},{5,6},{6,5},{7,8},{8,7},{9,10},{10,9},{11,... | collective-permute-start | bytes 221192 | tf_op jit(solution)/shard_map/ppermute | solution.py:291
  23.8 0.1 collective-permute-start.2
  23.9 6.7 %collective-permute-done.3.rest_4_ = f32[144,128]{1,0:T(8,128)S(1)} collective-permute-done((f32[144,128]{1,0:T(8,128)S(1)}, f32[144,128]{1,0:T(8,128)S(1)}, u32[]{:S(2)}, u32[]{:S(2)}) %collective-permute-start.3) | collective-permute-done | bytes 73760 | tf_op jit(solution)/shard_map/ppermute | solution.py:291
  30.7 0.6 shard_map.112
  31.3 3.1 %collective-permute-start.5 = (f32[144,128]{1,0:T(8,128)S(1)}, f32[144,128]{1,0:T(8,128)S(1)}, u32[]{:S(2)}, u32[]{:S(2)}) collective-permute-start(f32[144,128]{1,0:T(8,128)S(1)} %get-tuple-element.44.rest_2_), channel_id=1, source_target_pairs={{1,2},{2,1},{3,4},{4,3},{5,6},{6,5},{7,8},{8,7},{9,10},{10,9},{11,... | collective-permute-start | bytes 221192 | tf_op jit(solution)/shard_map/ppermute | solution.py:291
  34.3 0.1 collective-permute-start.4
  34.4 6.7 %collective-permute-done.5.rest_4_ = f32[144,128]{1,0:T(8,128)S(1)} collective-permute-done((f32[144,128]{1,0:T(8,128)S(1)}, f32[144,128]{1,0:T(8,128)S(1)}, u32[]{:S(2)}, u32[]{:S(2)}) %collective-permute-start.5) | collective-permute-done | bytes 73760 | tf_op jit(solution)/shard_map/ppermute | solution.py:291
  41.2 0.6 shard_map.113
  41.8 3.1 %collective-permute-start.7 = (f32[144,128]{1,0:T(8,128)S(1)}, f32[144,128]{1,0:T(8,128)S(1)}, u32[]{:S(2)}, u32[]{:S(2)}) collective-permute-start(f32[144,128]{1,0:T(8,128)S(1)} %get-tuple-element.47.rest_2_), channel_id=1, source_target_pairs={{1,2},{2,1},{3,4},{4,3},{5,6},{6,5},{7,8},{8,7},{9,10},{10,9},{11,... | collective-permute-start | bytes 221192 | tf_op jit(solution)/shard_map/ppermute | solution.py:291
  44.8 0.1 collective-permute-start.6
  44.9 6.7 %collective-permute-done.7.rest_4_ = f32[144,128]{1,0:T(8,128)S(1)} collective-permute-done((f32[144,128]{1,0:T(8,128)S(1)}, f32[144,128]{1,0:T(8,128)S(1)}, u32[]{:S(2)}, u32[]{:S(2)}) %collective-permute-start.7) | collective-permute-done | bytes 73760 | tf_op jit(solution)/shard_map/ppermute | solution.py:291
  51.7 0.7 %shard_map.114 = (f32[24,8,128]{2,1,0:T(8,128)S(1)}, bf16[96,512]{1,0:T(8,128)(2,1)S(1)}, f32[144,128]{1,0:T(8,128)S(1)}) custom-call(f32[288,8,128]{2,1,0:T(8,128)S(1)} %bitcast.26, bf16[512,384]{1,0:T(8,128)(2,1)S(1)} %copy-done.4, f32[24,8,128]{2,1,0:T(8,128)S(1)} %get-tuple-element.45.u_ref, f32[24,8,128]{2,1,0:T(8,128)S(1)} %bitcast.31, ...), custom_call_target="tpu_custom_call" | custom-call | tf_op jit(solution)/shard_map/pallas_call | solution.py:275
  52.4 3.1 %collective-permute-start.9 = (f32[144,128]{1,0:T(8,128)S(1)}, f32[144,128]{1,0:T(8,128)S(1)}, u32[]{:S(2)}, u32[]{:S(2)}) collective-permute-start(f32[144,128]{1,0:T(8,128)S(1)} %get-tuple-element.50.rest_2_), channel_id=1, source_target_pairs={{1,2},{2,1},{3,4},{4,3},{5,6},{6,5},{7,8},{8,7},{9,10},{10,9},{11,... | collective-permute-start | bytes 221192 | tf_op jit(solution)/shard_map/ppermute | solution.py:291
  55.5 0.1 collective-permute-start.8
  55.6 6.7 %collective-permute-done.9.rest_4_ = f32[144,128]{1,0:T(8,128)S(1)} collective-permute-done((f32[144,128]{1,0:T(8,128)S(1)}, f32[144,128]{1,0:T(8,128)S(1)}, u32[]{:S(2)}, u32[]{:S(2)}) %collective-permute-start.9) | collective-permute-done | bytes 73760 | tf_op jit(solution)/shard_map/ppermute | solution.py:291
  62.3 1.2 %shard_map.115 = f32[24,8,128]{2,1,0:T(8,128)} custom-call(f32[288,8,128]{2,1,0:T(8,128)S(1)} %bitcast.27, f32[24,8,128]{2,1,0:T(8,128)S(1)} %get-tuple-element.48.u_ref, f32[24,8,128]{2,1,0:T(8,128)S(1)} %bitcast.32, bf16[96,512]{1,0:T(8,128)(2,1)S(1)} %get-tuple-element.49.rest_1_, f32[144,128]{1,0:T(8,128)S(1)} %get-tuple-element.50.rest_2_, ...), custom_call_target="tpu_custom_call" | custom-call | tf_op jit(solution)/shard_map/pallas_call | solution.py:275
  (23 shorter events, 0.0 us)
Async XLA Ops:
  0.0 13.3 %copy-start.10 = (s32[4,6]{1,0:T(4,128)S(1)}, s32[4,6]{1,0:T(4,128)}, u32[]{:S(2)}) copy-start(s32[4,6]{1,0:T(4,128)} %owner_ref.1) | copy-start | bytes 292
  0.0 1.3 %copy-start = (f32[4,12,12,512]{3,0,2,1:T(4,128)S(1)}, f32[4,12,12,512]{3,0,2,1:T(4,128)}, u32[]{:S(2)}) copy-start(f32[4,12,12,512]{3,0,2,1:T(4,128)} %param.15) | copy-start | bytes 3538948
  1.3 1.0 %copy-start.3 = (bf16[512,384]{1,0:T(8,128)(2,1)S(1)}, bf16[512,384]{1,0:T(8,128)(2,1)}, u32[]{:S(2)}) copy-start(bf16[512,384]{1,0:T(8,128)(2,1)} %constant.8.clone.trace_ref) | copy-start | bytes 1179652
  2.3 0.9 %copy-start.5 = (f32[4,12,512]{2,0,1:T(4,128)S(1)}, f32[4,12,512]{2,0,1:T(4,128)}, u32[]{:S(2)}) copy-start(f32[4,12,512]{2,0,1:T(4,128)} %param.11) | copy-start | bytes 294916
  3.2 16.8 %copy-start.1 = (f32[4,12,12,512]{3,0,2,1:T(4,128)S(1)}, f32[4,12,12,512]{3,0,2,1:T(4,128)}, u32[]{:S(2)}) copy-start(f32[4,12,12,512]{3,0,2,1:T(4,128)} %param.15) | copy-start | bytes 3538948
  3.2 16.8 %copy-start.2 = (bf16[384,512]{1,0:T(8,128)(2,1)S(1)}, bf16[384,512]{1,0:T(8,128)(2,1)}, u32[]{:S(2)}) copy-start(bf16[384,512]{1,0:T(8,128)(2,1)} %constant.9.clone.rest_12_) | copy-start | bytes 1179652
  3.2 16.8 %copy-start.4 = (bf16[512,384]{1,0:T(8,128)(2,1)S(1)}, bf16[512,384]{1,0:T(8,128)(2,1)}, u32[]{:S(2)}) copy-start(bf16[512,384]{1,0:T(8,128)(2,1)} %constant.8.clone.trace_ref) | copy-start | bytes 1179652
  3.2 16.8 %copy-start.6 = (f32[4,12,512]{2,0,1:T(4,128)S(1)}, f32[4,12,512]{2,0,1:T(4,128)}, u32[]{:S(2)}) copy-start(f32[4,12,512]{2,0,1:T(4,128)} %param.11) | copy-start | bytes 294916
  3.5 16.5 %collective-permute-start.1 = (f32[144,128]{1,0:T(8,128)S(1)}, f32[144,128]{1,0:T(8,128)S(1)}, u32[]{:S(2)}, u32[]{:S(2)}) collective-permute-start(f32[144,128]{1,0:T(8,128)S(1)} %get-tuple-element.30.rest_2_), channel_id=1, source_target_pairs={{1,2},{2,1},{3,4},{4,3},{5,6},{6,5},{7,8},{8,7},{9,10},{10,9},{11,... | collective-permute-start | bytes 221192 | tf_op jit(solution)/shard_map/ppermute | solution.py:291
  13.2 6.8 %collective-permute-start = (f32[144,128]{1,0:T(8,128)S(1)}, f32[144,128]{1,0:T(8,128)S(1)}, u32[]{:S(2)}, u32[]{:S(2)}) collective-permute-start(f32[144,128]{1,0:T(8,128)S(1)} %get-tuple-element.30.rest_2_), channel_id=1, source_target_pairs={{0,1},{1,0},{2,3},{3,2},{4,5},{5,4},{6,7},{7,6},{8,9},{9,8},{10,11... | collective-permute-start | bytes 221192 | tf_op jit(solution)/shard_map/ppermute | solution.py:292
  13.3 1.2 %copy-start.7 = (f32[512,512]{1,0:T(8,128)S(1)}, f32[512,512]{1,0:T(8,128)}, u32[]{:S(2)}) copy-start(f32[512,512]{1,0:T(8,128)} %stiff_ref.1) | copy-start | bytes 3145732
  14.5 0.9 %copy-start.8 = (f32[4,6,12,12]{3,0,2,1:T(4,128)S(1)}, f32[4,6,12,12]{3,0,2,1:T(4,128)}, u32[]{:S(2)}) copy-start(f32[4,6,12,12]{3,0,2,1:T(4,128)} %param.14) | copy-start | bytes 41476
  15.4 0.7 %copy-start.9 = (f32[4,12,12]{2,0,1:T(4,128)S(1)}, f32[4,12,12]{2,0,1:T(4,128)}, u32[]{:S(2)}) copy-start(f32[4,12,12]{2,0,1:T(4,128)} %param.13) | copy-start | bytes 6916
  16.2 0.7 %copy-start.11 = (s32[4,6]{1,0:T(4,128)S(1)}, s32[4,6]{1,0:T(4,128)}, u32[]{:S(2)}) copy-start(s32[4,6]{1,0:T(4,128)} %elem_ref.1) | copy-start | bytes 292
  16.9 0.7 %copy-start.12 = (s32[4,6]{1,0:T(4,128)S(1)}, s32[4,6]{1,0:T(4,128)}, u32[]{:S(2)}) copy-start(s32[4,6]{1,0:T(4,128)} %side_ref.1) | copy-start | bytes 292
  17.5 0.7 %copy-start.13 = (s32[4,6]{1,0:T(4,128)S(1)}, s32[4,6]{1,0:T(4,128)}, u32[]{:S(2)}) copy-start(s32[4,6]{1,0:T(4,128)} %turn_ref.1) | copy-start | bytes 292
  20.8 9.9 %collective-permute-start.3 = (f32[144,128]{1,0:T(8,128)S(1)}, f32[144,128]{1,0:T(8,128)S(1)}, u32[]{:S(2)}, u32[]{:S(2)}) collective-permute-start(f32[144,128]{1,0:T(8,128)S(1)} %get-tuple-element.40.rest_2_), channel_id=1, source_target_pairs={{1,2},{2,1},{3,4},{4,3},{5,6},{6,5},{7,8},{8,7},{9,10},{10,9},{11,... | collective-permute-start | bytes 221192 | tf_op jit(solution)/shard_map/ppermute | solution.py:291
  23.8 6.8 %collective-permute-start.2 = (f32[144,128]{1,0:T(8,128)S(1)}, f32[144,128]{1,0:T(8,128)S(1)}, u32[]{:S(2)}, u32[]{:S(2)}) collective-permute-start(f32[144,128]{1,0:T(8,128)S(1)} %get-tuple-element.40.rest_2_), channel_id=1, source_target_pairs={{0,1},{1,0},{2,3},{3,2},{4,5},{5,4},{6,7},{7,6},{8,9},{9,8},{10,11... | collective-permute-start | bytes 221192 | tf_op jit(solution)/shard_map/ppermute | solution.py:292
  31.3 9.9 %collective-permute-start.5 = (f32[144,128]{1,0:T(8,128)S(1)}, f32[144,128]{1,0:T(8,128)S(1)}, u32[]{:S(2)}, u32[]{:S(2)}) collective-permute-start(f32[144,128]{1,0:T(8,128)S(1)} %get-tuple-element.44.rest_2_), channel_id=1, source_target_pairs={{1,2},{2,1},{3,4},{4,3},{5,6},{6,5},{7,8},{8,7},{9,10},{10,9},{11,... | collective-permute-start | bytes 221192 | tf_op jit(solution)/shard_map/ppermute | solution.py:291
  34.3 6.8 %collective-permute-start.4 = (f32[144,128]{1,0:T(8,128)S(1)}, f32[144,128]{1,0:T(8,128)S(1)}, u32[]{:S(2)}, u32[]{:S(2)}) collective-permute-start(f32[144,128]{1,0:T(8,128)S(1)} %get-tuple-element.44.rest_2_), channel_id=1, source_target_pairs={{0,1},{1,0},{2,3},{3,2},{4,5},{5,4},{6,7},{7,6},{8,9},{9,8},{10,11... | collective-permute-start | bytes 221192 | tf_op jit(solution)/shard_map/ppermute | solution.py:292
  41.8 9.9 %collective-permute-start.7 = (f32[144,128]{1,0:T(8,128)S(1)}, f32[144,128]{1,0:T(8,128)S(1)}, u32[]{:S(2)}, u32[]{:S(2)}) collective-permute-start(f32[144,128]{1,0:T(8,128)S(1)} %get-tuple-element.47.rest_2_), channel_id=1, source_target_pairs={{1,2},{2,1},{3,4},{4,3},{5,6},{6,5},{7,8},{8,7},{9,10},{10,9},{11,... | collective-permute-start | bytes 221192 | tf_op jit(solution)/shard_map/ppermute | solution.py:291
  44.8 6.8 %collective-permute-start.6 = (f32[144,128]{1,0:T(8,128)S(1)}, f32[144,128]{1,0:T(8,128)S(1)}, u32[]{:S(2)}, u32[]{:S(2)}) collective-permute-start(f32[144,128]{1,0:T(8,128)S(1)} %get-tuple-element.47.rest_2_), channel_id=1, source_target_pairs={{0,1},{1,0},{2,3},{3,2},{4,5},{5,4},{6,7},{7,6},{8,9},{9,8},{10,11... | collective-permute-start | bytes 221192 | tf_op jit(solution)/shard_map/ppermute | solution.py:292
  52.4 9.9 %collective-permute-start.9 = (f32[144,128]{1,0:T(8,128)S(1)}, f32[144,128]{1,0:T(8,128)S(1)}, u32[]{:S(2)}, u32[]{:S(2)}) collective-permute-start(f32[144,128]{1,0:T(8,128)S(1)} %get-tuple-element.50.rest_2_), channel_id=1, source_target_pairs={{1,2},{2,1},{3,4},{4,3},{5,6},{6,5},{7,8},{8,7},{9,10},{10,9},{11,... | collective-permute-start | bytes 221192 | tf_op jit(solution)/shard_map/ppermute | solution.py:291
  55.5 6.8 %collective-permute-start.8 = (f32[144,128]{1,0:T(8,128)S(1)}, f32[144,128]{1,0:T(8,128)S(1)}, u32[]{:S(2)}, u32[]{:S(2)}) collective-permute-start(f32[144,128]{1,0:T(8,128)S(1)} %get-tuple-element.50.rest_2_), channel_id=1, source_target_pairs={{0,1},{1,0},{2,3},{3,2},{4,5},{5,4},{6,7},{7,6},{8,9},{9,8},{10,11... | collective-permute-start | bytes 221192 | tf_op jit(solution)/shard_map/ppermute | solution.py:292

commit v2 on v1

--- a/solution.py
+++ b/solution.py
@@ -31,6 +31,11 @@
     return matrix
 
 
+def low_trace_matrix():
+    places = [face * 64 + a * 8 + b for face in range(6) for a in range(QC) for b in range(QC)]
+    return np.pad(trace_matrix()[:, places], ((0, 0), (0, 32)))
+
+
 def lift_matrix():
     degrees = np.stack(np.meshgrid(*[np.arange(QF)] * 3, indexing="ij"), -1).reshape(512, 3)
     scale = np.stack([(2.0 * degrees[:, face // 2] + 1.0) / 16.0 for face in range(6)], -1)
@@ -53,9 +58,8 @@
     return jnp.where(low, first, half_swap(second)), jnp.where(low, half_swap(first), second)
 
 
-def prepare_body(me_ref, owner_ref, elem_ref, side_ref, turn_ref, vj_ref, fj_ref, stiff_ref,
-                 start_ref, idx_ref, sign_ref, vjc_ref, fjc_ref, khi_ref, klo_ref):
-    me = me_ref[0]
+def prepare_tables(me, owner_ref, elem_ref, side_ref, turn_ref, vj_ref, fj_ref,
+                   start_ref, idx_ref, sign_ref, low_start_ref, low_idx_ref, vjc_ref, fjc_ref):
     rows = rows8()
     lane = lanes8()
     low = rows < 4
@@ -64,8 +68,7 @@
     b = lane & 7
     signs = []
     for face in range(6):
-        swap = jnp.zeros((8, 128), jnp.int32)
-        parity = jnp.zeros((8, 128), jnp.int32)
+        sides = jnp.zeros((8, 128), jnp.int32)
         turns = jnp.zeros((8, 128), jnp.int32)
         present = jnp.zeros((8, 128), jnp.int32)
         for e in range(4):
@@ -74,12 +77,14 @@
             block = jnp.where(owner == me, 0, jnp.where(owner == (me ^ 1), 1, 2))
             block = jnp.where(owner < 0, 0, block)
             start_ref[face * 4 + e] = block * 144 + (side >> 1) * 48 + elem_ref[e, face]
+            low_start_ref[face * 4 + e] = block * 48 + elem_ref[e, face]
             here = element == e
             turns = jnp.where(here, turn_ref[e, face], turns)
-            parity = jnp.where(here, side & 1, parity)
+            sides = jnp.where(here, side, sides)
             present = jnp.where(here, jnp.where(owner >= 0, 1, 0), present)
-        swap = turns & 1
-        idx_ref[face] = parity * 64 + jnp.where(swap == 1, b * 8 + a, a * 8 + b)
+        swap = (turns & 1) == 1
+        idx_ref[face] = (sides & 1) * 64 + jnp.where(swap, b * 8 + a, a * 8 + b)
+        low_idx_ref[face] = sides * 16 + jnp.where(swap, (b & 3) * 4 + (a & 3), (a & 3) * 4 + (b & 3))
         flips = (((turns >> 1) & a) + ((turns >> 2) & b)) & 1
         signs.append((present * (1 - 2 * flips)).astype(F32))
     for f2 in range(3):
@@ -101,10 +106,6 @@
                     jnp.broadcast_to(even[:, w : w + 1], (8, 128)),
                     jnp.broadcast_to(odd[:, w : w + 1], (8, 128)),
                 )
-    stiff = stiff_ref[...]
-    high = stiff.astype(BF16)
-    khi_ref[...] = high
-    klo_ref[...] = (stiff - high.astype(F32)).astype(BF16)
 
 
 def apply_inverse(inv_ref, residual, halves):
@@ -125,7 +126,7 @@
     ref[48 + row : 64 + row, column : column + 128] = (both - high.astype(F32)).astype(BF16)
 
 
-def emit(state, halves, trace_ref, split_ref, face_ref):
+def emit(state, halves, trace_ref, split_ref, face_ref, low_ref=None):
     low = rows8() < 4
     for h in range(halves):
         matrix = {}
@@ -135,8 +136,11 @@
             for vq in range(3):
                 store_split(split_ref, vq * 16, (2 * h + part) * 128, matrix[2 * vq][part], matrix[2 * vq + 1][part])
     width = 256 * halves
-    both = jnp.dot(split_ref[:, :width], trace_ref[:width, :], preferred_element_type=F32)
+    columns = 384 if low_ref is None else 512
+    both = jnp.dot(split_ref[:, :width], trace_ref[:width, :columns], preferred_element_type=F32)
     traces = both[:48] + both[48:]
+    if low_ref is not None:
+        low_ref[...] = traces[:, 384:]
     for f2 in range(3):
         face_ref[f2 * 48 : f2 * 48 + 48, :] = traces[:, f2 * 128 : f2 * 128 + 128]
 
@@ -151,13 +155,14 @@
     return state
 
 
-def residual_of(u_ref, base_ref, split_ref, own_ref, even_ref, odd_ref, start_ref, idx_ref, sign_ref,
+def residual_of(u_ref, base_ref, split_ref, own_ref, mine_ref, even_ref, odd_ref, start_ref, idx_ref, sign_ref,
                 vjc_ref, fjc_ref, khi_ref, klo_ref, lift_ref, pool, pick0, pick1, jump_ref, halves_in, halves):
     low = rows8() < 4
     left = lanes8() < 64
-    pool[0:144, :] = own_ref[...]
-    pool[144:288, :] = even_ref[...]
-    pool[288:432, :] = odd_ref[...]
+    size = mine_ref.shape[0]
+    pool[0:size, :] = mine_ref[...]
+    pool[size : 2 * size, :] = even_ref[...]
+    pool[2 * size : 3 * size, :] = odd_ref[...]
     for face in range(6):
         target = pick1 if face % 2 else pick0
         for e in range(4):
@@ -204,27 +209,52 @@
     return jnp.zeros((8, 128), F32)
 
 
-def first_body(inv_ref, rhs_ref, trace_ref, u_ref, split_ref, face_ref):
+def first_body(me_ref, *refs):
+    sources, outs, targets, sems = refs[:11], refs[11:23], refs[23:34], refs[34]
+    owner_ref, elem_ref, side_ref, turn_ref, vj_ref, fj_ref, inv_ref, rhs_ref, trace_ref, stiff_ref, lift_ref = targets
+    u_ref, split_ref, face_ref, khi_ref, klo_ref = *outs[:3], *outs[10:]
+    copies = [pltpu.make_async_copy(sources[at], targets[at], sems.at[at]) for at in range(11)]
+    for copy in copies:
+        copy.start()
+    for copy in copies[:6]:
+        copy.wait()
+    prepare_tables(me_ref[0], owner_ref, elem_ref, side_ref, turn_ref, vj_ref, fj_ref, *outs[3:10])
+    for copy in copies[6:8]:
+        copy.wait()
     state = apply_inverse(inv_ref, {(v, h): rhs_ref[2 * v + h] for v in range(VARS) for h in range(2)}, 2)
     for v in range(VARS):
         for h in range(2):
             u_ref[2 * v + h] = state[v, h]
+    copies[8].wait()
     emit(state, 2, trace_ref, split_ref, face_ref)
+    copies[9].wait()
+    stiff = stiff_ref[...]
+    high = stiff.astype(BF16)
+    khi_ref[...] = high
+    klo_ref[...] = (stiff - high.astype(F32)).astype(BF16)
+    copies[10].wait()
 
 
 def fine_body(inv_ref, trace_ref, u_ref, *rest):
-    shared, (out_ref, split_ref, face_ref), scratch = rest[:13], rest[13:16], rest[16:]
+    fine_step(inv_ref, trace_ref, u_ref, rest[:14], *rest[14:17], None, rest[17:])
+
+
+def fine_low_body(inv_ref, trace_ref, u_ref, *rest):
+    fine_step(inv_ref, trace_ref, u_ref, rest[:14], *rest[14:18], rest[18:])
+
+
+def fine_step(inv_ref, trace_ref, u_ref, shared, out_ref, split_ref, face_ref, low_ref, scratch):
     residual = residual_of(u_ref, *shared, *scratch, 2, 2)
     state = apply_inverse(inv_ref, residual, 2)
     for v in range(VARS):
         for h in range(2):
             state[v, h] = state[v, h] + u_ref[2 * v + h]
             out_ref[2 * v + h] = state[v, h]
-    emit(state, 2, trace_ref, split_ref, face_ref)
+    emit(state, 2, trace_ref, split_ref, face_ref, low_ref)
 
 
 def last_body(inv_ref, u_ref, *rest):
-    shared, out_ref, scratch = rest[:13], rest[13], rest[14:]
+    shared, out_ref, scratch = rest[:14], rest[14], rest[15:]
     residual = residual_of(u_ref, *shared, *scratch, 2, 2)
     state = apply_inverse(inv_ref, residual, 2)
     for v in range(VARS):
@@ -233,7 +263,7 @@
 
 
 def restrict_body(inv_ref, trace_ref, u_ref, *rest):
-    shared, (low_ref, out_ref, split_ref, face_ref), scratch = rest[:13], rest[13:17], rest[17:]
+    shared, (low_ref, out_ref, split_ref, face_ref, mine_ref), scratch = rest[:14], rest[14:19], rest[19:]
     residual = residual_of(u_ref, *shared, *scratch, 2, 1)
     mask = coarse_mask()
     residual = {key: tile * mask for key, tile in residual.items()}
@@ -243,11 +273,11 @@
         low_ref[2 * v + 1] = zero_tile()
         out_ref[2 * v] = state[v, 0]
         out_ref[2 * v + 1] = zero_tile()
-    emit(state, 1, trace_ref, split_ref, face_ref)
+    emit(state, 1, trace_ref, split_ref, face_ref, mine_ref)
 
 
 def coarse_body(inv_ref, trace_ref, fine_ref, u_ref, *rest):
-    shared, (out_ref, split_ref, face_ref), scratch = rest[:13], rest[13:16], rest[16:]
+    shared, (out_ref, split_ref, face_ref), scratch = rest[:14], rest[14:17], rest[17:]
     residual = residual_of(u_ref, *shared, *scratch, 1, 1)
     mask = coarse_mask()
     residual = {key: tile * mask for key, tile in residual.items()}
@@ -263,22 +293,24 @@
 STATE = VMEM((24, 8, 128), F32)
 SPLIT = VMEM((96, 512), BF16)
 FACES = VMEM((144, 128), F32)
+LOW_FACES = VMEM((48, 128), F32)
 
 
 def in_vmem(value):
     return pltpu.with_memory_space_constraint(value, VMEM)
 
 
-def call(body, outs, args, scratch=(), smem=(), smem_outs=()):
+def call(body, outs, args, scratch=(), smem=(), smem_outs=(), far=False):
     spec = pl.BlockSpec(memory_space=VMEM)
+    source = pl.BlockSpec(memory_space=pl.ANY) if far else spec
     scalar = pl.BlockSpec(memory_space=pltpu.SMEM)
     return pl.pallas_call(
         body,
         out_shape=list(outs),
-        in_specs=[scalar if at in smem else spec for at in range(len(args))],
+        in_specs=[scalar if at in smem else source for at in range(len(args))],
         out_specs=[scalar if at in smem_outs else spec for at in range(len(outs))],
         scratch_shapes=list(scratch),
-        compiler_params=pltpu.CompilerParams(vmem_limit_bytes=32 * 1024 * 1024),
+        compiler_params=pltpu.CompilerParams(vmem_limit_bytes=6 * 1024 * 1024),
     )(*args)
 
 
@@ -295,43 +327,63 @@
 
 def local(rhs, stiffness, vol_jac, face_jac, block_inv, face_owner, face_elem, face_side, face_turn):
     me = lax.axis_index("dom").astype(jnp.int32).reshape(1)
-    rhs_state = in_vmem(rhs.reshape(4, 12, 4, 128).transpose(1, 2, 0, 3).reshape(24, 8, 128))
-    inverse = in_vmem(block_inv.reshape(4, 12, 12, 4, 128).transpose(1, 2, 3, 0, 4).reshape(288, 8, 128))
+    rhs_state = rhs.reshape(4, 12, 4, 128).transpose(1, 2, 0, 3).reshape(24, 8, 128)
+    inverse = block_inv.reshape(4, 12, 12, 4, 128).transpose(1, 2, 3, 0, 4).reshape(288, 8, 128)
     vj = vol_jac.transpose(1, 0, 2).reshape(6, 8, 12)
     fj = face_jac.transpose(1, 2, 0, 3).reshape(36, 8, 12)
-    trace = in_vmem(jnp.asarray(trace_matrix(), BF16))
-    lift = in_vmem(jnp.asarray(lift_matrix(), BF16))
-
-    u, split, faces = call(first_body, (STATE, SPLIT, FACES), (inverse, rhs_state, trace))
-    start, idx, sign, vjc, fjc, khi, klo = call(
-        prepare_body,
+    trace = jnp.asarray(np.concatenate([trace_matrix(), low_trace_matrix()], 1), BF16)
+    lift = jnp.asarray(lift_matrix(), BF16)
+    loads = (face_owner, face_elem, face_side, face_turn, vj, fj, inverse, rhs_state, trace, stiffness, lift)
+    u, split, faces, start, idx, sign, low_start, low_idx, vjc, fjc, khi, klo, *loads = call(
+        first_body,
         (
+            STATE,
+            SPLIT,
+            FACES,
             pltpu.SMEM((24,), jnp.int32),
             VMEM((6, 8, 128), jnp.int32),
             VMEM((3, 8, 128), F32),
+            pltpu.SMEM((24,), jnp.int32),
+            VMEM((6, 8, 128), jnp.int32),
             VMEM((144, 8, 128), F32),
             VMEM((216, 8, 128), F32),
             VMEM((512, 512), BF16),
             VMEM((512, 512), BF16),
+            *((pltpu.SMEM if at < 4 else VMEM)(load.shape, load.dtype) for at, load in enumerate(loads)),
         ),
-        (me, face_owner, face_elem, face_side, face_turn, vj, fj, stiffness),
-        smem=(0, 1, 2, 3, 4),
-        smem_outs=(0,),
+        (me, *(pltpu.with_memory_space_constraint(load, pltpu.HBM) for load in loads)),
+        (pltpu.SemaphoreType.DMA((len(loads),)),),
+        smem=(0,),
+        smem_outs=(3, 6, 12, 13, 14, 15),
+        far=True,
     )
-    tables = (start, idx, sign, vjc, fjc, khi, klo, lift)
+    inverse, rhs_state, trace, stiffness, lift = loads[6:]
+    tables = (sign, vjc, fjc, khi, klo, lift)
     scratch = (VMEM((432, 128), F32), FACES, FACES, VMEM((96, 384), BF16))
 
-    def stage(body, outs, head, u, base, split, faces):
-        even, odd = exchange(faces)
-        args = (*head, u, base, split, faces, even, odd, *tables)
-        return call(body, outs, args, scratch, smem=(len(head) + 6,))
-
-    fine_two, split, faces = stage(fine_body, (STATE, SPLIT, FACES), (inverse, trace), u, rhs_state, split, faces)
-    low_rhs, coarse, split, faces = stage(
-        restrict_body, (STATE, STATE, SPLIT, FACES), (inverse, trace), fine_two, rhs_state, split, faces
+    def stage(body, outs, head, u, base, split, faces, sent=None):
+        low = sent is not None
+        sent = sent if low else faces
+        even, odd = exchange(sent)
+        places = (low_start, low_idx) if low else (start, idx)
+        args = (*head, u, base, split, faces, sent, even, odd, *places, *tables)
+        return call(body, outs, args, scratch, smem=(len(head) + 7,))
+
+    fine_two, split, faces, sent = stage(
+        fine_low_body, (STATE, SPLIT, FACES, LOW_FACES), (inverse, trace), u, rhs_state, split, faces
+    )
+    low_rhs, coarse, split, faces, sent = stage(
+        restrict_body,
+        (STATE, STATE, SPLIT, FACES, LOW_FACES),
+        (inverse, trace),
+        fine_two,
+        rhs_state,
+        split,
+        faces,
+        sent,
     )
     u, split, faces = stage(
-        coarse_body, (STATE, SPLIT, FACES), (inverse, trace, fine_two), coarse, low_rhs, split, faces
+        coarse_body, (STATE, SPLIT, FACES), (inverse, trace, fine_two), coarse, low_rhs, split, faces, sent
     )
     u, split, faces = stage(fine_body, (STATE, SPLIT, FACES), (inverse, trace), u, rhs_state, split, faces)
     (u,) = stage(last_body, (jax.ShapeDtypeStruct((24, 8, 128), F32),), (inverse,), u, rhs_state, split, faces)

time: 64 us -> 57.7 us (0.902)
  starting transfers between devices: 22.4 us -> 41.5 us
  waiting for transfers between devices: 26.9 us -> 8.58 us
  local copies, waits for them, and re-layouts: 8.1 us -> 0 us
  Pallas kernels: 5.85 us -> 7.21 us
    ppermute x5, starting transfers between devices: 22 us -> 41 us  [exchange(): from_odd = lax.ppermute(faces, 'dom', odd)]
    ppermute x5, waiting for transfers between devices: 26.9 us -> 8.56 us  [exchange(): from_odd = lax.ppermute(faces, 'dom', odd)]
    unnamed x28 -> x0, local copies, waits for them, and re-layouts: 8.1 us -> none
    pallas_call x7 -> x6, Pallas kernels: 5.85 us -> 7.21 us  [call(): pl.pallas_call(body, out_shape=list(outs), in_specs=[scalar if at in smem...]
  transfers between devices with their start and end apart: 10 -> 10, of which waited for: 4 -> 5; matrix products, arithmetic and copies ran while one was open for 0% -> 0% of each run, Pallas kernels for 3% -> 0%
where the time goes in v2:
time: 57.7 us; the launch traced here: 57.4 us
  starting transfers between devices  41.5 us (72%)
  waiting for transfers between devices  8.58 us (15%)
  Pallas kernels  7.21 us (12%)
    ppermute x5, starting transfers between devices, exchange(): from_odd = lax.ppermute(faces, 'dom', odd)  41 us
    ppermute x5, waiting for transfers between devices, exchange(): from_odd = lax.ppermute(faces, 'dom', odd)  8.56 us
    pallas_call x6, Pallas kernels, call(): pl.pallas_call(body, out_shape=list(outs), in_specs=[scalar if at in smem...  7.21 us
  transfers between devices with their start and end apart: 10, of which 5 were waited for; matrix products, arithmetic and copies ran while one was open for 0% of the time, Pallas kernels for 0%

profile of v2, /device:TPU:24, one launch (start us, length us, event | category | flops | bytes accessed | tf_op | source)
XLA Modules:
  0.0 57.4 jit_solution(8782834899297396291)
XLA Ops:
  0.0 3.4 %shard_map.109 = (f32[24,8,128]{2,1,0:T(8,128)S(1)}, bf16[96,512]{1,0:T(8,128)(2,1)S(1)}, f32[144,128]{1,0:T(8,128)S(1)}, s32[24]{0:T(128)S(4)}, s32[6,8,128]{2,...) custom-call(s32[1]{0:T(128)} %bitcast.me_ref, ...), custom_call_target="tpu_custom_call" | custom-call | tf_op jit(solution)/shard_map/pallas_call | solution.py:307
  3.4 9.6 %collective-permute-start.1 = (f32[144,128]{1,0:T(8,128)S(1)}, f32[144,128]{1,0:T(8,128)S(1)}, u32[]{:S(2)}, u32[]{:S(2)}) collective-permute-start(f32[144,128]{1,0:T(8,128)S(1)} %get-tuple-element.41.rest_2_.rest_3_), channel_id=1, source_target_pairs={{1,2},{2,1},{3,4},{4,3},{5,6},{6,5},{7,8},{8,7},{9,10},{10,9},{11,... | collective-permute-start | bytes 221192 | tf_op jit(solution)/shard_map/ppermute | solution.py:323
  13.0 0.1 collective-permute-start
  13.1 1.9 %collective-permute-done.1.rest_5_ = f32[144,128]{1,0:T(8,128)S(1)} collective-permute-done((f32[144,128]{1,0:T(8,128)S(1)}, f32[144,128]{1,0:T(8,128)S(1)}, u32[]{:S(2)}, u32[]{:S(2)}) %collective-permute-start.1) | collective-permute-done | bytes 73760 | tf_op jit(solution)/shard_map/ppermute | solution.py:323
  15.1 0.0 collective-permute-done.rest_4_
  15.1 0.7 %shard_map.110 = (f32[24,8,128]{2,1,0:T(8,128)S(1)}, bf16[96,512]{1,0:T(8,128)(2,1)S(1)}, f32[144,128]{1,0:T(8,128)S(1)}, f32[48,128]{1,0:T(8,128)S(1)}) custom-call(f32[288,8,128]{2,1,0:T(8,128)S(1)} %get-tuple-element.36.inv_ref, bf16[512,512]{1,0:T(8,128)(2,1)S(1)} %get-tuple-element.37.trace_ref, f32[24,8,128]{2,1,0:T(8,128)S(1)} %get-tuple-element.38.u_ref, ...), custom_call_target="tpu_custom_call" | custom-call | tf_op jit(solution)/shard_map/pallas_call | solution.py:307
  15.8 7.9 %collective-permute-start.3 = (f32[48,128]{1,0:T(8,128)S(1)}, f32[48,128]{1,0:T(8,128)S(1)}, u32[]{:S(2)}, u32[]{:S(2)}) collective-permute-start(f32[48,128]{1,0:T(8,128)S(1)} %get-tuple-element.53.rest_3_), channel_id=1, source_target_pairs={{1,2},{2,1},{3,4},{4,3},{5,6},{6,5},{7,8},{8,7},{9,10},{10,9},{11,... | collective-permute-start | bytes 73736 | tf_op jit(solution)/shard_map/ppermute | solution.py:323
  23.6 0.1 collective-permute-start.2
  23.7 1.4 %collective-permute-done.3.rest_5_ = f32[48,128]{1,0:T(8,128)S(1)} collective-permute-done((f32[48,128]{1,0:T(8,128)S(1)}, f32[48,128]{1,0:T(8,128)S(1)}, u32[]{:S(2)}, u32[]{:S(2)}) %collective-permute-start.3) | collective-permute-done | bytes 24608 | tf_op jit(solution)/shard_map/ppermute | solution.py:323
  25.1 0.0 collective-permute-done.2.rest_4_
  25.1 0.6 shard_map.111
  25.7 7.9 %collective-permute-start.5 = (f32[48,128]{1,0:T(8,128)S(1)}, f32[48,128]{1,0:T(8,128)S(1)}, u32[]{:S(2)}, u32[]{:S(2)}) collective-permute-start(f32[48,128]{1,0:T(8,128)S(1)} %get-tuple-element.60.rest_3_), channel_id=1, source_target_pairs={{1,2},{2,1},{3,4},{4,3},{5,6},{6,5},{7,8},{8,7},{9,10},{10,9},{11,... | collective-permute-start | bytes 73736 | tf_op jit(solution)/shard_map/ppermute | solution.py:323
  33.6 0.1 collective-permute-start.4
  33.7 1.4 %collective-permute-done.5.rest_5_ = f32[48,128]{1,0:T(8,128)S(1)} collective-permute-done((f32[48,128]{1,0:T(8,128)S(1)}, f32[48,128]{1,0:T(8,128)S(1)}, u32[]{:S(2)}, u32[]{:S(2)}) %collective-permute-start.5) | collective-permute-done | bytes 24608 | tf_op jit(solution)/shard_map/ppermute | solution.py:323
  35.1 0.0 collective-permute-done.4.rest_4_
  35.1 0.6 %shard_map.112 = (f32[24,8,128]{2,1,0:T(8,128)S(1)}, bf16[96,512]{1,0:T(8,128)(2,1)S(1)}, f32[144,128]{1,0:T(8,128)S(1)}) custom-call(f32[288,8,128]{2,1,0:T(8,128)S(1)} %get-tuple-element.36.inv_ref, bf16[512,512]{1,0:T(8,128)(2,1)S(1)} %get-tuple-element.37.trace_ref, f32[24,8,128]{2,1,0:T(8,128)S(1)} %get-tuple-element.50.u_ref.fine_ref, ...), custom_call_target="tpu_custom_call" | custom-call | tf_op jit(solution)/shard_map/pallas_call | solution.py:307
  35.7 7.9 %collective-permute-start.7 = (f32[144,128]{1,0:T(8,128)S(1)}, f32[144,128]{1,0:T(8,128)S(1)}, u32[]{:S(2)}, u32[]{:S(2)}) collective-permute-start(f32[144,128]{1,0:T(8,128)S(1)} %get-tuple-element.63.rest_2_.rest_3_), channel_id=1, source_target_pairs={{1,2},{2,1},{3,4},{4,3},{5,6},{6,5},{7,8},{8,7},{9,10},{10,9},{11,... | collective-permute-start | bytes 221192 | tf_op jit(solution)/shard_map/ppermute | solution.py:323
  43.5 0.1 collective-permute-start.6
  43.6 1.9 %collective-permute-done.7.rest_5_ = f32[144,128]{1,0:T(8,128)S(1)} collective-permute-done((f32[144,128]{1,0:T(8,128)S(1)}, f32[144,128]{1,0:T(8,128)S(1)}, u32[]{:S(2)}, u32[]{:S(2)}) %collective-permute-start.7) | collective-permute-done | bytes 73760 | tf_op jit(solution)/shard_map/ppermute | solution.py:323
  45.6 0.0 collective-permute-done.6.rest_4_
  45.6 0.7 %shard_map.113 = (f32[24,8,128]{2,1,0:T(8,128)S(1)}, bf16[96,512]{1,0:T(8,128)(2,1)S(1)}, f32[144,128]{1,0:T(8,128)S(1)}) custom-call(f32[288,8,128]{2,1,0:T(8,128)S(1)} %get-tuple-element.36.inv_ref, bf16[512,512]{1,0:T(8,128)(2,1)S(1)} %get-tuple-element.37.trace_ref, f32[24,8,128]{2,1,0:T(8,128)S(1)} %get-tuple-element.61.u_ref, ...), custom_call_target="tpu_custom_call" | custom-call | tf_op jit(solution)/shard_map/pallas_call | solution.py:307
  46.3 7.9 %collective-permute-start.9 = (f32[144,128]{1,0:T(8,128)S(1)}, f32[144,128]{1,0:T(8,128)S(1)}, u32[]{:S(2)}, u32[]{:S(2)}) collective-permute-start(f32[144,128]{1,0:T(8,128)S(1)} %get-tuple-element.66.rest_2_.rest_3_), channel_id=1, source_target_pairs={{1,2},{2,1},{3,4},{4,3},{5,6},{6,5},{7,8},{8,7},{9,10},{10,9},{11,... | collective-permute-start | bytes 221192 | tf_op jit(solution)/shard_map/ppermute | solution.py:323
  54.2 0.1 collective-permute-start.8
  54.3 1.9 %collective-permute-done.9.rest_5_ = f32[144,128]{1,0:T(8,128)S(1)} collective-permute-done((f32[144,128]{1,0:T(8,128)S(1)}, f32[144,128]{1,0:T(8,128)S(1)}, u32[]{:S(2)}, u32[]{:S(2)}) %collective-permute-start.9) | collective-permute-done | bytes 73760 | tf_op jit(solution)/shard_map/ppermute | solution.py:323
  56.2 0.0 collective-permute-done.8.rest_4_
  56.2 1.2 %shard_map.114 = f32[24,8,128]{2,1,0:T(8,128)} custom-call(f32[288,8,128]{2,1,0:T(8,128)S(1)} %get-tuple-element.36.inv_ref, f32[24,8,128]{2,1,0:T(8,128)S(1)} %get-tuple-element.64.u_ref, f32[24,8,128]{2,1,0:T(8,128)S(1)} %get-tuple-element.39.rest_0_, bf16[96,512]{1,0:T(8,128)(2,1)S(1)} %get-tuple-element.65.rest_1_, ...), custom_call_target="tpu_custom_call" | custom-call | tf_op jit(solution)/shard_map/pallas_call | solution.py:307
Async XLA Ops:
  3.4 11.6 %collective-permute-start.1 = (f32[144,128]{1,0:T(8,128)S(1)}, f32[144,128]{1,0:T(8,128)S(1)}, u32[]{:S(2)}, u32[]{:S(2)}) collective-permute-start(f32[144,128]{1,0:T(8,128)S(1)} %get-tuple-element.41.rest_2_.rest_3_), channel_id=1, source_target_pairs={{1,2},{2,1},{3,4},{4,3},{5,6},{6,5},{7,8},{8,7},{9,10},{10,9},{11,... | collective-permute-start | bytes 221192 | tf_op jit(solution)/shard_map/ppermute | solution.py:323
  13.0 2.0 %collective-permute-start = (f32[144,128]{1,0:T(8,128)S(1)}, f32[144,128]{1,0:T(8,128)S(1)}, u32[]{:S(2)}, u32[]{:S(2)}) collective-permute-start(f32[144,128]{1,0:T(8,128)S(1)} %get-tuple-element.41.rest_2_.rest_3_), channel_id=1, source_target_pairs={{0,1},{1,0},{2,3},{3,2},{4,5},{5,4},{6,7},{7,6},{8,9},{9,8},{10,11... | collective-permute-start | bytes 221192 | tf_op jit(solution)/shard_map/ppermute | solution.py:324
  15.8 9.4 %collective-permute-start.3 = (f32[48,128]{1,0:T(8,128)S(1)}, f32[48,128]{1,0:T(8,128)S(1)}, u32[]{:S(2)}, u32[]{:S(2)}) collective-permute-start(f32[48,128]{1,0:T(8,128)S(1)} %get-tuple-element.53.rest_3_), channel_id=1, source_target_pairs={{1,2},{2,1},{3,4},{4,3},{5,6},{6,5},{7,8},{8,7},{9,10},{10,9},{11,... | collective-permute-start | bytes 73736 | tf_op jit(solution)/shard_map/ppermute | solution.py:323
  23.6 1.5 %collective-permute-start.2 = (f32[48,128]{1,0:T(8,128)S(1)}, f32[48,128]{1,0:T(8,128)S(1)}, u32[]{:S(2)}, u32[]{:S(2)}) collective-permute-start(f32[48,128]{1,0:T(8,128)S(1)} %get-tuple-element.53.rest_3_), channel_id=1, source_target_pairs={{0,1},{1,0},{2,3},{3,2},{4,5},{5,4},{6,7},{7,6},{8,9},{9,8},{10,11... | collective-permute-start | bytes 73736 | tf_op jit(solution)/shard_map/ppermute | solution.py:324
  25.7 9.4 %collective-permute-start.5 = (f32[48,128]{1,0:T(8,128)S(1)}, f32[48,128]{1,0:T(8,128)S(1)}, u32[]{:S(2)}, u32[]{:S(2)}) collective-permute-start(f32[48,128]{1,0:T(8,128)S(1)} %get-tuple-element.60.rest_3_), channel_id=1, source_target_pairs={{1,2},{2,1},{3,4},{4,3},{5,6},{6,5},{7,8},{8,7},{9,10},{10,9},{11,... | collective-permute-start | bytes 73736 | tf_op jit(solution)/shard_map/ppermute | solution.py:323
  33.6 1.5 %collective-permute-start.4 = (f32[48,128]{1,0:T(8,128)S(1)}, f32[48,128]{1,0:T(8,128)S(1)}, u32[]{:S(2)}, u32[]{:S(2)}) collective-permute-start(f32[48,128]{1,0:T(8,128)S(1)} %get-tuple-element.60.rest_3_), channel_id=1, source_target_pairs={{0,1},{1,0},{2,3},{3,2},{4,5},{5,4},{6,7},{7,6},{8,9},{9,8},{10,11... | collective-permute-start | bytes 73736 | tf_op jit(solution)/shard_map/ppermute | solution.py:324
  35.7 9.9 %collective-permute-start.7 = (f32[144,128]{1,0:T(8,128)S(1)}, f32[144,128]{1,0:T(8,128)S(1)}, u32[]{:S(2)}, u32[]{:S(2)}) collective-permute-start(f32[144,128]{1,0:T(8,128)S(1)} %get-tuple-element.63.rest_2_.rest_3_), channel_id=1, source_target_pairs={{1,2},{2,1},{3,4},{4,3},{5,6},{6,5},{7,8},{8,7},{9,10},{10,9},{11,... | collective-permute-start | bytes 221192 | tf_op jit(solution)/shard_map/ppermute | solution.py:323
  43.5 2.0 %collective-permute-start.6 = (f32[144,128]{1,0:T(8,128)S(1)}, f32[144,128]{1,0:T(8,128)S(1)}, u32[]{:S(2)}, u32[]{:S(2)}) collective-permute-start(f32[144,128]{1,0:T(8,128)S(1)} %get-tuple-element.63.rest_2_.rest_3_), channel_id=1, source_target_pairs={{0,1},{1,0},{2,3},{3,2},{4,5},{5,4},{6,7},{7,6},{8,9},{9,8},{10,11... | collective-permute-start | bytes 221192 | tf_op jit(solution)/shard_map/ppermute | solution.py:324
  46.3 9.9 %collective-permute-start.9 = (f32[144,128]{1,0:T(8,128)S(1)}, f32[144,128]{1,0:T(8,128)S(1)}, u32[]{:S(2)}, u32[]{:S(2)}) collective-permute-start(f32[144,128]{1,0:T(8,128)S(1)} %get-tuple-element.66.rest_2_.rest_3_), channel_id=1, source_target_pairs={{1,2},{2,1},{3,4},{4,3},{5,6},{6,5},{7,8},{8,7},{9,10},{10,9},{11,... | collective-permute-start | bytes 221192 | tf_op jit(solution)/shard_map/ppermute | solution.py:323
  54.2 2.0 %collective-permute-start.8 = (f32[144,128]{1,0:T(8,128)S(1)}, f32[144,128]{1,0:T(8,128)S(1)}, u32[]{:S(2)}, u32[]{:S(2)}) collective-permute-start(f32[144,128]{1,0:T(8,128)S(1)} %get-tuple-element.66.rest_2_.rest_3_), channel_id=1, source_target_pairs={{0,1},{1,0},{2,3},{3,2},{4,5},{5,4},{6,7},{7,6},{8,9},{9,8},{10,11... | collective-permute-start | bytes 221192 | tf_op jit(solution)/shard_map/ppermute | solution.py:324

commit v3 on v2

--- a/solution.py
+++ b/solution.py
@@ -209,30 +209,40 @@
     return jnp.zeros((8, 128), F32)
 
 
-def first_body(me_ref, *refs):
-    sources, outs, targets, sems = refs[:11], refs[11:23], refs[23:34], refs[34]
-    owner_ref, elem_ref, side_ref, turn_ref, vj_ref, fj_ref, inv_ref, rhs_ref, trace_ref, stiff_ref, lift_ref = targets
-    u_ref, split_ref, face_ref, khi_ref, klo_ref = *outs[:3], *outs[10:]
-    copies = [pltpu.make_async_copy(sources[at], targets[at], sems.at[at]) for at in range(11)]
+def start_all(sources, targets, sems):
+    copies = [pltpu.make_async_copy(source, target, sems.at[at]) for at, (source, target) in enumerate(zip(sources, targets))]
     for copy in copies:
         copy.start()
-    for copy in copies[:6]:
-        copy.wait()
-    prepare_tables(me_ref[0], owner_ref, elem_ref, side_ref, turn_ref, vj_ref, fj_ref, *outs[3:10])
-    for copy in copies[6:8]:
-        copy.wait()
+    return copies
+
+
+def first_body(*refs):
+    sources, (u_ref, split_ref, face_ref), targets, sems = refs[:3], refs[3:6], refs[6:9], refs[9]
+    inv_ref, rhs_ref, trace_ref = targets
+    copies = start_all(sources, targets, sems)
+    copies[0].wait()
+    copies[1].wait()
     state = apply_inverse(inv_ref, {(v, h): rhs_ref[2 * v + h] for v in range(VARS) for h in range(2)}, 2)
     for v in range(VARS):
         for h in range(2):
             u_ref[2 * v + h] = state[v, h]
-    copies[8].wait()
+    copies[2].wait()
     emit(state, 2, trace_ref, split_ref, face_ref)
-    copies[9].wait()
+
+
+def prepare_body(me_ref, *refs):
+    sources, tables, (khi_ref, klo_ref, lift_ref) = refs[:8], refs[8:15], refs[15:18]
+    owner_ref, elem_ref, side_ref, turn_ref, vj_ref, fj_ref, stiff_ref, sems = refs[18:]
+    copies = start_all(sources, (owner_ref, elem_ref, side_ref, turn_ref, vj_ref, fj_ref, stiff_ref, lift_ref), sems)
+    for copy in copies[:6]:
+        copy.wait()
+    prepare_tables(me_ref[0], owner_ref, elem_ref, side_ref, turn_ref, vj_ref, fj_ref, *tables)
+    copies[6].wait()
     stiff = stiff_ref[...]
     high = stiff.astype(BF16)
     khi_ref[...] = high
     klo_ref[...] = (stiff - high.astype(F32)).astype(BF16)
-    copies[10].wait()
+    copies[7].wait()
 
 
 def fine_body(inv_ref, trace_ref, u_ref, *rest):
@@ -254,12 +264,21 @@
 
 
 def last_body(inv_ref, u_ref, *rest):
-    shared, out_ref, scratch = rest[:14], rest[14], rest[15:]
+    shared, out_hbm, scratch, out_ref, sems = rest[:14], rest[14], rest[15:19], rest[19], rest[20]
     residual = residual_of(u_ref, *shared, *scratch, 2, 2)
-    state = apply_inverse(inv_ref, residual, 2)
-    for v in range(VARS):
-        for h in range(2):
-            out_ref[2 * v + h] = state[v, h] + u_ref[2 * v + h]
+    copies = []
+    for part in range(3):
+        for v in range(4 * part, 4 * part + 4):
+            for h in range(2):
+                acc = inv_ref[(v * VARS) * 2 + h] * residual[0, h]
+                for w in range(1, VARS):
+                    acc = acc + inv_ref[(v * VARS + w) * 2 + h] * residual[w, h]
+                out_ref[2 * v + h] = OMEGA * acc + u_ref[2 * v + h]
+        piece = pl.ds(8 * part, 8)
+        copies.append(pltpu.make_async_copy(out_ref.at[piece], out_hbm.at[piece], sems.at[part]))
+        copies[-1].start()
+    for copy in copies:
+        copy.wait()
 
 
 def restrict_body(inv_ref, trace_ref, u_ref, *rest):
@@ -300,15 +319,20 @@
     return pltpu.with_memory_space_constraint(value, VMEM)
 
 
-def call(body, outs, args, scratch=(), smem=(), smem_outs=(), far=False):
+def in_hbm(value):
+    return pltpu.with_memory_space_constraint(value, pltpu.HBM)
+
+
+def call(body, outs, args, scratch=(), smem=(), smem_outs=(), far=False, far_out=False):
     spec = pl.BlockSpec(memory_space=VMEM)
     source = pl.BlockSpec(memory_space=pl.ANY) if far else spec
+    target = pl.BlockSpec(memory_space=pl.ANY) if far_out else spec
     scalar = pl.BlockSpec(memory_space=pltpu.SMEM)
     return pl.pallas_call(
         body,
         out_shape=list(outs),
         in_specs=[scalar if at in smem else source for at in range(len(args))],
-        out_specs=[scalar if at in smem_outs else spec for at in range(len(outs))],
+        out_specs=[scalar if at in smem_outs else target for at in range(len(outs))],
         scratch_shapes=list(scratch),
         compiler_params=pltpu.CompilerParams(vmem_limit_bytes=6 * 1024 * 1024),
     )(*args)
@@ -333,13 +357,18 @@
     fj = face_jac.transpose(1, 2, 0, 3).reshape(36, 8, 12)
     trace = jnp.asarray(np.concatenate([trace_matrix(), low_trace_matrix()], 1), BF16)
     lift = jnp.asarray(lift_matrix(), BF16)
-    loads = (face_owner, face_elem, face_side, face_turn, vj, fj, inverse, rhs_state, trace, stiffness, lift)
-    u, split, faces, start, idx, sign, low_start, low_idx, vjc, fjc, khi, klo, *loads = call(
+    loads = (inverse, rhs_state, trace)
+    u, split, faces, inverse, rhs_state, trace = call(
         first_body,
+        (STATE, SPLIT, FACES, *(VMEM(load.shape, load.dtype) for load in loads)),
+        tuple(in_hbm(load) for load in loads),
+        (pltpu.SemaphoreType.DMA((3,)),),
+        far=True,
+    )
+    loads = (face_owner, face_elem, face_side, face_turn, vj, fj, stiffness, lift)
+    start, idx, sign, low_start, low_idx, vjc, fjc, khi, klo, lift = call(
+        prepare_body,
         (
-            STATE,
-            SPLIT,
-            FACES,
             pltpu.SMEM((24,), jnp.int32),
             VMEM((6, 8, 128), jnp.int32),
             VMEM((3, 8, 128), F32),
@@ -349,25 +378,30 @@
             VMEM((216, 8, 128), F32),
             VMEM((512, 512), BF16),
             VMEM((512, 512), BF16),
-            *((pltpu.SMEM if at < 4 else VMEM)(load.shape, load.dtype) for at, load in enumerate(loads)),
+            VMEM((384, 512), BF16),
         ),
-        (me, *(pltpu.with_memory_space_constraint(load, pltpu.HBM) for load in loads)),
-        (pltpu.SemaphoreType.DMA((len(loads),)),),
+        (me, *(in_hbm(load) for load in loads)),
+        (
+            *(pltpu.SMEM((4, 6), jnp.int32) for _ in range(4)),
+            VMEM((6, 8, 12), F32),
+            VMEM((36, 8, 12), F32),
+            VMEM((512, 512), F32),
+            pltpu.SemaphoreType.DMA((8,)),
+        ),
         smem=(0,),
-        smem_outs=(3, 6, 12, 13, 14, 15),
+        smem_outs=(0, 3),
         far=True,
     )
-    inverse, rhs_state, trace, stiffness, lift = loads[6:]
     tables = (sign, vjc, fjc, khi, klo, lift)
     scratch = (VMEM((432, 128), F32), FACES, FACES, VMEM((96, 384), BF16))
 
-    def stage(body, outs, head, u, base, split, faces, sent=None):
+    def stage(body, outs, head, u, base, split, faces, sent=None, more=(), far_out=False):
         low = sent is not None
         sent = sent if low else faces
         even, odd = exchange(sent)
         places = (low_start, low_idx) if low else (start, idx)
         args = (*head, u, base, split, faces, sent, even, odd, *places, *tables)
-        return call(body, outs, args, scratch, smem=(len(head) + 7,))
+        return call(body, outs, args, (*scratch, *more), smem=(len(head) + 7,), far_out=far_out)
 
     fine_two, split, faces, sent = stage(
         fine_low_body, (STATE, SPLIT, FACES, LOW_FACES), (inverse, trace), u, rhs_state, split, faces
@@ -386,7 +420,17 @@
         coarse_body, (STATE, SPLIT, FACES), (inverse, trace, fine_two), coarse, low_rhs, split, faces, sent
     )
     u, split, faces = stage(fine_body, (STATE, SPLIT, FACES), (inverse, trace), u, rhs_state, split, faces)
-    (u,) = stage(last_body, (jax.ShapeDtypeStruct((24, 8, 128), F32),), (inverse,), u, rhs_state, split, faces)
+    (u,) = stage(
+        last_body,
+        (jax.ShapeDtypeStruct((24, 8, 128), F32),),
+        (inverse,),
+        u,
+        rhs_state,
+        split,
+        faces,
+        more=(STATE, pltpu.SemaphoreType.DMA((3,))),
+        far_out=True,
+    )
     return u.reshape(12, 4, 4, 128).transpose(2, 0, 1, 3).reshape(4, 12, 512)
 
 

time: 57.7 us -> 56 us (0.971)
  waiting for transfers between devices: 8.58 us -> 7.36 us
  starting transfers between devices: 41.5 us -> 40.8 us
    ppermute x5, waiting for transfers between devices: 8.56 us -> 7.35 us  [exchange(): from_odd = lax.ppermute(faces, 'dom', odd)]
    ppermute x5, starting transfers between devices: 41 us -> 40.3 us  [exchange(): from_odd = lax.ppermute(faces, 'dom', odd)]
    pallas_call x6 -> x7, Pallas kernels: 7.21 us -> 7.52 us  [call(): pl.pallas_call(body, out_shape=list(outs), in_specs=[scalar if at in smem...]
  transfers between devices with their start and end apart: 10 -> 10, of which waited for: 5 -> 4; matrix products, arithmetic and copies ran while one was open for 0% -> 0% of each run, Pallas kernels for 0% -> 4%
where the time goes in v3:
time: 56 us; the launch traced here: 55.8 us
  starting transfers between devices  40.8 us (73%)
  Pallas kernels  7.52 us (13%)
  waiting for transfers between devices  7.36 us (13%)
    ppermute x5, starting transfers between devices, exchange(): from_odd = lax.ppermute(faces, 'dom', odd)  40.3 us
    pallas_call x7, Pallas kernels, call(): pl.pallas_call(body, out_shape=list(outs), in_specs=[scalar if at in smem...  7.52 us
    ppermute x5, waiting for transfers between devices, exchange(): from_odd = lax.ppermute(faces, 'dom', odd)  7.35 us
  transfers between devices with their start and end apart: 10, of which 4 were waited for; matrix products, arithmetic and copies ran while one was open for 0% of the time, Pallas kernels for 4%

profile of v3, /device:TPU:24, one launch (start us, length us, event | category | flops | bytes accessed | tf_op | source)
XLA Modules:
  0.0 55.8 jit_solution(8120858529848805241)
XLA Ops:
  0.0 1.7 %shard_map.109 = (f32[24,8,128]{2,1,0:T(8,128)S(1)}, bf16[96,512]{1,0:T(8,128)(2,1)S(1)}, f32[144,128]{1,0:T(8,128)S(1)}, f32[288,8,128]{2,1,0:T(8,128)S(1)}, f3...) custom-call(f32[288,8,128]{2,1,0:T(8,128)} %bitcast.22, f32[24,8,128]{2,1,0:T(8,128)} %bitcast.24, ...), custom_call_target="tpu_custom_call" | custom-call | tf_op jit(solution)/shard_map/pallas_call | solution.py:331
  1.7 9.6 %collective-permute-start.1 = (f32[144,128]{1,0:T(8,128)S(1)}, f32[144,128]{1,0:T(8,128)S(1)}, u32[]{:S(2)}, u32[]{:S(2)}) collective-permute-start(f32[144,128]{1,0:T(8,128)S(1)} %get-tuple-element.41.rest_2_.rest_3_), channel_id=1, source_target_pairs={{1,2},{2,1},{3,4},{4,3},{5,6},{6,5},{7,8},{8,7},{9,10},{10,9},{11,... | collective-permute-start | bytes 221192 | tf_op jit(solution)/shard_map/ppermute | solution.py:347
  11.3 0.1 collective-permute-start
  11.4 2.1 %shard_map.110 = (s32[24]{0:T(128)S(4)}, s32[6,8,128]{2,1,0:T(8,128)S(1)}, f32[3,8,128]{2,1,0:T(8,128)S(1)}, s32[24]{0:T(128)S(4)}, s32[6,8,128]{2,1,0:T(8,128)S...) custom-call(s32[1]{0:T(128)} %bitcast.6.me_ref, ...), custom_call_target="tpu_custom_call" | custom-call | tf_op jit(solution)/shard_map/pallas_call | solution.py:331
  13.4 0.0 collective-permute-done.1.rest_5_
  13.5 0.0 collective-permute-done.rest_4_
  13.5 0.7 %shard_map.111 = (f32[24,8,128]{2,1,0:T(8,128)S(1)}, bf16[96,512]{1,0:T(8,128)(2,1)S(1)}, f32[144,128]{1,0:T(8,128)S(1)}, f32[48,128]{1,0:T(8,128)S(1)}) custom-call(f32[288,8,128]{2,1,0:T(8,128)S(1)} %get-tuple-element.36.inv_ref, bf16[512,512]{1,0:T(8,128)(2,1)S(1)} %get-tuple-element.37.trace_ref, f32[24,8,128]{2,1,0:T(8,128)S(1)} %get-tuple-element.38.u_ref, ...), custom_call_target="tpu_custom_call" | custom-call | tf_op jit(solution)/shard_map/pallas_call | solution.py:331
  14.2 7.7 %collective-permute-start.3 = (f32[48,128]{1,0:T(8,128)S(1)}, f32[48,128]{1,0:T(8,128)S(1)}, u32[]{:S(2)}, u32[]{:S(2)}) collective-permute-start(f32[48,128]{1,0:T(8,128)S(1)} %get-tuple-element.53.rest_3_), channel_id=1, source_target_pairs={{1,2},{2,1},{3,4},{4,3},{5,6},{6,5},{7,8},{8,7},{9,10},{10,9},{11,... | collective-permute-start | bytes 73736 | tf_op jit(solution)/shard_map/ppermute | solution.py:347
  21.9 0.1 collective-permute-start.2
  22.0 1.6 %collective-permute-done.3.rest_5_ = f32[48,128]{1,0:T(8,128)S(1)} collective-permute-done((f32[48,128]{1,0:T(8,128)S(1)}, f32[48,128]{1,0:T(8,128)S(1)}, u32[]{:S(2)}, u32[]{:S(2)}) %collective-permute-start.3) | collective-permute-done | bytes 24608 | tf_op jit(solution)/shard_map/ppermute | solution.py:347
  23.6 0.0 collective-permute-done.2.rest_4_
  23.6 0.6 shard_map.112
  24.1 7.7 %collective-permute-start.5 = (f32[48,128]{1,0:T(8,128)S(1)}, f32[48,128]{1,0:T(8,128)S(1)}, u32[]{:S(2)}, u32[]{:S(2)}) collective-permute-start(f32[48,128]{1,0:T(8,128)S(1)} %get-tuple-element.60.rest_3_), channel_id=1, source_target_pairs={{1,2},{2,1},{3,4},{4,3},{5,6},{6,5},{7,8},{8,7},{9,10},{10,9},{11,... | collective-permute-start | bytes 73736 | tf_op jit(solution)/shard_map/ppermute | solution.py:347
  31.8 0.1 collective-permute-start.4
  31.9 1.6 %collective-permute-done.5.rest_5_ = f32[48,128]{1,0:T(8,128)S(1)} collective-permute-done((f32[48,128]{1,0:T(8,128)S(1)}, f32[48,128]{1,0:T(8,128)S(1)}, u32[]{:S(2)}, u32[]{:S(2)}) %collective-permute-start.5) | collective-permute-done | bytes 24608 | tf_op jit(solution)/shard_map/ppermute | solution.py:347
  33.5 0.0 collective-permute-done.4.rest_4_
  33.5 0.6 %shard_map.113 = (f32[24,8,128]{2,1,0:T(8,128)S(1)}, bf16[96,512]{1,0:T(8,128)(2,1)S(1)}, f32[144,128]{1,0:T(8,128)S(1)}) custom-call(f32[288,8,128]{2,1,0:T(8,128)S(1)} %get-tuple-element.36.inv_ref, bf16[512,512]{1,0:T(8,128)(2,1)S(1)} %get-tuple-element.37.trace_ref, f32[24,8,128]{2,1,0:T(8,128)S(1)} %get-tuple-element.50.u_ref.fine_ref, ...), custom_call_target="tpu_custom_call" | custom-call | tf_op jit(solution)/shard_map/pallas_call | solution.py:331
  34.1 7.7 %collective-permute-start.7 = (f32[144,128]{1,0:T(8,128)S(1)}, f32[144,128]{1,0:T(8,128)S(1)}, u32[]{:S(2)}, u32[]{:S(2)}) collective-permute-start(f32[144,128]{1,0:T(8,128)S(1)} %get-tuple-element.63.rest_2_.rest_3_), channel_id=1, source_target_pairs={{1,2},{2,1},{3,4},{4,3},{5,6},{6,5},{7,8},{8,7},{9,10},{10,9},{11,... | collective-permute-start | bytes 221192 | tf_op jit(solution)/shard_map/ppermute | solution.py:347
  41.8 0.1 collective-permute-start.6
  41.9 2.1 %collective-permute-done.7.rest_5_ = f32[144,128]{1,0:T(8,128)S(1)} collective-permute-done((f32[144,128]{1,0:T(8,128)S(1)}, f32[144,128]{1,0:T(8,128)S(1)}, u32[]{:S(2)}, u32[]{:S(2)}) %collective-permute-start.7) | collective-permute-done | bytes 73760 | tf_op jit(solution)/shard_map/ppermute | solution.py:347
  44.0 0.0 collective-permute-done.6.rest_4_
  44.0 0.7 %shard_map.114 = (f32[24,8,128]{2,1,0:T(8,128)S(1)}, bf16[96,512]{1,0:T(8,128)(2,1)S(1)}, f32[144,128]{1,0:T(8,128)S(1)}) custom-call(f32[288,8,128]{2,1,0:T(8,128)S(1)} %get-tuple-element.36.inv_ref, bf16[512,512]{1,0:T(8,128)(2,1)S(1)} %get-tuple-element.37.trace_ref, f32[24,8,128]{2,1,0:T(8,128)S(1)} %get-tuple-element.61.u_ref, ...), custom_call_target="tpu_custom_call" | custom-call | tf_op jit(solution)/shard_map/pallas_call | solution.py:331
  44.7 7.7 %collective-permute-start.9 = (f32[144,128]{1,0:T(8,128)S(1)}, f32[144,128]{1,0:T(8,128)S(1)}, u32[]{:S(2)}, u32[]{:S(2)}) collective-permute-start(f32[144,128]{1,0:T(8,128)S(1)} %get-tuple-element.66.rest_2_.rest_3_), channel_id=1, source_target_pairs={{1,2},{2,1},{3,4},{4,3},{5,6},{6,5},{7,8},{8,7},{9,10},{10,9},{11,... | collective-permute-start | bytes 221192 | tf_op jit(solution)/shard_map/ppermute | solution.py:347
  52.4 0.1 collective-permute-start.8
  52.5 2.1 %collective-permute-done.9.rest_5_ = f32[144,128]{1,0:T(8,128)S(1)} collective-permute-done((f32[144,128]{1,0:T(8,128)S(1)}, f32[144,128]{1,0:T(8,128)S(1)}, u32[]{:S(2)}, u32[]{:S(2)}) %collective-permute-start.9) | collective-permute-done | bytes 73760 | tf_op jit(solution)/shard_map/ppermute | solution.py:347
  54.6 0.0 collective-permute-done.8.rest_4_
  54.6 1.2 %shard_map.115 = f32[24,8,128]{2,1,0:T(8,128)} custom-call(f32[288,8,128]{2,1,0:T(8,128)S(1)} %get-tuple-element.36.inv_ref, f32[24,8,128]{2,1,0:T(8,128)S(1)} %get-tuple-element.64.u_ref, f32[24,8,128]{2,1,0:T(8,128)S(1)} %get-tuple-element.39.rest_0_, bf16[96,512]{1,0:T(8,128)(2,1)S(1)} %get-tuple-element.65.rest_1_, ...), custom_call_target="tpu_custom_call" | custom-call | tf_op jit(solution)/shard_map/pallas_call | solution.py:331
Async XLA Ops:
  1.7 11.8 %collective-permute-start.1 = (f32[144,128]{1,0:T(8,128)S(1)}, f32[144,128]{1,0:T(8,128)S(1)}, u32[]{:S(2)}, u32[]{:S(2)}) collective-permute-start(f32[144,128]{1,0:T(8,128)S(1)} %get-tuple-element.41.rest_2_.rest_3_), channel_id=1, source_target_pairs={{1,2},{2,1},{3,4},{4,3},{5,6},{6,5},{7,8},{8,7},{9,10},{10,9},{11,... | collective-permute-start | bytes 221192 | tf_op jit(solution)/shard_map/ppermute | solution.py:347
  11.3 2.2 %collective-permute-start = (f32[144,128]{1,0:T(8,128)S(1)}, f32[144,128]{1,0:T(8,128)S(1)}, u32[]{:S(2)}, u32[]{:S(2)}) collective-permute-start(f32[144,128]{1,0:T(8,128)S(1)} %get-tuple-element.41.rest_2_.rest_3_), channel_id=1, source_target_pairs={{0,1},{1,0},{2,3},{3,2},{4,5},{5,4},{6,7},{7,6},{8,9},{9,8},{10,11... | collective-permute-start | bytes 221192 | tf_op jit(solution)/shard_map/ppermute | solution.py:348
  14.2 9.4 %collective-permute-start.3 = (f32[48,128]{1,0:T(8,128)S(1)}, f32[48,128]{1,0:T(8,128)S(1)}, u32[]{:S(2)}, u32[]{:S(2)}) collective-permute-start(f32[48,128]{1,0:T(8,128)S(1)} %get-tuple-element.53.rest_3_), channel_id=1, source_target_pairs={{1,2},{2,1},{3,4},{4,3},{5,6},{6,5},{7,8},{8,7},{9,10},{10,9},{11,... | collective-permute-start | bytes 73736 | tf_op jit(solution)/shard_map/ppermute | solution.py:347
  21.9 1.7 %collective-permute-start.2 = (f32[48,128]{1,0:T(8,128)S(1)}, f32[48,128]{1,0:T(8,128)S(1)}, u32[]{:S(2)}, u32[]{:S(2)}) collective-permute-start(f32[48,128]{1,0:T(8,128)S(1)} %get-tuple-element.53.rest_3_), channel_id=1, source_target_pairs={{0,1},{1,0},{2,3},{3,2},{4,5},{5,4},{6,7},{7,6},{8,9},{9,8},{10,11... | collective-permute-start | bytes 73736 | tf_op jit(solution)/shard_map/ppermute | solution.py:348
  24.1 9.4 %collective-permute-start.5 = (f32[48,128]{1,0:T(8,128)S(1)}, f32[48,128]{1,0:T(8,128)S(1)}, u32[]{:S(2)}, u32[]{:S(2)}) collective-permute-start(f32[48,128]{1,0:T(8,128)S(1)} %get-tuple-element.60.rest_3_), channel_id=1, source_target_pairs={{1,2},{2,1},{3,4},{4,3},{5,6},{6,5},{7,8},{8,7},{9,10},{10,9},{11,... | collective-permute-start | bytes 73736 | tf_op jit(solution)/shard_map/ppermute | solution.py:347
  31.8 1.7 %collective-permute-start.4 = (f32[48,128]{1,0:T(8,128)S(1)}, f32[48,128]{1,0:T(8,128)S(1)}, u32[]{:S(2)}, u32[]{:S(2)}) collective-permute-start(f32[48,128]{1,0:T(8,128)S(1)} %get-tuple-element.60.rest_3_), channel_id=1, source_target_pairs={{0,1},{1,0},{2,3},{3,2},{4,5},{5,4},{6,7},{7,6},{8,9},{9,8},{10,11... | collective-permute-start | bytes 73736 | tf_op jit(solution)/shard_map/ppermute | solution.py:348
  34.1 9.9 %collective-permute-start.7 = (f32[144,128]{1,0:T(8,128)S(1)}, f32[144,128]{1,0:T(8,128)S(1)}, u32[]{:S(2)}, u32[]{:S(2)}) collective-permute-start(f32[144,128]{1,0:T(8,128)S(1)} %get-tuple-element.63.rest_2_.rest_3_), channel_id=1, source_target_pairs={{1,2},{2,1},{3,4},{4,3},{5,6},{6,5},{7,8},{8,7},{9,10},{10,9},{11,... | collective-permute-start | bytes 221192 | tf_op jit(solution)/shard_map/ppermute | solution.py:347
  41.8 2.2 %collective-permute-start.6 = (f32[144,128]{1,0:T(8,128)S(1)}, f32[144,128]{1,0:T(8,128)S(1)}, u32[]{:S(2)}, u32[]{:S(2)}) collective-permute-start(f32[144,128]{1,0:T(8,128)S(1)} %get-tuple-element.63.rest_2_.rest_3_), channel_id=1, source_target_pairs={{0,1},{1,0},{2,3},{3,2},{4,5},{5,4},{6,7},{7,6},{8,9},{9,8},{10,11... | collective-permute-start | bytes 221192 | tf_op jit(solution)/shard_map/ppermute | solution.py:348
  44.7 9.9 %collective-permute-start.9 = (f32[144,128]{1,0:T(8,128)S(1)}, f32[144,128]{1,0:T(8,128)S(1)}, u32[]{:S(2)}, u32[]{:S(2)}) collective-permute-start(f32[144,128]{1,0:T(8,128)S(1)} %get-tuple-element.66.rest_2_.rest_3_), channel_id=1, source_target_pairs={{1,2},{2,1},{3,4},{4,3},{5,6},{6,5},{7,8},{8,7},{9,10},{10,9},{11,... | collective-permute-start | bytes 221192 | tf_op jit(solution)/shard_map/ppermute | solution.py:347
  52.4 2.2 %collective-permute-start.8 = (f32[144,128]{1,0:T(8,128)S(1)}, f32[144,128]{1,0:T(8,128)S(1)}, u32[]{:S(2)}, u32[]{:S(2)}) collective-permute-start(f32[144,128]{1,0:T(8,128)S(1)} %get-tuple-element.66.rest_2_.rest_3_), channel_id=1, source_target_pairs={{0,1},{1,0},{2,3},{3,2},{4,5},{5,4},{6,7},{7,6},{8,9},{9,8},{10,11... | collective-permute-start | bytes 221192 | tf_op jit(solution)/shard_map/ppermute | solution.py:348

commit v4 on v3

--- a/solution.py
+++ b/solution.py
@@ -10,6 +10,9 @@
 QF = 8
 QC = 4
 VARS = 12
+FLUX_ROW = 144 + 288
+NUMBER_ROW = FLUX_ROW + 40
+MESSAGE_ROWS = NUMBER_ROW + 16
 SIGMA = 2.0
 OMEGA = 0.7
 F32 = jnp.float32
@@ -58,11 +61,10 @@
     return jnp.where(low, first, half_swap(second)), jnp.where(low, half_swap(first), second)
 
 
-def prepare_tables(me, owner_ref, elem_ref, side_ref, turn_ref, vj_ref, fj_ref,
-                   start_ref, idx_ref, sign_ref, low_start_ref, low_idx_ref, vjc_ref, fjc_ref):
+def face_tables(other, number, start_ref, low_start_ref, idx_ref, low_idx_ref, block_of, masks):
+    owner_of, elem_of, side_of, turn_of = number
     rows = rows8()
     lane = lanes8()
-    low = rows < 4
     element = rows & 3
     a = (lane >> 3) & 7
     b = lane & 7
@@ -70,25 +72,69 @@
     for face in range(6):
         sides = jnp.zeros((8, 128), jnp.int32)
         turns = jnp.zeros((8, 128), jnp.int32)
-        present = jnp.zeros((8, 128), jnp.int32)
+        here_far = jnp.zeros((8, 128), jnp.int32)
+        here_near = jnp.zeros((8, 128), jnp.int32)
         for e in range(4):
-            owner = owner_ref[e, face]
-            side = side_ref[e, face]
-            block = jnp.where(owner == me, 0, jnp.where(owner == (me ^ 1), 1, 2))
-            block = jnp.where(owner < 0, 0, block)
-            start_ref[face * 4 + e] = block * 144 + (side >> 1) * 48 + elem_ref[e, face]
-            low_start_ref[face * 4 + e] = block * 48 + elem_ref[e, face]
+            owner = owner_of(e, face)
+            side = side_of(e, face)
+            elem = elem_of(e, face)
+            block = block_of(owner)
+            start_ref[face * 4 + e] = block * 144 + (side >> 1) * 48 + elem
+            low_start_ref[face * 4 + e] = block * 48 + elem
+            masks(face * 4 + e, (side >> 1) * 48 + elem, elem)
             here = element == e
-            turns = jnp.where(here, turn_ref[e, face], turns)
+            turns = jnp.where(here, turn_of(e, face), turns)
             sides = jnp.where(here, side, sides)
-            present = jnp.where(here, jnp.where(owner >= 0, 1, 0), present)
+            far = jnp.where((owner >= 0) & (owner == other), 1, 0)
+            here_far = jnp.where(here, far, here_far)
+            here_near = jnp.where(here, jnp.where(owner >= 0, 1, 0) - far, here_near)
         swap = (turns & 1) == 1
         idx_ref[face] = (sides & 1) * 64 + jnp.where(swap, b * 8 + a, a * 8 + b)
         low_idx_ref[face] = sides * 16 + jnp.where(swap, (b & 3) * 4 + (a & 3), (a & 3) * 4 + (b & 3))
-        flips = (((turns >> 1) & a) + ((turns >> 2) & b)) & 1
-        signs.append((present * (1 - 2 * flips)).astype(F32))
+        flips = 1 - 2 * ((((turns >> 1) & a) + ((turns >> 2) & b)) & 1)
+        signs.append(((here_near * flips).astype(F32), (here_far * flips).astype(F32)))
+    return signs
+
+
+def flux_table(block_of, fjc_ref):
+    left = lanes8() < 64
     for f2 in range(3):
-        sign_ref[f2] = jnp.where(lane < 64, signs[2 * f2], signs[2 * f2 + 1])
+        for vp in range(6):
+            even = block_of(2 * f2 * 6 + vp)
+            odd = block_of((2 * f2 + 1) * 6 + vp)
+            for w in range(VARS):
+                fjc_ref[(f2 * 6 + vp) * VARS + w] = jnp.where(
+                    left,
+                    jnp.broadcast_to(even[:, w : w + 1], (8, 128)),
+                    jnp.broadcast_to(odd[:, w : w + 1], (8, 128)),
+                )
+
+
+def odd_partner(me):
+    return me - 1 + 2 * (me & 1)
+
+
+def prepare_tables(me, owner_ref, elem_ref, side_ref, turn_ref, vj_ref, fj_ref, start_ref, idx_ref, sign_ref,
+                   low_start_ref, low_idx_ref, near_ref, far_ref, plain_ref, low_plain_ref, vjc_ref, fjc_ref):
+    left = lanes8() < 64
+    low = rows8() < 4
+
+    def block_of(owner):
+        block = jnp.where(owner == me, 0, jnp.where(owner == (me ^ 1), 1, 2))
+        return jnp.where(owner < 0, 0, block)
+
+    def plain(at, value, low_value):
+        plain_ref[at] = value
+        low_plain_ref[at] = low_value
+
+    number = [lambda e, face, ref=ref: ref[e, face] for ref in (owner_ref, elem_ref, side_ref, turn_ref)]
+    signs = face_tables(odd_partner(me), number, start_ref, low_start_ref, idx_ref, low_idx_ref, block_of, plain)
+    for f2 in range(3):
+        near = jnp.where(left, signs[2 * f2][0], signs[2 * f2 + 1][0])
+        far = jnp.where(left, signs[2 * f2][1], signs[2 * f2 + 1][1])
+        sign_ref[f2] = near + far
+        near_ref[f2] = near
+        far_ref[f2] = far
     for vp in range(6):
         block = vj_ref[vp]
         for w in range(VARS):
@@ -96,25 +142,16 @@
             other = half_swap(spread)
             vjc_ref[(2 * vp) * VARS + w] = jnp.where(low, spread, other)
             vjc_ref[(2 * vp + 1) * VARS + w] = jnp.where(low, other, spread)
-    for f2 in range(3):
-        for vp in range(6):
-            even = fj_ref[2 * f2 * 6 + vp]
-            odd = fj_ref[(2 * f2 + 1) * 6 + vp]
-            for w in range(VARS):
-                fjc_ref[(f2 * 6 + vp) * VARS + w] = jnp.where(
-                    lane < 64,
-                    jnp.broadcast_to(even[:, w : w + 1], (8, 128)),
-                    jnp.broadcast_to(odd[:, w : w + 1], (8, 128)),
-                )
-
-
-def apply_inverse(inv_ref, residual, halves):
+    flux_table(lambda at: fj_ref[at], fjc_ref)
+
+
+def apply_inverse(inv_ref, residual, halves, stride=2):
     result = {}
     for h in range(halves):
         for v in range(VARS):
-            acc = inv_ref[(v * VARS) * 2 + h] * residual[0, h]
+            acc = inv_ref[(v * VARS) * stride + h] * residual[0, h]
             for w in range(1, VARS):
-                acc = acc + inv_ref[(v * VARS + w) * 2 + h] * residual[w, h]
+                acc = acc + inv_ref[(v * VARS + w) * stride + h] * residual[w, h]
             result[v, h] = OMEGA * acc
     return result
 
@@ -155,25 +192,25 @@
     return state
 
 
-def residual_of(u_ref, base_ref, split_ref, own_ref, mine_ref, even_ref, odd_ref, start_ref, idx_ref, sign_ref,
-                vjc_ref, fjc_ref, khi_ref, klo_ref, lift_ref, pool, pick0, pick1, jump_ref, halves_in, halves):
-    low = rows8() < 4
-    left = lanes8() < 64
-    size = mine_ref.shape[0]
-    pool[0:size, :] = mine_ref[...]
-    pool[size : 2 * size, :] = even_ref[...]
-    pool[2 * size : 3 * size, :] = odd_ref[...]
+def gather(source, start_ref, pick0, pick1):
     for face in range(6):
         target = pick1 if face % 2 else pick0
         for e in range(4):
-            target[pl.ds((face // 2) * 48 + e, 12, stride=4), :] = pool[pl.ds(start_ref[face * 4 + e], 12, stride=4), :]
+            target[pl.ds((face // 2) * 48 + e, 12, stride=4), :] = source[pl.ds(start_ref[face * 4 + e], 12, stride=4), :]
+
+
+def lifted_flux(own_ref, idx_ref, sign_ref, fjc_ref, lift_ref, pick0, pick1, jump_ref, halves):
+    low = rows8() < 4
+    left = lanes8() < 64
     for f2 in range(3):
         spread = {}
         for vp in range(6):
             at = f2 * 48 + vp * 8
             even = jnp.take_along_axis(pick0[at : at + 8, :], idx_ref[2 * f2], axis=1)
             odd = jnp.take_along_axis(pick1[at : at + 8, :], idx_ref[2 * f2 + 1], axis=1)
-            jump = own_ref[at : at + 8, :] - jnp.where(left, even, odd) * sign_ref[f2]
+            jump = jnp.where(left, even, odd) * sign_ref[f2]
+            if own_ref is not None:
+                jump = own_ref[at : at + 8, :] - jump
             spread[2 * vp], spread[2 * vp + 1] = pair_turn(jump, jump, low)
         flux = []
         for vp in range(6):
@@ -183,13 +220,26 @@
             flux.append(acc)
         for vq in range(3):
             store_split(jump_ref, vq * 16, f2 * 128, flux[2 * vq], flux[2 * vq + 1])
+    lifted = jnp.dot(jump_ref[...], lift_ref[:, : 256 * halves], preferred_element_type=F32)
+    return to_state(lifted[:48] + lifted[48:], halves, low)
+
+
+def residual_of(u_ref, base_ref, split_ref, own_ref, mine_ref, even_ref, odd_ref, start_ref, idx_ref, sign_ref,
+                vjc_ref, fjc_ref, khi_ref, klo_ref, lift_ref, pool, pick0, pick1, jump_ref, halves_in, halves):
+    size = mine_ref.shape[0]
+    pool[0:size, :] = mine_ref[...]
+    pool[size : 2 * size, :] = even_ref[...]
+    if odd_ref is not None:
+        pool[2 * size : 3 * size, :] = odd_ref[0:size, :]
+    else:
+        pool[2 * size : 3 * size, :] = mine_ref[...]
+    gather(pool, start_ref, pick0, pick1)
+    lifted = lifted_flux(own_ref, idx_ref, sign_ref, fjc_ref, lift_ref, pick0, pick1, jump_ref, halves)
     kin = 256 * halves_in
     kout = 256 * halves
     blended = jnp.dot(split_ref[:, :kin], khi_ref[:kin, :kout], preferred_element_type=F32)
     rest = jnp.dot(split_ref[0:48, :kin], klo_ref[:kin, :kout], preferred_element_type=F32)
-    blended = to_state(blended[:48] + blended[48:] + rest, halves, low)
-    lifted = jnp.dot(jump_ref[...], lift_ref[:, :kout], preferred_element_type=F32)
-    lifted = to_state(lifted[:48] + lifted[48:], halves, low)
+    blended = to_state(blended[:48] + blended[48:] + rest, halves, rows8() < 4)
     residual = {}
     for h in range(halves):
         for v in range(VARS):
@@ -216,23 +266,63 @@
     return copies
 
 
-def first_body(*refs):
-    sources, (u_ref, split_ref, face_ref), targets, sems = refs[:3], refs[3:6], refs[6:9], refs[9]
-    inv_ref, rhs_ref, trace_ref = targets
-    copies = start_all(sources, targets, sems)
-    copies[0].wait()
-    copies[1].wait()
+def first_body(me_ref, *refs):
+    sources, (u_ref, split_ref, face_ref, message_ref, inv_ref, rhs_ref, trace_ref) = refs[:8], refs[8:15]
+    fj_ref, numbers, sems = refs[15], refs[16:20], refs[20]
+    copies = start_all(sources, (*numbers, fj_ref, inv_ref, rhs_ref, trace_ref), sems)
+    for copy in copies[:5]:
+        copy.wait()
+    for at in range(36):
+        row = FLUX_ROW + 8 * (at // 8)
+        column = 16 * (at % 8)
+        message_ref[row : row + 8, column : column + 12] = fj_ref[at]
+    for at in range(4):
+        row = NUMBER_ROW + 4 * at
+        message_ref[row : row + 4, 0:6] = numbers[at][...].astype(F32)
+    copies[5].wait()
+    copies[6].wait()
     state = apply_inverse(inv_ref, {(v, h): rhs_ref[2 * v + h] for v in range(VARS) for h in range(2)}, 2)
     for v in range(VARS):
         for h in range(2):
             u_ref[2 * v + h] = state[v, h]
-    copies[2].wait()
+    lane = lanes8()
+    place = ((lane >> 4) & 1) * 64 + ((lane >> 2) & 3) * 8 + (lane & 3)
+    for at in range(36):
+        tiles = [jnp.take_along_axis(inv_ref[2 * (4 * at + part)], place, axis=1) for part in range(4)]
+        packed = jnp.where(lane < 64, jnp.where(lane < 32, tiles[0], tiles[1]), jnp.where(lane < 96, tiles[2], tiles[3]))
+        message_ref[144 + 8 * at : 152 + 8 * at, :] = packed
+    copies[7].wait()
     emit(state, 2, trace_ref, split_ref, face_ref)
+    message_ref[0:144, :] = face_ref[...]
+
+
+def ghost_prepare_body(me_ref, far_ref, start_ref, idx_ref, sign_ref, fjc_ref, inv_ref,
+                       fine_start_ref, fine_idx_ref, number_ref, sems):
+    copy = pltpu.make_async_copy(far_ref.at[pl.ds(NUMBER_ROW, 16)], number_ref, sems.at[0])
+    copy.start()
+    flux_table(
+        lambda at: far_ref[FLUX_ROW + 8 * (at // 8) : FLUX_ROW + 8 * (at // 8) + 8, 16 * (at % 8) : 16 * (at % 8) + 12],
+        fjc_ref,
+    )
+    lane = lanes8()
+    place = ((lane >> 6) & 1) * 16 + ((lane >> 3) & 3) * 4 + (lane & 3)
+    for at in range(36):
+        packed = far_ref[144 + 8 * at : 152 + 8 * at, :]
+        for part in range(4):
+            inv_ref[4 * at + part] = jnp.take_along_axis(packed, place + 32 * part, axis=1)
+    copy.wait()
+    left = lanes8() < 64
+    number = [lambda e, face, at=at: number_ref[4 * at + e, face].astype(jnp.int32) for at in range(4)]
+    signs = face_tables(
+        me_ref[0], number, fine_start_ref, start_ref, fine_idx_ref, idx_ref, lambda owner: 0, lambda *values: None
+    )
+    for f2 in range(3):
+        sign_ref[f2] = jnp.where(left, signs[2 * f2][1], signs[2 * f2 + 1][1])
 
 
 def prepare_body(me_ref, *refs):
-    sources, tables, (khi_ref, klo_ref, lift_ref) = refs[:8], refs[8:15], refs[15:18]
-    owner_ref, elem_ref, side_ref, turn_ref, vj_ref, fj_ref, stiff_ref, sems = refs[18:]
+    sources, tables, (khi_ref, klo_ref, lift_ref) = refs[:8], refs[8:19], refs[19:22]
+    owner_ref, elem_ref, side_ref, turn_ref, vj_ref, fj_ref, stiff_ref, sems = refs[22:]
     copies = start_all(sources, (owner_ref, elem_ref, side_ref, turn_ref, vj_ref, fj_ref, stiff_ref, lift_ref), sems)
     for copy in copies[:6]:
         copy.wait()
@@ -281,18 +371,53 @@
         copy.wait()
 
 
-def restrict_body(inv_ref, trace_ref, u_ref, *rest):
-    shared, (low_ref, out_ref, split_ref, face_ref, mine_ref), scratch = rest[:14], rest[14:19], rest[19:]
-    residual = residual_of(u_ref, *shared, *scratch, 2, 1)
+def local_step(coarse, u_ref, base_ref, split_ref, own_ref, mine_ref, even_ref, *rest):
+    tables, payload_ref, scratch = rest[:8], rest[8], rest[9:]
+    halves = 1 if coarse else 2
+    residual = residual_of(u_ref, base_ref, split_ref, own_ref, mine_ref, even_ref, None, *tables, *scratch, 2, halves)
+    size = mine_ref.shape[0]
+    payload_ref[0:size, :] = mine_ref[...]
+    mask = coarse_mask() if coarse else None
+    for v in range(VARS):
+        for h in range(halves):
+            at = size + 8 * (halves * v + h)
+            payload_ref[at : at + 8, :] = residual[v, h] * mask if coarse else residual[v, h]
+
+
+def local_low_body(*refs):
+    local_step(True, *refs)
+
+
+def joined(base_ref, source_ref, halves, start_ref, idx_ref, sign_ref, fjc_ref, lift_ref, pick0, pick1, jump_ref):
+    gather(source_ref, start_ref, pick0, pick1)
+    lifted = lifted_flux(None, idx_ref, sign_ref, fjc_ref, lift_ref, pick0, pick1, jump_ref, halves)
+    size = base_ref.shape[0] - 96 * halves
     mask = coarse_mask()
-    residual = {key: tile * mask for key, tile in residual.items()}
+    residual = {}
+    for v in range(VARS):
+        for h in range(halves):
+            at = size + 8 * (halves * v + h)
+            flux = lifted[v, h] * mask if halves == 1 else lifted[v, h]
+            residual[v, h] = base_ref[at : at + 8, :] + flux
+    return residual
+
+
+def own_low_body(inv_ref, trace_ref, mine_ref, far_ref, *rest):
+    tables, (low_ref, out_ref, split_ref, face_ref, sent_ref), scratch = rest[:5], rest[5:10], rest[10:]
+    residual = joined(mine_ref, far_ref, 1, *tables, *scratch)
     state = apply_inverse(inv_ref, residual, 1)
     for v in range(VARS):
         low_ref[2 * v] = residual[v, 0]
         low_ref[2 * v + 1] = zero_tile()
         out_ref[2 * v] = state[v, 0]
         out_ref[2 * v + 1] = zero_tile()
-    emit(state, 1, trace_ref, split_ref, face_ref, mine_ref)
+    emit(state, 1, trace_ref, split_ref, face_ref, sent_ref)
+
+
+def ghost_low_body(inv_ref, trace_ref, mine_ref, far_ref, *rest):
+    tables, sent_ref, scratch = rest[:5], rest[5], rest[6:]
+    residual = joined(far_ref, mine_ref, 1, *tables, *scratch[:3])
+    emit(apply_inverse(inv_ref, residual, 1, stride=1), 1, trace_ref, scratch[3], scratch[4], sent_ref)
 
 
 def coarse_body(inv_ref, trace_ref, fine_ref, u_ref, *rest):
@@ -338,18 +463,19 @@
     )(*args)
 
 
-def exchange(faces):
+def odd_swap(value):
     count = lax.axis_size("dom")
-    odd = []
+    route = []
     for at in range(1, count - 1, 2):
-        odd += [(at, at + 1), (at + 1, at)]
-    even = [(at, at ^ 1) for at in range(count)]
-    from_odd = lax.ppermute(faces, "dom", odd)
-    from_even = lax.ppermute(faces, "dom", even)
-    return in_vmem(from_even), in_vmem(from_odd)
-
-
-def local(rhs, stiffness, vol_jac, face_jac, block_inv, face_owner, face_elem, face_side, face_turn):
+        route += [(at, at + 1), (at + 1, at)]
+    return lax.ppermute(value, "dom", route)
+
+
+def even_swap(value):
+    return in_vmem(lax.ppermute(value, "dom", [(at, at ^ 1) for at in range(lax.axis_size("dom"))]))
+
+
+def cycle(rhs, stiffness, vol_jac, face_jac, block_inv, face_owner, face_elem, face_side, face_turn):
     me = lax.axis_index("dom").astype(jnp.int32).reshape(1)
     rhs_state = rhs.reshape(4, 12, 4, 128).transpose(1, 2, 0, 3).reshape(24, 8, 128)
     inverse = block_inv.reshape(4, 12, 12, 4, 128).transpose(1, 2, 3, 0, 4).reshape(288, 8, 128)
@@ -357,23 +483,41 @@
     fj = face_jac.transpose(1, 2, 0, 3).reshape(36, 8, 12)
     trace = jnp.asarray(np.concatenate([trace_matrix(), low_trace_matrix()], 1), BF16)
     lift = jnp.asarray(lift_matrix(), BF16)
-    loads = (inverse, rhs_state, trace)
-    u, split, faces, inverse, rhs_state, trace = call(
+    numbers = (face_owner, face_elem, face_side, face_turn)
+    integers = pltpu.SMEM((24,), jnp.int32)
+    indices = VMEM((6, 8, 128), jnp.int32)
+    signs = VMEM((3, 8, 128), F32)
+    u, split, faces, message, inverse, rhs_state, trace = call(
         first_body,
-        (STATE, SPLIT, FACES, *(VMEM(load.shape, load.dtype) for load in loads)),
-        tuple(in_hbm(load) for load in loads),
-        (pltpu.SemaphoreType.DMA((3,)),),
+        (
+            STATE,
+            SPLIT,
+            FACES,
+            VMEM((MESSAGE_ROWS, 128), F32),
+            VMEM((288, 8, 128), F32),
+            STATE,
+            VMEM(trace.shape, BF16),
+        ),
+        (me, *(in_hbm(load) for load in (*numbers, fj, inverse, rhs_state, trace))),
+        (VMEM((36, 8, 12), F32), *(VMEM((4, 6), jnp.int32) for _ in range(4)), pltpu.SemaphoreType.DMA((8,))),
+        smem=(0,),
         far=True,
     )
-    loads = (face_owner, face_elem, face_side, face_turn, vj, fj, stiffness, lift)
-    start, idx, sign, low_start, low_idx, vjc, fjc, khi, klo, lift = call(
+    far_message = in_vmem(odd_swap(message))
+    even = even_swap(faces)
+    loads = (*numbers, vj, fj, stiffness, lift)
+    start, idx, sign, low_start, low_idx, near, far, _, low_plain, vjc, fjc, khi, klo, lift = call(
         prepare_body,
         (
-            pltpu.SMEM((24,), jnp.int32),
-            VMEM((6, 8, 128), jnp.int32),
-            VMEM((3, 8, 128), F32),
-            pltpu.SMEM((24,), jnp.int32),
-            VMEM((6, 8, 128), jnp.int32),
+            integers,
+            indices,
+            signs,
+            integers,
+            indices,
+            signs,
+            signs,
+            integers,
+            integers,
             VMEM((144, 8, 128), F32),
             VMEM((216, 8, 128), F32),
             VMEM((512, 512), BF16),
@@ -389,46 +533,81 @@
             pltpu.SemaphoreType.DMA((8,)),
         ),
         smem=(0,),
-        smem_outs=(0, 3),
+        smem_outs=(0, 3, 7, 8),
         far=True,
     )
-    tables = (sign, vjc, fjc, khi, klo, lift)
-    scratch = (VMEM((432, 128), F32), FACES, FACES, VMEM((96, 384), BF16))
-
-    def stage(body, outs, head, u, base, split, faces, sent=None, more=(), far_out=False):
-        low = sent is not None
-        sent = sent if low else faces
-        even, odd = exchange(sent)
-        places = (low_start, low_idx) if low else (start, idx)
-        args = (*head, u, base, split, faces, sent, even, odd, *places, *tables)
-        return call(body, outs, args, (*scratch, *more), smem=(len(head) + 7,), far_out=far_out)
-
-    fine_two, split, faces, sent = stage(
-        fine_low_body, (STATE, SPLIT, FACES, LOW_FACES), (inverse, trace), u, rhs_state, split, faces
-    )
-    low_rhs, coarse, split, faces, sent = stage(
-        restrict_body,
+    volume = (vjc, fjc, khi, klo, lift)
+    picks = (FACES, FACES, VMEM((96, 384), BF16))
+    pool = (VMEM((432, 128), F32), *picks)
+
+    fine_two, split, faces, sent = call(
+        fine_low_body,
+        (STATE, SPLIT, FACES, LOW_FACES),
+        (inverse, trace, u, rhs_state, split, faces, faces, even, far_message, start, idx, sign, *volume),
+        pool,
+        smem=(9,),
+    )
+    even = even_swap(sent)
+    (payload,) = call(
+        local_low_body,
+        (FACES,),
+        (fine_two, rhs_state, split, faces, sent, even, low_start, low_idx, near, *volume),
+        pool,
+        smem=(6,),
+    )
+    far_payload = in_vmem(odd_swap(payload))
+    ghost_start, ghost_idx, ghost_sign, ghost_fjc, ghost_inverse = call(
+        ghost_prepare_body,
+        (integers, indices, signs, VMEM((216, 8, 128), F32), VMEM((144, 8, 128), F32)),
+        (me, far_message),
+        (
+            pltpu.SMEM((24,), jnp.int32),
+            VMEM((6, 8, 128), jnp.int32),
+            pltpu.SMEM((16, 128), F32),
+            pltpu.SemaphoreType.DMA((1,)),
+        ),
+        smem=(0,),
+        smem_outs=(0,),
+    )
+    low_rhs, coarse, split, faces, sent = call(
+        own_low_body,
         (STATE, STATE, SPLIT, FACES, LOW_FACES),
-        (inverse, trace),
-        fine_two,
-        rhs_state,
-        split,
-        faces,
-        sent,
-    )
-    u, split, faces = stage(
-        coarse_body, (STATE, SPLIT, FACES), (inverse, trace, fine_two), coarse, low_rhs, split, faces, sent
-    )
-    u, split, faces = stage(fine_body, (STATE, SPLIT, FACES), (inverse, trace), u, rhs_state, split, faces)
-    (u,) = stage(
+        (inverse, trace, payload, far_payload, low_plain, low_idx, far, fjc, lift),
+        picks,
+        smem=(4,),
+    )
+    even = even_swap(sent)
+    (odd,) = call(
+        ghost_low_body,
+        (LOW_FACES,),
+        (ghost_inverse, trace, payload, far_payload, ghost_start, ghost_idx, ghost_sign, ghost_fjc, lift),
+        (*picks, SPLIT, FACES),
+        smem=(4,),
+    )
+    u, split, faces = call(
+        coarse_body,
+        (STATE, SPLIT, FACES),
+        (inverse, trace, fine_two, coarse, low_rhs, split, faces, sent, even, odd, low_start, low_idx, sign, *volume),
+        pool,
+        smem=(10,),
+    )
+    odd = in_vmem(odd_swap(faces))
+    even = even_swap(faces)
+    u, split, faces = call(
+        fine_body,
+        (STATE, SPLIT, FACES),
+        (inverse, trace, u, rhs_state, split, faces, faces, even, odd, start, idx, sign, *volume),
+        pool,
+        smem=(9,),
+    )
+    odd = in_vmem(odd_swap(faces))
+    even = even_swap(faces)
+    (u,) = call(
         last_body,
         (jax.ShapeDtypeStruct((24, 8, 128), F32),),
-        (inverse,),
-        u,
-        rhs_state,
-        split,
-        faces,
-        more=(STATE, pltpu.SemaphoreType.DMA((3,))),
+        (inverse, u, rhs_state, split, faces, faces, even, odd, start, idx, sign, *volume),
+        (*pool, STATE, pltpu.SemaphoreType.DMA((3,))),
+        smem=(8,),
         far_out=True,
     )
     return u.reshape(12, 4, 4, 128).transpose(2, 0, 1, 3).reshape(4, 12, 512)
@@ -437,7 +616,7 @@
 def solution(mesh):
     dom = P("dom")
     return jax.shard_map(
-        local,
+        cycle,
         mesh=mesh,
         in_specs=(dom, P(), dom, dom, dom, dom, dom, dom, dom),
         out_specs=dom,

time: 56 us -> 54.1 us (0.966)
  starting transfers between devices: 40.8 us -> 34 us
  Pallas kernels: 7.52 us -> 10.7 us
  waiting for transfers between devices: 7.36 us -> 9 us
    ppermute x10 -> x9, starting transfers between devices: 40.8 us -> 34 us  [the longest x4 33.1 us: odd_swap(): return lax.ppermute(value, 'dom', route)]
    pallas_call x7 -> x10, Pallas kernels: 7.52 us -> 10.7 us  [call(): pl.pallas_call(body, out_shape=list(outs), in_specs=[scalar if at in smem...]
    ppermute x10 -> x9, waiting for transfers between devices: 7.36 us -> 9 us  [the longest x4 7.8 us: odd_swap(): return lax.ppermute(value, 'dom', route)]
  transfers between devices with their start and end apart: 10 -> 9, of which waited for: 4 -> 5; matrix products, arithmetic and copies ran while one was open for 0% -> 0% of each run, Pallas kernels for 4% -> 8%
where the time goes in v4:
time: 54.1 us; the launch traced here: 53.9 us
  starting transfers between devices  34 us (63%)
  Pallas kernels  10.7 us (20%)
  waiting for transfers between devices  9 us (17%)
    ppermute x4, starting transfers between devices, odd_swap(): return lax.ppermute(value, 'dom', route)  33.1 us
    pallas_call x10, Pallas kernels, call(): pl.pallas_call(body, out_shape=list(outs), in_specs=[scalar if at in smem...  10.7 us
    ppermute x4, waiting for transfers between devices, odd_swap(): return lax.ppermute(value, 'dom', route)  7.8 us
    ppermute x5, waiting for transfers between devices, even_swap(): lax.ppermute(value, 'dom', [(at, at ^ 1) for at in range(lax.axis_size('d...  1.2 us
  transfers between devices with their start and end apart: 9, of which 5 were waited for; matrix products, arithmetic and copies ran while one was open for 0% of the time, Pallas kernels for 8%

profile of v4, /device:TPU:24, one launch (start us, length us, event | category | flops | bytes accessed | tf_op | source)
XLA Modules:
  0.0 53.9 jit_solution(17009793955312599108)
XLA Ops:
  0.0 2.0 %shard_map.109 = (f32[24,8,128]{2,1,0:T(8,128)S(1)}, bf16[96,512]{1,0:T(8,128)(2,1)S(1)}, f32[144,128]{1,0:T(8,128)S(1)}, f32[488,128]{1,0:T(8,128)S(1)}, f32[28...) custom-call(s32[1]{0:T(128)} %bitcast.me_ref, s32[4,6]{1,0:T(4,128)} %refs_0_.3, ...), custom_call_target="tpu_custom_call" | custom-call | tf_op jit(solution)/shard_map/pallas_call | solution.py:456
  2.0 9.6 %collective-permute-start.1 = (f32[488,128]{1,0:T(8,128)S(1)}, f32[488,128]{1,0:T(8,128)S(1)}, u32[]{:S(2)}, u32[]{:S(2)}) collective-permute-start(f32[488,128]{1,0:T(8,128)S(1)} %get-tuple-element.51), channel_id=1, source_target_pairs={{1,2},{2,1},{3,4},{4,3},{5,6},{6,5},{7,8},{8,7},{9,10},{10,9},{11,... | collective-permute-start | bytes 749576 | tf_op jit(solution)/shard_map/ppermute | solution.py:471
  11.6 0.1 collective-permute-start
  11.7 2.1 %shard_map.110 = (s32[24]{0:T(128)S(4)}, s32[6,8,128]{2,1,0:T(8,128)S(1)}, f32[3,8,128]{2,1,0:T(8,128)S(1)}, s32[24]{0:T(128)S(4)}, s32[6,8,128]{2,1,0:T(8,128)S...) custom-call(s32[1]{0:T(128)} %bitcast.me_ref, ...), custom_call_target="tpu_custom_call" | custom-call | tf_op jit(solution)/shard_map/pallas_call | solution.py:456
  13.8 0.0 collective-permute-done.rest_4_
  13.8 1.7 %collective-permute-done.1.rest_5_.far_ref = f32[488,128]{1,0:T(8,128)S(1)} collective-permute-done((f32[488,128]{1,0:T(8,128)S(1)}, f32[488,128]{1,0:T(8,128)S(1)}, u32[]{:S(2)}, u32[]{:S(2)}) %collective-permute-start.1) | collective-permute-done | bytes 249888 | tf_op jit(solution)/shard_map/ppermute | solution.py:471
  15.5 0.9 %shard_map.111 = (f32[24,8,128]{2,1,0:T(8,128)S(1)}, bf16[96,512]{1,0:T(8,128)(2,1)S(1)}, f32[144,128]{1,0:T(8,128)S(1)}, f32[48,128]{1,0:T(8,128)S(1)}) custom-call(f32[288,8,128]{2,1,0:T(8,128)S(1)} %get-tuple-element.45.inv_ref, bf16[512,512]{1,0:T(8,128)(2,1)S(1)} %get-tuple-element.46.trace_ref, f32[24,8,128]{2,1,0:T(8,128)S(1)} %get-tuple-element.47.u_ref, ...), custom_call_target="tpu_custom_call" | custom-call | tf_op jit(solution)/shard_map/pallas_call | solution.py:456
  16.4 0.0 collective-permute-start.2
  16.4 1.2 %collective-permute-done.2.refs_5_ = f32[48,128]{1,0:T(8,128)S(1)} collective-permute-done((f32[48,128]{1,0:T(8,128)S(1)}, f32[48,128]{1,0:T(8,128)S(1)}, u32[]{:S(2)}, u32[]{:S(2)}) %collective-permute-start.2) | collective-permute-done | bytes 24608 | tf_op jit(solution)/shard_map/ppermute | solution.py:475
  17.6 0.4 shard_map.112.mine_ref
  18.0 7.8 %collective-permute-start.3 = (f32[144,128]{1,0:T(8,128)S(1)}, f32[144,128]{1,0:T(8,128)S(1)}, u32[]{:S(2)}, u32[]{:S(2)}) collective-permute-start(f32[144,128]{1,0:T(8,128)S(1)} %shard_map.112.mine_ref), channel_id=1, source_target_pairs={{1,2},{2,1},{3,4},{4,3},{5,6},{6,5},{7,8},{8,7},{9,10},{10,9},{11,... | collective-permute-start | bytes 221192 | tf_op jit(solution)/shard_map/ppermute | solution.py:471
  25.9 2.0 %collective-permute-done.3.far_ref = f32[144,128]{1,0:T(8,128)S(1)} collective-permute-done((f32[144,128]{1,0:T(8,128)S(1)}, f32[144,128]{1,0:T(8,128)S(1)}, u32[]{:S(2)}, u32[]{:S(2)}) %collective-permute-start.3) | collective-permute-done | bytes 73760 | tf_op jit(solution)/shard_map/ppermute | solution.py:471
  27.9 0.5 %shard_map.113 = (f32[24,8,128]{2,1,0:T(8,128)S(1)}, f32[24,8,128]{2,1,0:T(8,128)S(1)}, bf16[96,512]{1,0:T(8,128)(2,1)S(1)}, f32[144,128]{1,0:T(8,128)S(1)}, f32[48,128]{1,0:T(8,128)S(1)}) custom-call(f32[288,8,128]{2,1,0:T(8,128)S(1)} %get-tuple-element.45.inv_ref, bf16[512,512]{1,0:T(8,128)(2,1)S(1)} %get-tuple-element.46.trace_ref, ...), custom_call_target="tpu_custom_call" | custom-call | tf_op jit(solution)/shard_map/pallas_call | solution.py:456
  28.5 0.1 collective-permute-start.4
  28.6 1.4 %shard_map.114 = (s32[24]{0:T(128)S(4)}, s32[6,8,128]{2,1,0:T(8,128)S(1)}, f32[3,8,128]{2,1,0:T(8,128)S(1)}, f32[216,8,128]{2,1,0:T(8,128)S(1)}, f32[144,8,128]{2,1,0:T(8,128)S(1)}) custom-call(s32[1]{0:T(128)} %bitcast.me_ref, f32[488,128]{1,0:T(8,128)S(1)} %collective-permute-done.1.rest_5_.far_ref), custom_call_target="tpu_custom_call" | custom-call | tf_op jit(solution)/shard_map/pallas_call | solution.py:456
  30.0 0.5 %shard_map.115.rest_5_ = f32[48,128]{1,0:T(8,128)S(1)} custom-call(f32[144,8,128]{2,1,0:T(8,128)S(1)} %get-tuple-element.74.inv_ref, bf16[512,512]{1,0:T(8,128)(2,1)S(1)} %get-tuple-element.46.trace_ref, f32[144,128]{1,0:T(8,128)S(1)} %shard_map.112.mine_ref, f32[144,128]{1,0:T(8,128)S(1)} %collective-permute-done.3.far_ref, ...), custom_call_target="tpu_custom_call" | custom-call | tf_op jit(solution)/shard_map/pallas_call | solution.py:456
  30.6 0.0 collective-permute-done.4.rest_4_
  30.6 0.6 %shard_map.116 = (f32[24,8,128]{2,1,0:T(8,128)S(1)}, bf16[96,512]{1,0:T(8,128)(2,1)S(1)}, f32[144,128]{1,0:T(8,128)S(1)}) custom-call(f32[288,8,128]{2,1,0:T(8,128)S(1)} %get-tuple-element.45.inv_ref, bf16[512,512]{1,0:T(8,128)(2,1)S(1)} %get-tuple-element.46.trace_ref, f32[24,8,128]{2,1,0:T(8,128)S(1)} %get-tuple-element.60.refs_0_.fine_ref, ...), custom_call_target="tpu_custom_call" | custom-call | tf_op jit(solution)/shard_map/pallas_call | solution.py:456
  31.2 0.6 %collective-permute-start.5 = (f32[144,128]{1,0:T(8,128)S(1)}, f32[144,128]{1,0:T(8,128)S(1)}, u32[]{:S(2)}, u32[]{:S(2)}) collective-permute-start(f32[144,128]{1,0:T(8,128)S(1)} %get-tuple-element.81.rest_2_.rest_3_), channel_id=1, source_target_pairs={{0,1},{1,0},{2,3},{3,2},{4,5},{5,4},{6,7},{7,6},{8,9},{9,8},{10,11... | collective-permute-start | bytes 221192 | tf_op jit(solution)/shard_map/ppermute | solution.py:475
  31.8 7.8 %collective-permute-start.6 = (f32[144,128]{1,0:T(8,128)S(1)}, f32[144,128]{1,0:T(8,128)S(1)}, u32[]{:S(2)}, u32[]{:S(2)}) collective-permute-start(f32[144,128]{1,0:T(8,128)S(1)} %get-tuple-element.81.rest_2_.rest_3_), channel_id=1, source_target_pairs={{1,2},{2,1},{3,4},{4,3},{5,6},{6,5},{7,8},{8,7},{9,10},{10,9},{11,... | collective-permute-start | bytes 221192 | tf_op jit(solution)/shard_map/ppermute | solution.py:471
  39.6 0.0 collective-permute-done.5.rest_4_
  39.6 2.0 %collective-permute-done.6.rest_5_ = f32[144,128]{1,0:T(8,128)S(1)} collective-permute-done((f32[144,128]{1,0:T(8,128)S(1)}, f32[144,128]{1,0:T(8,128)S(1)}, u32[]{:S(2)}, u32[]{:S(2)}) %collective-permute-start.6) | collective-permute-done | bytes 73760 | tf_op jit(solution)/shard_map/ppermute | solution.py:471
  41.7 0.9 %shard_map.117 = (f32[24,8,128]{2,1,0:T(8,128)S(1)}, bf16[96,512]{1,0:T(8,128)(2,1)S(1)}, f32[144,128]{1,0:T(8,128)S(1)}) custom-call(f32[288,8,128]{2,1,0:T(8,128)S(1)} %get-tuple-element.45.inv_ref, bf16[512,512]{1,0:T(8,128)(2,1)S(1)} %get-tuple-element.46.trace_ref, f32[24,8,128]{2,1,0:T(8,128)S(1)} %get-tuple-element.79.u_ref, ...), custom_call_target="tpu_custom_call" | custom-call | tf_op jit(solution)/shard_map/pallas_call | solution.py:456
  42.5 0.1 collective-permute-start.7
  42.6 7.8 %collective-permute-start.8 = (f32[144,128]{1,0:T(8,128)S(1)}, f32[144,128]{1,0:T(8,128)S(1)}, u32[]{:S(2)}, u32[]{:S(2)}) collective-permute-start(f32[144,128]{1,0:T(8,128)S(1)} %get-tuple-element.84.rest_2_.rest_3_), channel_id=1, source_target_pairs={{1,2},{2,1},{3,4},{4,3},{5,6},{6,5},{7,8},{8,7},{9,10},{10,9},{11,... | collective-permute-start | bytes 221192 | tf_op jit(solution)/shard_map/ppermute | solution.py:471
  50.5 0.0 collective-permute-done.7.rest_4_
  50.5 2.0 %collective-permute-done.8.rest_5_ = f32[144,128]{1,0:T(8,128)S(1)} collective-permute-done((f32[144,128]{1,0:T(8,128)S(1)}, f32[144,128]{1,0:T(8,128)S(1)}, u32[]{:S(2)}, u32[]{:S(2)}) %collective-permute-start.8) | collective-permute-done | bytes 73760 | tf_op jit(solution)/shard_map/ppermute | solution.py:471
  52.5 1.3 %shard_map.118 = f32[24,8,128]{2,1,0:T(8,128)} custom-call(f32[288,8,128]{2,1,0:T(8,128)S(1)} %get-tuple-element.45.inv_ref, f32[24,8,128]{2,1,0:T(8,128)S(1)} %get-tuple-element.82.u_ref, f32[24,8,128]{2,1,0:T(8,128)S(1)} %get-tuple-element.48.rest_0_.refs_1_, bf16[96,512]{1,0:T(8,128)(2,1)S(1)} %get-tuple-element.83.rest_1_, ...), custom_call_target="tpu_custom_call" | custom-call | tf_op jit(solution)/shard_map/pallas_call | solution.py:456
Async XLA Ops:
  2.0 13.5 %collective-permute-start.1 = (f32[488,128]{1,0:T(8,128)S(1)}, f32[488,128]{1,0:T(8,128)S(1)}, u32[]{:S(2)}, u32[]{:S(2)}) collective-permute-start(f32[488,128]{1,0:T(8,128)S(1)} %get-tuple-element.51), channel_id=1, source_target_pairs={{1,2},{2,1},{3,4},{4,3},{5,6},{6,5},{7,8},{8,7},{9,10},{10,9},{11,... | collective-permute-start | bytes 749576 | tf_op jit(solution)/shard_map/ppermute | solution.py:471
  11.6 2.2 %collective-permute-start = (f32[144,128]{1,0:T(8,128)S(1)}, f32[144,128]{1,0:T(8,128)S(1)}, u32[]{:S(2)}, u32[]{:S(2)}) collective-permute-start(f32[144,128]{1,0:T(8,128)S(1)} %get-tuple-element.50.rest_2_.rest_3_), channel_id=1, source_target_pairs={{0,1},{1,0},{2,3},{3,2},{4,5},{5,4},{6,7},{7,6},{8,9},{9,8},{10,11... | collective-permute-start | bytes 221192 | tf_op jit(solution)/shard_map/ppermute | solution.py:475
  16.4 1.2 %collective-permute-start.2 = (f32[48,128]{1,0:T(8,128)S(1)}, f32[48,128]{1,0:T(8,128)S(1)}, u32[]{:S(2)}, u32[]{:S(2)}) collective-permute-start(f32[48,128]{1,0:T(8,128)S(1)} %get-tuple-element.63.refs_4_), channel_id=1, source_target_pairs={{0,1},{1,0},{2,3},{3,2},{4,5},{5,4},{6,7},{7,6},{8,9},{9,8},{10,11... | collective-permute-start | bytes 73736 | tf_op jit(solution)/shard_map/ppermute | solution.py:475
  18.0 9.9 %collective-permute-start.3 = (f32[144,128]{1,0:T(8,128)S(1)}, f32[144,128]{1,0:T(8,128)S(1)}, u32[]{:S(2)}, u32[]{:S(2)}) collective-permute-start(f32[144,128]{1,0:T(8,128)S(1)} %shard_map.112.mine_ref), channel_id=1, source_target_pairs={{1,2},{2,1},{3,4},{4,3},{5,6},{6,5},{7,8},{8,7},{9,10},{10,9},{11,... | collective-permute-start | bytes 221192 | tf_op jit(solution)/shard_map/ppermute | solution.py:471
  28.5 2.1 %collective-permute-start.4 = (f32[48,128]{1,0:T(8,128)S(1)}, f32[48,128]{1,0:T(8,128)S(1)}, u32[]{:S(2)}, u32[]{:S(2)}) collective-permute-start(f32[48,128]{1,0:T(8,128)S(1)} %get-tuple-element.73.rest_3_), channel_id=1, source_target_pairs={{0,1},{1,0},{2,3},{3,2},{4,5},{5,4},{6,7},{7,6},{8,9},{9,8},{10,11... | collective-permute-start | bytes 73736 | tf_op jit(solution)/shard_map/ppermute | solution.py:475
  31.2 8.4 %collective-permute-start.5 = (f32[144,128]{1,0:T(8,128)S(1)}, f32[144,128]{1,0:T(8,128)S(1)}, u32[]{:S(2)}, u32[]{:S(2)}) collective-permute-start(f32[144,128]{1,0:T(8,128)S(1)} %get-tuple-element.81.rest_2_.rest_3_), channel_id=1, source_target_pairs={{0,1},{1,0},{2,3},{3,2},{4,5},{5,4},{6,7},{7,6},{8,9},{9,8},{10,11... | collective-permute-start | bytes 221192 | tf_op jit(solution)/shard_map/ppermute | solution.py:475
  31.8 9.9 %collective-permute-start.6 = (f32[144,128]{1,0:T(8,128)S(1)}, f32[144,128]{1,0:T(8,128)S(1)}, u32[]{:S(2)}, u32[]{:S(2)}) collective-permute-start(f32[144,128]{1,0:T(8,128)S(1)} %get-tuple-element.81.rest_2_.rest_3_), channel_id=1, source_target_pairs={{1,2},{2,1},{3,4},{4,3},{5,6},{6,5},{7,8},{8,7},{9,10},{10,9},{11,... | collective-permute-start | bytes 221192 | tf_op jit(solution)/shard_map/ppermute | solution.py:471
  42.5 8.0 %collective-permute-start.7 = (f32[144,128]{1,0:T(8,128)S(1)}, f32[144,128]{1,0:T(8,128)S(1)}, u32[]{:S(2)}, u32[]{:S(2)}) collective-permute-start(f32[144,128]{1,0:T(8,128)S(1)} %get-tuple-element.84.rest_2_.rest_3_), channel_id=1, source_target_pairs={{0,1},{1,0},{2,3},{3,2},{4,5},{5,4},{6,7},{7,6},{8,9},{9,8},{10,11... | collective-permute-start | bytes 221192 | tf_op jit(solution)/shard_map/ppermute | solution.py:475
  42.6 9.9 %collective-permute-start.8 = (f32[144,128]{1,0:T(8,128)S(1)}, f32[144,128]{1,0:T(8,128)S(1)}, u32[]{:S(2)}, u32[]{:S(2)}) collective-permute-start(f32[144,128]{1,0:T(8,128)S(1)} %get-tuple-element.84.rest_2_.rest_3_), channel_id=1, source_target_pairs={{1,2},{2,1},{3,4},{4,3},{5,6},{6,5},{7,8},{8,7},{9,10},{10,9},{11,... | collective-permute-start | bytes 221192 | tf_op jit(solution)/shard_map/ppermute | solution.py:471

commit v5 on v4

--- a/solution.py
+++ b/solution.py
@@ -61,19 +61,22 @@
     return jnp.where(low, first, half_swap(second)), jnp.where(low, half_swap(first), second)
 
 
-def face_tables(other, number, start_ref, low_start_ref, idx_ref, low_idx_ref, block_of, masks):
+def face_tables(other, number, start_ref, low_start_ref, idx_ref, low_idx_ref, block_of, masks,
+                short_start_ref, short_idx_ref):
     owner_of, elem_of, side_of, turn_of = number
     rows = rows8()
     lane = lanes8()
     element = rows & 3
     a = (lane >> 3) & 7
     b = lane & 7
+    count = jnp.int32(0)
     signs = []
     for face in range(6):
         sides = jnp.zeros((8, 128), jnp.int32)
         turns = jnp.zeros((8, 128), jnp.int32)
         here_far = jnp.zeros((8, 128), jnp.int32)
         here_near = jnp.zeros((8, 128), jnp.int32)
+        parities = jnp.zeros((8, 128), jnp.int32)
         for e in range(4):
             owner = owner_of(e, face)
             side = side_of(e, face)
@@ -86,10 +89,15 @@
             turns = jnp.where(here, turn_of(e, face), turns)
             sides = jnp.where(here, side, sides)
             far = jnp.where((owner >= 0) & (owner == other), 1, 0)
+            short_start_ref[face * 4 + e] = jnp.where(far == 1, 288 + (count >> 1), block * 144 + (side >> 1) * 48 + elem)
+            parities = jnp.where(here, jnp.where(far == 1, count & 1, side & 1), parities)
+            count = count + far
             here_far = jnp.where(here, far, here_far)
             here_near = jnp.where(here, jnp.where(owner >= 0, 1, 0) - far, here_near)
         swap = (turns & 1) == 1
-        idx_ref[face] = (sides & 1) * 64 + jnp.where(swap, b * 8 + a, a * 8 + b)
+        place = jnp.where(swap, b * 8 + a, a * 8 + b)
+        idx_ref[face] = (sides & 1) * 64 + place
+        short_idx_ref[face] = parities * 64 + place
         low_idx_ref[face] = sides * 16 + jnp.where(swap, (b & 3) * 4 + (a & 3), (a & 3) * 4 + (b & 3))
         flips = 1 - 2 * ((((turns >> 1) & a) + ((turns >> 2) & b)) & 1)
         signs.append(((here_near * flips).astype(F32), (here_far * flips).astype(F32)))
@@ -115,7 +123,8 @@
 
 
 def prepare_tables(me, owner_ref, elem_ref, side_ref, turn_ref, vj_ref, fj_ref, start_ref, idx_ref, sign_ref,
-                   low_start_ref, low_idx_ref, near_ref, far_ref, plain_ref, low_plain_ref, vjc_ref, fjc_ref):
+                   low_start_ref, low_idx_ref, near_ref, far_ref, low_plain_ref, short_start_ref, short_idx_ref,
+                   vjc_ref, fjc_ref):
     left = lanes8() < 64
     low = rows8() < 4
 
@@ -124,11 +133,11 @@
         return jnp.where(owner < 0, 0, block)
 
     def plain(at, value, low_value):
-        plain_ref[at] = value
         low_plain_ref[at] = low_value
 
     number = [lambda e, face, ref=ref: ref[e, face] for ref in (owner_ref, elem_ref, side_ref, turn_ref)]
-    signs = face_tables(odd_partner(me), number, start_ref, low_start_ref, idx_ref, low_idx_ref, block_of, plain)
+    signs = face_tables(odd_partner(me), number, start_ref, low_start_ref, idx_ref, low_idx_ref, block_of, plain,
+                        short_start_ref, short_idx_ref)
     for f2 in range(3):
         near = jnp.where(left, signs[2 * f2][0], signs[2 * f2 + 1][0])
         far = jnp.where(left, signs[2 * f2][1], signs[2 * f2 + 1][1])
@@ -180,6 +189,18 @@
         low_ref[...] = traces[:, 384:]
     for f2 in range(3):
         face_ref[f2 * 48 : f2 * 48 + 48, :] = traces[:, f2 * 128 : f2 * 128 + 128]
+
+
+def answer(face_ref, ask_ref, ask_idx_ref, pick0, pick1, short_ref):
+    left = lanes8() < 64
+    for at in range(8):
+        target = pick1 if at % 2 else pick0
+        target[pl.ds(at // 2, 12, stride=4), :] = face_ref[pl.ds(ask_ref[at], 12, stride=4), :]
+    for vp in range(6):
+        row = 8 * vp
+        even = jnp.take_along_axis(pick0[row : row + 8, :], ask_idx_ref[0], axis=1)
+        odd = jnp.take_along_axis(pick1[row : row + 8, :], ask_idx_ref[1], axis=1)
+        short_ref[row : row + 8, :] = jnp.where(left, even, odd)
 
 
 def to_state(matrix, halves, low):
@@ -226,19 +247,19 @@
 
 def residual_of(u_ref, base_ref, split_ref, own_ref, mine_ref, even_ref, odd_ref, start_ref, idx_ref, sign_ref,
                 vjc_ref, fjc_ref, khi_ref, klo_ref, lift_ref, pool, pick0, pick1, jump_ref, halves_in, halves):
+    kin = 256 * halves_in
+    kout = 256 * halves
+    blended = jnp.dot(split_ref[:, :kin], khi_ref[:kin, :kout], preferred_element_type=F32)
+    rest = jnp.dot(split_ref[0:48, :kin], klo_ref[:kin, :kout], preferred_element_type=F32)
     size = mine_ref.shape[0]
     pool[0:size, :] = mine_ref[...]
     pool[size : 2 * size, :] = even_ref[...]
     if odd_ref is not None:
-        pool[2 * size : 3 * size, :] = odd_ref[0:size, :]
+        count = min(size, odd_ref.shape[0])
+        pool[2 * size : 2 * size + count, :] = odd_ref[0:count, :]
     else:
         pool[2 * size : 3 * size, :] = mine_ref[...]
     gather(pool, start_ref, pick0, pick1)
-    lifted = lifted_flux(own_ref, idx_ref, sign_ref, fjc_ref, lift_ref, pick0, pick1, jump_ref, halves)
-    kin = 256 * halves_in
-    kout = 256 * halves
-    blended = jnp.dot(split_ref[:, :kin], khi_ref[:kin, :kout], preferred_element_type=F32)
-    rest = jnp.dot(split_ref[0:48, :kin], klo_ref[:kin, :kout], preferred_element_type=F32)
     blended = to_state(blended[:48] + blended[48:] + rest, halves, rows8() < 4)
     residual = {}
     for h in range(halves):
@@ -246,8 +267,9 @@
             acc = vjc_ref[v * VARS] * blended[0, h]
             for w in range(1, VARS):
                 acc = acc + vjc_ref[v * VARS + w] * blended[w, h]
-            residual[v, h] = base_ref[2 * v + h] - SIGMA * u_ref[2 * v + h] - acc - lifted[v, h]
-    return residual
+            residual[v, h] = base_ref[2 * v + h] - SIGMA * u_ref[2 * v + h] - acc
+    lifted = lifted_flux(own_ref, idx_ref, sign_ref, fjc_ref, lift_ref, pick0, pick1, jump_ref, halves)
+    return {key: tile - lifted[key] for key, tile in residual.items()}
 
 
 def coarse_mask():
@@ -285,19 +307,19 @@
     for v in range(VARS):
         for h in range(2):
             u_ref[2 * v + h] = state[v, h]
+    copies[7].wait()
+    emit(state, 2, trace_ref, split_ref, face_ref)
     lane = lanes8()
     place = ((lane >> 4) & 1) * 64 + ((lane >> 2) & 3) * 8 + (lane & 3)
     for at in range(36):
         tiles = [jnp.take_along_axis(inv_ref[2 * (4 * at + part)], place, axis=1) for part in range(4)]
         packed = jnp.where(lane < 64, jnp.where(lane < 32, tiles[0], tiles[1]), jnp.where(lane < 96, tiles[2], tiles[3]))
         message_ref[144 + 8 * at : 152 + 8 * at, :] = packed
-    copies[7].wait()
-    emit(state, 2, trace_ref, split_ref, face_ref)
     message_ref[0:144, :] = face_ref[...]
 
 
-def ghost_prepare_body(me_ref, far_ref, start_ref, idx_ref, sign_ref, fjc_ref, inv_ref,
-                       fine_start_ref, fine_idx_ref, number_ref, sems):
+def ghost_prepare_body(me_ref, far_ref, start_ref, idx_ref, sign_ref, fjc_ref, inv_ref, ask_ref, ask_idx_ref,
+                       fine_start_ref, fine_idx_ref, parity_ref, number_ref, sems):
     copy = pltpu.make_async_copy(far_ref.at[pl.ds(NUMBER_ROW, 16)], number_ref, sems.at[0])
     copy.start()
     flux_table(
@@ -314,15 +336,31 @@
     left = lanes8() < 64
     number = [lambda e, face, at=at: number_ref[4 * at + e, face].astype(jnp.int32) for at in range(4)]
     signs = face_tables(
-        me_ref[0], number, fine_start_ref, start_ref, fine_idx_ref, idx_ref, lambda owner: 0, lambda *values: None
-    )
+        me_ref[0], number, fine_start_ref, start_ref, fine_idx_ref, idx_ref, lambda owner: 0, lambda *values: None,
+        fine_start_ref, fine_idx_ref,
+    )
+    for at in range(32):
+        ask_ref[at] = 0
+        parity_ref[at] = 0
+    count = jnp.int32(0)
+    for face in range(6):
+        for e in range(4):
+            side = number[2](e, face)
+            ask_ref[count] = (side >> 1) * 48 + number[1](e, face)
+            parity_ref[count] = side & 1
+            count = count + jnp.where(number[0](e, face) == me_ref[0], 1, 0)
+    for half in range(2):
+        parity = jnp.zeros((8, 128), jnp.int32)
+        for quarter in range(4):
+            parity = jnp.where((rows8() & 3) == quarter, parity_ref[2 * quarter + half], parity)
+        ask_idx_ref[half] = parity * 64 + (lane & 63)
     for f2 in range(3):
         sign_ref[f2] = jnp.where(left, signs[2 * f2][1], signs[2 * f2 + 1][1])
 
 
 def prepare_body(me_ref, *refs):
-    sources, tables, (khi_ref, klo_ref, lift_ref) = refs[:8], refs[8:19], refs[19:22]
-    owner_ref, elem_ref, side_ref, turn_ref, vj_ref, fj_ref, stiff_ref, sems = refs[22:]
+    sources, tables, (khi_ref, klo_ref, lift_ref) = refs[:8], refs[8:20], refs[20:23]
+    owner_ref, elem_ref, side_ref, turn_ref, vj_ref, fj_ref, stiff_ref, sems = refs[23:]
     copies = start_all(sources, (owner_ref, elem_ref, side_ref, turn_ref, vj_ref, fj_ref, stiff_ref, lift_ref), sems)
     for copy in copies[:6]:
         copy.wait()
@@ -336,7 +374,8 @@
 
 
 def fine_body(inv_ref, trace_ref, u_ref, *rest):
-    fine_step(inv_ref, trace_ref, u_ref, rest[:14], *rest[14:17], None, rest[17:])
+    fine_step(inv_ref, trace_ref, u_ref, rest[:14], *rest[16:19], None, rest[20:])
+    answer(rest[18], *rest[14:16], *rest[21:23], rest[19])
 
 
 def fine_low_body(inv_ref, trace_ref, u_ref, *rest):
@@ -421,7 +460,7 @@
 
 
 def coarse_body(inv_ref, trace_ref, fine_ref, u_ref, *rest):
-    shared, (out_ref, split_ref, face_ref), scratch = rest[:14], rest[14:17], rest[17:]
+    shared, (out_ref, split_ref, face_ref), scratch = rest[:14], rest[16:19], rest[20:]
     residual = residual_of(u_ref, *shared, *scratch, 1, 1)
     mask = coarse_mask()
     residual = {key: tile * mask for key, tile in residual.items()}
@@ -432,6 +471,7 @@
         out_ref[2 * v] = state[v, 0]
         out_ref[2 * v + 1] = state[v, 1]
     emit(state, 2, trace_ref, split_ref, face_ref)
+    answer(face_ref, *rest[14:16], *scratch[1:3], rest[19])
 
 
 STATE = VMEM((24, 8, 128), F32)
@@ -506,7 +546,7 @@
     far_message = in_vmem(odd_swap(message))
     even = even_swap(faces)
     loads = (*numbers, vj, fj, stiffness, lift)
-    start, idx, sign, low_start, low_idx, near, far, _, low_plain, vjc, fjc, khi, klo, lift = call(
+    start, idx, sign, low_start, low_idx, near, far, low_plain, short_start, short_idx, vjc, fjc, khi, klo, lift = call(
         prepare_body,
         (
             integers,
@@ -518,6 +558,7 @@
             signs,
             integers,
             integers,
+            indices,
             VMEM((144, 8, 128), F32),
             VMEM((216, 8, 128), F32),
             VMEM((512, 512), BF16),
@@ -556,18 +597,27 @@
         smem=(6,),
     )
     far_payload = in_vmem(odd_swap(payload))
-    ghost_start, ghost_idx, ghost_sign, ghost_fjc, ghost_inverse = call(
+    ghost_start, ghost_idx, ghost_sign, ghost_fjc, ghost_inverse, ask, ask_idx = call(
         ghost_prepare_body,
-        (integers, indices, signs, VMEM((216, 8, 128), F32), VMEM((144, 8, 128), F32)),
+        (
+            integers,
+            indices,
+            signs,
+            VMEM((216, 8, 128), F32),
+            VMEM((144, 8, 128), F32),
+            pltpu.SMEM((32,), jnp.int32),
+            VMEM((2, 8, 128), jnp.int32),
+        ),
         (me, far_message),
         (
             pltpu.SMEM((24,), jnp.int32),
             VMEM((6, 8, 128), jnp.int32),
+            pltpu.SMEM((32,), jnp.int32),
             pltpu.SMEM((16, 128), F32),
             pltpu.SemaphoreType.DMA((1,)),
         ),
         smem=(0,),
-        smem_outs=(0,),
+        smem_outs=(0, 5),
     )
     low_rhs, coarse, split, faces, sent = call(
         own_low_body,
@@ -584,28 +634,29 @@
         (*picks, SPLIT, FACES),
         smem=(4,),
     )
-    u, split, faces = call(
+    tables = (short_start, short_idx, sign, *volume)
+    u, split, faces, short = call(
         coarse_body,
-        (STATE, SPLIT, FACES),
-        (inverse, trace, fine_two, coarse, low_rhs, split, faces, sent, even, odd, low_start, low_idx, sign, *volume),
+        (STATE, SPLIT, FACES, LOW_FACES),
+        (inverse, trace, fine_two, coarse, low_rhs, split, faces, sent, even, odd, low_start, low_idx, sign, *volume, ask, ask_idx),
         pool,
-        smem=(10,),
-    )
-    odd = in_vmem(odd_swap(faces))
+        smem=(10, 18),
+    )
+    odd = in_vmem(odd_swap(short))
     even = even_swap(faces)
-    u, split, faces = call(
+    u, split, faces, short = call(
         fine_body,
-        (STATE, SPLIT, FACES),
-        (inverse, trace, u, rhs_state, split, faces, faces, even, odd, start, idx, sign, *volume),
+        (STATE, SPLIT, FACES, LOW_FACES),
+        (inverse, trace, u, rhs_state, split, faces, faces, even, odd, *tables, ask, ask_idx),
         pool,
-        smem=(9,),
-    )
-    odd = in_vmem(odd_swap(faces))
+        smem=(9, 17),
+    )
+    odd = in_vmem(odd_swap(short))
     even = even_swap(faces)
     (u,) = call(
         last_body,
         (jax.ShapeDtypeStruct((24, 8, 128), F32),),
-        (inverse, u, rhs_state, split, faces, faces, even, odd, start, idx, sign, *volume),
+        (inverse, u, rhs_state, split, faces, faces, even, odd, *tables),
         (*pool, STATE, pltpu.SemaphoreType.DMA((3,))),
         smem=(8,),
         far_out=True,

time: 54.1 us -> 52.8 us (0.976)
  waiting for transfers between devices: 9 us -> 7.94 us
    ppermute x4, waiting for transfers between devices: 7.8 us -> 6.74 us  [odd_swap(): return lax.ppermute(value, 'dom', route)]
where the time goes in v5:
time: 52.8 us; the launch traced here: 52.6 us
  starting transfers between devices  34 us (64%)
  Pallas kernels  10.5 us (20%)
  waiting for transfers between devices  7.94 us (15%)
    ppermute x4, starting transfers between devices, odd_swap(): return lax.ppermute(value, 'dom', route)  33.1 us
    pallas_call x10, Pallas kernels, call(): pl.pallas_call(body, out_shape=list(outs), in_specs=[scalar if at in smem...  10.5 us
    ppermute x4, waiting for transfers between devices, odd_swap(): return lax.ppermute(value, 'dom', route)  6.74 us
    ppermute x5, waiting for transfers between devices, even_swap(): lax.ppermute(value, 'dom', [(at, at ^ 1) for at in range(lax.axis_size('d...  1.2 us
  transfers between devices with their start and end apart: 9, of which 5 were waited for; matrix products, arithmetic and copies ran while one was open for 0% of the time, Pallas kernels for 8%

profile of v5, /device:TPU:24, one launch (start us, length us, event | category | flops | bytes accessed | tf_op | source)
XLA Modules:
  0.0 52.6 jit_solution(14930144613795706712)
XLA Ops:
  0.0 1.9 %shard_map.109 = (f32[24,8,128]{2,1,0:T(8,128)S(1)}, bf16[96,512]{1,0:T(8,128)(2,1)S(1)}, f32[144,128]{1,0:T(8,128)S(1)}, f32[488,128]{1,0:T(8,128)S(1)}, f32[28...) custom-call(s32[1]{0:T(128)} %bitcast.me_ref, s32[4,6]{1,0:T(4,128)} %refs_0_.3, ...), custom_call_target="tpu_custom_call" | custom-call | tf_op jit(solution)/shard_map/pallas_call | solution.py:496
  1.9 9.6 %collective-permute-start.1 = (f32[488,128]{1,0:T(8,128)S(1)}, f32[488,128]{1,0:T(8,128)S(1)}, u32[]{:S(2)}, u32[]{:S(2)}) collective-permute-start(f32[488,128]{1,0:T(8,128)S(1)} %get-tuple-element.57), channel_id=1, source_target_pairs={{1,2},{2,1},{3,4},{4,3},{5,6},{6,5},{7,8},{8,7},{9,10},{10,9},{11,... | collective-permute-start | bytes 749576 | tf_op jit(solution)/shard_map/ppermute | solution.py:511
  11.5 0.1 collective-permute-start
  11.6 2.1 %shard_map.110 = (s32[24]{0:T(128)S(4)}, s32[6,8,128]{2,1,0:T(8,128)S(1)}, f32[3,8,128]{2,1,0:T(8,128)S(1)}, s32[24]{0:T(128)S(4)}, s32[6,8,128]{2,1,0:T(8,128)S...) custom-call(s32[1]{0:T(128)} %bitcast.me_ref, ...), custom_call_target="tpu_custom_call" | custom-call | tf_op jit(solution)/shard_map/pallas_call | solution.py:496
  13.7 0.0 collective-permute-done.rest_4_
  13.7 1.7 %collective-permute-done.1.rest_5_.far_ref = f32[488,128]{1,0:T(8,128)S(1)} collective-permute-done((f32[488,128]{1,0:T(8,128)S(1)}, f32[488,128]{1,0:T(8,128)S(1)}, u32[]{:S(2)}, u32[]{:S(2)}) %collective-permute-start.1) | collective-permute-done | bytes 249888 | tf_op jit(solution)/shard_map/ppermute | solution.py:511
  15.4 0.7 %shard_map.111 = (f32[24,8,128]{2,1,0:T(8,128)S(1)}, bf16[96,512]{1,0:T(8,128)(2,1)S(1)}, f32[144,128]{1,0:T(8,128)S(1)}, f32[48,128]{1,0:T(8,128)S(1)}) custom-call(f32[288,8,128]{2,1,0:T(8,128)S(1)} %get-tuple-element.51.inv_ref, bf16[512,512]{1,0:T(8,128)(2,1)S(1)} %get-tuple-element.52.trace_ref, f32[24,8,128]{2,1,0:T(8,128)S(1)} %get-tuple-element.53.u_ref, ...), custom_call_target="tpu_custom_call" | custom-call | tf_op jit(solution)/shard_map/pallas_call | solution.py:496
  16.1 0.0 collective-permute-start.2
  16.1 1.2 %collective-permute-done.2.refs_5_ = f32[48,128]{1,0:T(8,128)S(1)} collective-permute-done((f32[48,128]{1,0:T(8,128)S(1)}, f32[48,128]{1,0:T(8,128)S(1)}, u32[]{:S(2)}, u32[]{:S(2)}) %collective-permute-start.2) | collective-permute-done | bytes 24608 | tf_op jit(solution)/shard_map/ppermute | solution.py:515
  17.3 0.4 shard_map.112.mine_ref
  17.7 7.9 %collective-permute-start.3 = (f32[144,128]{1,0:T(8,128)S(1)}, f32[144,128]{1,0:T(8,128)S(1)}, u32[]{:S(2)}, u32[]{:S(2)}) collective-permute-start(f32[144,128]{1,0:T(8,128)S(1)} %shard_map.112.mine_ref), channel_id=1, source_target_pairs={{1,2},{2,1},{3,4},{4,3},{5,6},{6,5},{7,8},{8,7},{9,10},{10,9},{11,... | collective-permute-start | bytes 221192 | tf_op jit(solution)/shard_map/ppermute | solution.py:511
  25.5 2.0 %collective-permute-done.3.far_ref = f32[144,128]{1,0:T(8,128)S(1)} collective-permute-done((f32[144,128]{1,0:T(8,128)S(1)}, f32[144,128]{1,0:T(8,128)S(1)}, u32[]{:S(2)}, u32[]{:S(2)}) %collective-permute-start.3) | collective-permute-done | bytes 73760 | tf_op jit(solution)/shard_map/ppermute | solution.py:511
  27.6 0.5 %shard_map.113 = (f32[24,8,128]{2,1,0:T(8,128)S(1)}, f32[24,8,128]{2,1,0:T(8,128)S(1)}, bf16[96,512]{1,0:T(8,128)(2,1)S(1)}, f32[144,128]{1,0:T(8,128)S(1)}, f32[48,128]{1,0:T(8,128)S(1)}) custom-call(f32[288,8,128]{2,1,0:T(8,128)S(1)} %get-tuple-element.51.inv_ref, bf16[512,512]{1,0:T(8,128)(2,1)S(1)} %get-tuple-element.52.trace_ref, ...), custom_call_target="tpu_custom_call" | custom-call | tf_op jit(solution)/shard_map/pallas_call | solution.py:496
  28.1 0.1 collective-permute-start.4
  28.2 1.7 %shard_map.114 = (s32[24]{0:T(128)S(4)}, s32[6,8,128]{2,1,0:T(8,128)S(1)}, f32[3,8,128]{2,1,0:T(8,128)S(1)}, f32[216,8,128]{2,1,0:T(8,128)S(1)}, f32[144,8,128]{...) custom-call(s32[1]{0:T(128)} %bitcast.me_ref, f32[488,128]{1,0:T(8,128)S(1)} %collective-permute-done.1.rest_5_.far_ref), custom_call_target="tpu_custom_call" | custom-call | tf_op jit(solution)/shard_map/pallas_call | solution.py:496
  29.9 0.5 %shard_map.115.rest_5_ = f32[48,128]{1,0:T(8,128)S(1)} custom-call(f32[144,8,128]{2,1,0:T(8,128)S(1)} %get-tuple-element.80.inv_ref, bf16[512,512]{1,0:T(8,128)(2,1)S(1)} %get-tuple-element.52.trace_ref, f32[144,128]{1,0:T(8,128)S(1)} %shard_map.112.mine_ref, f32[144,128]{1,0:T(8,128)S(1)} %collective-permute-done.3.far_ref, ...), custom_call_target="tpu_custom_call" | custom-call | tf_op jit(solution)/shard_map/pallas_call | solution.py:496
  30.4 0.0 collective-permute-done.4.rest_4_
  30.5 0.7 %shard_map.116 = (f32[24,8,128]{2,1,0:T(8,128)S(1)}, bf16[96,512]{1,0:T(8,128)(2,1)S(1)}, f32[144,128]{1,0:T(8,128)S(1)}, f32[48,128]{1,0:T(8,128)S(1)}) custom-call(f32[288,8,128]{2,1,0:T(8,128)S(1)} %get-tuple-element.51.inv_ref, bf16[512,512]{1,0:T(8,128)(2,1)S(1)} %get-tuple-element.52.trace_ref, f32[24,8,128]{2,1,0:T(8,128)S(1)} %get-tuple-element.66.refs_0_.fine_ref, ...), custom_call_target="tpu_custom_call" | custom-call | tf_op jit(solution)/shard_map/pallas_call | solution.py:496
  31.2 0.6 %collective-permute-start.5 = (f32[144,128]{1,0:T(8,128)S(1)}, f32[144,128]{1,0:T(8,128)S(1)}, u32[]{:S(2)}, u32[]{:S(2)}) collective-permute-start(f32[144,128]{1,0:T(8,128)S(1)} %get-tuple-element.89.rest_2_.rest_3_), channel_id=1, source_target_pairs={{0,1},{1,0},{2,3},{3,2},{4,5},{5,4},{6,7},{7,6},{8,9},{9,8},{10,11... | collective-permute-start | bytes 221192 | tf_op jit(solution)/shard_map/ppermute | solution.py:515
  31.7 7.8 %collective-permute-start.6 = (f32[48,128]{1,0:T(8,128)S(1)}, f32[48,128]{1,0:T(8,128)S(1)}, u32[]{:S(2)}, u32[]{:S(2)}) collective-permute-start(f32[48,128]{1,0:T(8,128)S(1)} %get-tuple-element.90), channel_id=1, source_target_pairs={{1,2},{2,1},{3,4},{4,3},{5,6},{6,5},{7,8},{8,7},{9,10},{10,9},{11,... | collective-permute-start | bytes 73736 | tf_op jit(solution)/shard_map/ppermute | solution.py:511
  39.6 1.5 %collective-permute-done.6.rest_5_ = f32[48,128]{1,0:T(8,128)S(1)} collective-permute-done((f32[48,128]{1,0:T(8,128)S(1)}, f32[48,128]{1,0:T(8,128)S(1)}, u32[]{:S(2)}, u32[]{:S(2)}) %collective-permute-start.6) | collective-permute-done | bytes 24608 | tf_op jit(solution)/shard_map/ppermute | solution.py:511
  41.1 0.0 collective-permute-done.5.rest_4_
  41.1 0.8 %shard_map.117 = (f32[24,8,128]{2,1,0:T(8,128)S(1)}, bf16[96,512]{1,0:T(8,128)(2,1)S(1)}, f32[144,128]{1,0:T(8,128)S(1)}, f32[48,128]{1,0:T(8,128)S(1)}) custom-call(f32[288,8,128]{2,1,0:T(8,128)S(1)} %get-tuple-element.51.inv_ref, bf16[512,512]{1,0:T(8,128)(2,1)S(1)} %get-tuple-element.52.trace_ref, f32[24,8,128]{2,1,0:T(8,128)S(1)} %get-tuple-element.87.u_ref, ...), custom_call_target="tpu_custom_call" | custom-call | tf_op jit(solution)/shard_map/pallas_call | solution.py:496
  41.9 0.1 collective-permute-start.7
  42.0 7.9 %collective-permute-start.8 = (f32[48,128]{1,0:T(8,128)S(1)}, f32[48,128]{1,0:T(8,128)S(1)}, u32[]{:S(2)}, u32[]{:S(2)}) collective-permute-start(f32[48,128]{1,0:T(8,128)S(1)} %get-tuple-element.96), channel_id=1, source_target_pairs={{1,2},{2,1},{3,4},{4,3},{5,6},{6,5},{7,8},{8,7},{9,10},{10,9},{11,... | collective-permute-start | bytes 73736 | tf_op jit(solution)/shard_map/ppermute | solution.py:511
  49.9 1.5 %collective-permute-done.8.rest_5_ = f32[48,128]{1,0:T(8,128)S(1)} collective-permute-done((f32[48,128]{1,0:T(8,128)S(1)}, f32[48,128]{1,0:T(8,128)S(1)}, u32[]{:S(2)}, u32[]{:S(2)}) %collective-permute-start.8) | collective-permute-done | bytes 24608 | tf_op jit(solution)/shard_map/ppermute | solution.py:511
  51.4 0.0 collective-permute-done.7.rest_4_
  51.4 1.2 %shard_map.118 = f32[24,8,128]{2,1,0:T(8,128)} custom-call(f32[288,8,128]{2,1,0:T(8,128)S(1)} %get-tuple-element.51.inv_ref, f32[24,8,128]{2,1,0:T(8,128)S(1)} %get-tuple-element.93.u_ref, f32[24,8,128]{2,1,0:T(8,128)S(1)} %get-tuple-element.54.rest_0_.refs_1_, bf16[96,512]{1,0:T(8,128)(2,1)S(1)} %get-tuple-element.94.rest_1_, ...), custom_call_target="tpu_custom_call" | custom-call | tf_op jit(solution)/shard_map/pallas_call | solution.py:496
Async XLA Ops:
  1.9 13.5 %collective-permute-start.1 = (f32[488,128]{1,0:T(8,128)S(1)}, f32[488,128]{1,0:T(8,128)S(1)}, u32[]{:S(2)}, u32[]{:S(2)}) collective-permute-start(f32[488,128]{1,0:T(8,128)S(1)} %get-tuple-element.57), channel_id=1, source_target_pairs={{1,2},{2,1},{3,4},{4,3},{5,6},{6,5},{7,8},{8,7},{9,10},{10,9},{11,... | collective-permute-start | bytes 749576 | tf_op jit(solution)/shard_map/ppermute | solution.py:511
  11.5 2.2 %collective-permute-start = (f32[144,128]{1,0:T(8,128)S(1)}, f32[144,128]{1,0:T(8,128)S(1)}, u32[]{:S(2)}, u32[]{:S(2)}) collective-permute-start(f32[144,128]{1,0:T(8,128)S(1)} %get-tuple-element.56.rest_2_.rest_3_), channel_id=1, source_target_pairs={{0,1},{1,0},{2,3},{3,2},{4,5},{5,4},{6,7},{7,6},{8,9},{9,8},{10,11... | collective-permute-start | bytes 221192 | tf_op jit(solution)/shard_map/ppermute | solution.py:515
  16.1 1.2 %collective-permute-start.2 = (f32[48,128]{1,0:T(8,128)S(1)}, f32[48,128]{1,0:T(8,128)S(1)}, u32[]{:S(2)}, u32[]{:S(2)}) collective-permute-start(f32[48,128]{1,0:T(8,128)S(1)} %get-tuple-element.69.refs_4_), channel_id=1, source_target_pairs={{0,1},{1,0},{2,3},{3,2},{4,5},{5,4},{6,7},{7,6},{8,9},{9,8},{10,11... | collective-permute-start | bytes 73736 | tf_op jit(solution)/shard_map/ppermute | solution.py:515
  17.7 9.9 %collective-permute-start.3 = (f32[144,128]{1,0:T(8,128)S(1)}, f32[144,128]{1,0:T(8,128)S(1)}, u32[]{:S(2)}, u32[]{:S(2)}) collective-permute-start(f32[144,128]{1,0:T(8,128)S(1)} %shard_map.112.mine_ref), channel_id=1, source_target_pairs={{1,2},{2,1},{3,4},{4,3},{5,6},{6,5},{7,8},{8,7},{9,10},{10,9},{11,... | collective-permute-start | bytes 221192 | tf_op jit(solution)/shard_map/ppermute | solution.py:511
  28.1 2.3 %collective-permute-start.4 = (f32[48,128]{1,0:T(8,128)S(1)}, f32[48,128]{1,0:T(8,128)S(1)}, u32[]{:S(2)}, u32[]{:S(2)}) collective-permute-start(f32[48,128]{1,0:T(8,128)S(1)} %get-tuple-element.79.rest_3_), channel_id=1, source_target_pairs={{0,1},{1,0},{2,3},{3,2},{4,5},{5,4},{6,7},{7,6},{8,9},{9,8},{10,11... | collective-permute-start | bytes 73736 | tf_op jit(solution)/shard_map/ppermute | solution.py:515
  31.2 9.9 %collective-permute-start.5 = (f32[144,128]{1,0:T(8,128)S(1)}, f32[144,128]{1,0:T(8,128)S(1)}, u32[]{:S(2)}, u32[]{:S(2)}) collective-permute-start(f32[144,128]{1,0:T(8,128)S(1)} %get-tuple-element.89.rest_2_.rest_3_), channel_id=1, source_target_pairs={{0,1},{1,0},{2,3},{3,2},{4,5},{5,4},{6,7},{7,6},{8,9},{9,8},{10,11... | collective-permute-start | bytes 221192 | tf_op jit(solution)/shard_map/ppermute | solution.py:515
  31.7 9.4 %collective-permute-start.6 = (f32[48,128]{1,0:T(8,128)S(1)}, f32[48,128]{1,0:T(8,128)S(1)}, u32[]{:S(2)}, u32[]{:S(2)}) collective-permute-start(f32[48,128]{1,0:T(8,128)S(1)} %get-tuple-element.90), channel_id=1, source_target_pairs={{1,2},{2,1},{3,4},{4,3},{5,6},{6,5},{7,8},{8,7},{9,10},{10,9},{11,... | collective-permute-start | bytes 73736 | tf_op jit(solution)/shard_map/ppermute | solution.py:511
  41.9 9.5 %collective-permute-start.7 = (f32[144,128]{1,0:T(8,128)S(1)}, f32[144,128]{1,0:T(8,128)S(1)}, u32[]{:S(2)}, u32[]{:S(2)}) collective-permute-start(f32[144,128]{1,0:T(8,128)S(1)} %get-tuple-element.95.rest_2_.rest_3_), channel_id=1, source_target_pairs={{0,1},{1,0},{2,3},{3,2},{4,5},{5,4},{6,7},{7,6},{8,9},{9,8},{10,11... | collective-permute-start | bytes 221192 | tf_op jit(solution)/shard_map/ppermute | solution.py:515
  42.0 9.4 %collective-permute-start.8 = (f32[48,128]{1,0:T(8,128)S(1)}, f32[48,128]{1,0:T(8,128)S(1)}, u32[]{:S(2)}, u32[]{:S(2)}) collective-permute-start(f32[48,128]{1,0:T(8,128)S(1)} %get-tuple-element.96), channel_id=1, source_target_pairs={{1,2},{2,1},{3,4},{4,3},{5,6},{6,5},{7,8},{8,7},{9,10},{10,9},{11,... | collective-permute-start | bytes 73736 | tf_op jit(solution)/shard_map/ppermute | solution.py:511
